TPU v7x, 128 devices: a whole 4x4x4 slice. The times are simulated.
128 devices in a mesh: plane: 8 (over z_hi, x), tile: 16 (over z_lo, y, core).
Axes of the slice: x: 4, y: 4, z: 4 (z_hi: 2, z_lo: 2; z = z_hi * 2 + z_lo), core: 2. Of those that a mesh axis runs over, the one named last changes fastest.
Arguments:
- visibility: float32 [2, 262144], P(None, ('plane', 'tile')), may hold values from -6 to 6
- target: int32 [262144, 1], P(('plane', 'tile')), may hold values from 0 to 127; in each aligned block of 2048 rows (0 to 2047, 2048 to 4095, ...) at most 32 rows name the same one
- offset: int32 [262144], P(('plane', 'tile')), may hold values from 0 to 1048575
- taps: float32 [8], replicated, may hold values from 0.1 to 1
- w_plane: float32 [8], P('plane'), may hold values from -300 to 300
Outputs:
- dirty_image: float32 [4096, 4096], P('plane', 'tile')
Inputs may be any that keep to these rules, and one draw needn't show every extreme that they name: `target`: among the rows of one device no value occurs more than 32 times, and some value occurs exactly 32 times.
All inputs are finite; a program needn't handle non-finite values.
Results may differ from a plain program's by a relative error of at most 0.0042.
Values sent between devices are 32-bit elements; how exact they have to be, the bound alone decides.
No kernel may reach another device: no remote copies, remote signals or barrier semaphores. Data moves between devices by JAX's collectives and lax.ppermute only.
A program may use at most 128 MiB of HBM per device.

v0:
```python
import math

import jax
import jax.numpy as jnp
from jax import lax
from jax.sharding import Mesh
from jax.sharding import PartitionSpec as P

G = 4096
TILE = ("tile_0", "tile_1", "tile_2")
PLANE = ("plane_0", "plane_1")
PLANE_TILE = ("plane_0", "plane_1", "tile_0", "tile_1", "tile_2")


HIGHEST = lax.Precision.HIGHEST


def split_up(x, dim, length):
    dims = x.shape
    blocks = x.reshape(*dims[:dim], length, dims[dim] // length, *dims[dim + 1 :])
    return jnp.moveaxis(blocks, dim, 0)


def joined_along(blocks, dim):
    blocks = jnp.moveaxis(blocks, 0, dim)
    dims = blocks.shape
    return blocks.reshape(*dims[:dim], dims[dim] * dims[dim + 1], *dims[dim + 2 :])


def moved_by_axis(blocks, axes, sequence):
    dims = [lax.axis_size(a) for a in axes]
    blocks = blocks.reshape(*dims, *blocks.shape[1:])
    for k in sequence:
        blocks = lax.all_to_all(blocks, axes[k], split_axis=k, concat_axis=k, tiled=True)
    return blocks.reshape(-1, *blocks.shape[len(axes) :])


def exchange_by_chip(x, groups, sequence, split_dim, concat_dim):
    length = lax.axis_size(groups[0]) * lax.axis_size(groups[1])
    blocks = split_up(x, split_dim, length)
    return joined_along(moved_by_axis(blocks, groups, sequence), concat_dim)


def shifted(x, axis, by):
    length = lax.axis_size(axis)
    return lax.ppermute(x, axis, [(i, (i + by) % length) for i in range(length)])


def summed_on_arrival(x, axis, dim):
    blocks = split_up(x, dim, lax.axis_size(axis))
    arrived = lax.all_to_all(blocks, axis, split_axis=0, concat_axis=0, tiled=True)
    return arrived.sum(axis=0)


def direction(index, length):
    return ((index + length // 2) % length - length // 2).astype(jnp.float32) * (0.5 / length)


def angle_table(first, second, length):
    product = (
        jnp.arange(first, dtype=jnp.int32)[:, None]
        * jnp.arange(second, dtype=jnp.int32)[None, :]
        % length
    )
    angles = product.astype(jnp.float32) * (2.0 * math.pi / length)
    return (jnp.cos(angles), jnp.sin(angles))


def split_length(length):
    inner_len = math.gcd(length, 128)
    return (length // inner_len, inner_len)


def transform_last(real_part, imag_part):
    length = real_part.shape[-1]
    outer_len, inner_len = split_length(length)
    real_grid = real_part.reshape(-1, outer_len, inner_len)
    imag_grid = imag_part.reshape(-1, outer_len, inner_len)
    cos_one, sin_one = angle_table(outer_len, outer_len, outer_len)
    first_re = jnp.einsum("rab,ak->rkb", real_grid, cos_one, precision=HIGHEST) - jnp.einsum(
        "rab,ak->rkb", imag_grid, sin_one, precision=HIGHEST
    )
    first_im = jnp.einsum("rab,ak->rkb", real_grid, sin_one, precision=HIGHEST) + jnp.einsum(
        "rab,ak->rkb", imag_grid, cos_one, precision=HIGHEST
    )
    cos_tw, sin_tw = angle_table(outer_len, inner_len, length)
    twist_re = first_re * cos_tw - first_im * sin_tw
    twist_im = first_re * sin_tw + first_im * cos_tw
    cos_two, sin_two = angle_table(inner_len, inner_len, inner_len)
    out_re = jnp.einsum("rkb,bq->rqk", twist_re, cos_two, precision=HIGHEST) - jnp.einsum(
        "rkb,bq->rqk", twist_im, sin_two, precision=HIGHEST
    )
    out_im = jnp.einsum("rkb,bq->rqk", twist_re, sin_two, precision=HIGHEST) + jnp.einsum(
        "rkb,bq->rqk", twist_im, cos_two, precision=HIGHEST
    )
    return (out_re.reshape(-1, length), out_im.reshape(-1, length))


def transform_first(real_part, imag_part):
    length = real_part.shape[0]
    outer_len, inner_len = split_length(length)
    real_grid = real_part.reshape(outer_len, inner_len, -1)
    imag_grid = imag_part.reshape(outer_len, inner_len, -1)
    cos_one, sin_one = angle_table(outer_len, outer_len, outer_len)
    first_re = jnp.einsum("abc,ak->kbc", real_grid, cos_one, precision=HIGHEST) - jnp.einsum(
        "abc,ak->kbc", imag_grid, sin_one, precision=HIGHEST
    )
    first_im = jnp.einsum("abc,ak->kbc", real_grid, sin_one, precision=HIGHEST) + jnp.einsum(
        "abc,ak->kbc", imag_grid, cos_one, precision=HIGHEST
    )
    cos_tw, sin_tw = angle_table(outer_len, inner_len, length)
    twist_re = first_re * cos_tw[:, :, None] - first_im * sin_tw[:, :, None]
    twist_im = first_re * sin_tw[:, :, None] + first_im * cos_tw[:, :, None]
    cos_two, sin_two = angle_table(inner_len, inner_len, inner_len)
    out_re = jnp.einsum("kbc,bq->qkc", twist_re, cos_two, precision=HIGHEST) - jnp.einsum(
        "kbc,bq->qkc", twist_im, sin_two, precision=HIGHEST
    )
    out_im = jnp.einsum("kbc,bq->qkc", twist_re, sin_two, precision=HIGHEST) + jnp.einsum(
        "kbc,bq->qkc", twist_im, cos_two, precision=HIGHEST
    )
    return (out_re.reshape(length, -1), out_im.reshape(length, -1))


def grid_block(received, taps, start, block_len, band_rows, totals):
    piece = lax.dynamic_slice_in_dim(received, start, block_len, 1)
    encoded = jnp.maximum(piece[2].astype(jnp.int32) - 1, 0)
    band_row = encoded // G
    column = encoded % G
    kernel_len = taps.shape[0]
    taps_low = taps.astype(jnp.bfloat16)
    weight_re = (taps[None, :] * piece[0][:, None]).astype(jnp.bfloat16)
    weight_im = (taps[None, :] * piece[1][:, None]).astype(jnp.bfloat16)
    rel_row = jnp.arange(band_rows, dtype=jnp.int32)[None, :] - band_row[:, None]
    rel_col = (jnp.arange(G, dtype=jnp.int32)[None, :] - column[:, None]) % G
    row_re = jnp.zeros((block_len, band_rows), jnp.bfloat16)
    row_im = jnp.zeros((block_len, band_rows), jnp.bfloat16)
    col_table = jnp.zeros((block_len, G), jnp.bfloat16)
    for tap_index in range(kernel_len):
        row_re = jnp.where(rel_row == tap_index, weight_re[:, tap_index : tap_index + 1], row_re)
        row_im = jnp.where(rel_row == tap_index, weight_im[:, tap_index : tap_index + 1], row_im)
        col_table = jnp.where(rel_col == tap_index, taps_low[tap_index], col_table)
    row_table = jnp.concatenate([row_re, row_im], axis=1)
    return totals + lax.dot_general(
        row_table, col_table, (((0,), (0,)), ((), ())), preferred_element_type=jnp.float32
    )


def local(visibility, target, offset, taps, w_plane):
    tiles = lax.axis_size(TILE)
    planes = lax.axis_size(PLANE)
    devices = tiles * planes
    vis_dev = visibility.shape[1]
    capacity = 2 * vis_dev // devices
    slot_total = devices * capacity
    band = G // tiles
    columns = G // tiles
    kernel_len = taps.shape[0]
    band_rows = band + kernel_len - 1
    destination = target[:, 0]
    onehot = (destination[:, None] == jnp.arange(devices, dtype=jnp.int32)[None, :]).astype(
        jnp.int32
    )
    rank = jnp.sum(jnp.cumsum(onehot, axis=0) * onehot, axis=1) - 1
    slot = destination * capacity + rank
    payload = jnp.stack([visibility[0], visibility[1], offset.astype(jnp.float32) + 1.0])
    outgoing = jnp.zeros((3, slot_total), jnp.float32).at[:, slot].set(payload)
    received = exchange_by_chip(
        outgoing, (("plane_0", "plane_1", "tile_0", "tile_1"), "tile_2"), (1, 0), 1, 1
    )
    block_len = min(512, slot_total)
    empty = jnp.zeros((2 * band_rows, G), jnp.float32)

    def grid_step(index, totals):
        return grid_block(received, taps, index * block_len, block_len, band_rows, totals)

    gridded = lax.fori_loop(0, slot_total // block_len, grid_step, empty)
    gridded = gridded.reshape(2, band_rows, G)
    incoming = shifted(gridded[:, band:], TILE, 1)
    grid_band = gridded[:, :band].at[:, : kernel_len - 1].add(incoming)
    col_re, col_im = transform_last(grid_band[0], grid_band[1])
    stacked = jnp.stack([col_re, col_im]).reshape(2, band, tiles, columns)
    exchanged = lax.all_to_all(stacked, TILE, split_axis=2, concat_axis=1, tiled=True)
    item_count = exchanged.shape[3]
    rows_re, rows_im = transform_first(
        exchanged[0].reshape(G, item_count), exchanged[1].reshape(G, item_count)
    )
    image_parts = jnp.stack([rows_re, rows_im]).reshape(2, G, 1, item_count).reshape(2, G, columns)
    line_pos = jnp.arange(G, dtype=jnp.int32)
    column_pos = lax.axis_index(TILE) * columns + jnp.arange(columns, dtype=jnp.int32)
    cos_row = direction(line_pos, G)
    cos_col = direction(column_pos, G)
    n_minus = (
        jnp.sqrt(1.0 - cos_row[:, None] * cos_row[:, None] - cos_col[None, :] * cos_col[None, :])
        - 1.0
    )
    phase = 2.0 * math.pi * w_plane[0] * n_minus
    screened = jnp.cos(phase) * image_parts[0] - jnp.sin(phase) * image_parts[1]
    summed = summed_on_arrival(screened, PLANE, 0)
    return summed * (1.0 / math.sqrt(vis_dev * devices))


def solution(mesh):
    finer = Mesh(
        mesh.devices.reshape(2, 4, 2, 4, 2), ("plane_0", "plane_1", "tile_0", "tile_1", "tile_2")
    )
    return jax.shard_map(
        local,
        mesh=finer,
        in_specs=(P(None, PLANE_TILE), P(PLANE_TILE, None), P(PLANE_TILE), P(), P(PLANE)),
        out_specs=P(PLANE, TILE),
        check_vma=False,
    )
```

profile of v0, /device:TPU:1, one launch (start us, length us, event | category | flops | bytes accessed | tf_op | source)
XLA Modules:
  0.0 554.9 jit_solution(2011988327328630223)
XLA Ops:
  0.0 0.9 copy.67
  2.8 6.1 %scatter_custom_fusion = f32[3,4096]{0,1:T(8,128)S(1)} fusion(s32[2048]{0:T(1024)S(1)} %bitcast.168, f32[2048,3]{1,0:T(8,128)S(1)} %copy.69, f32[]{:T(128)} %constant.337.clone.1), kind=kCustom, calls=%fused_computation.153 | custom fusion | bytes 49156 | tf_op jit(solution)/shard_map/scatter | solution.py:166
  8.9 0.9 copy.70
  10.1 4.8 all_to_all.30
  15.4 0.8 reduce.36
  16.4 0.9 reshape.301
  17.3 11.5 %all-to-all-start.1 = ((f32[64,1,192]{2,1,0:T(1,128)}), f32[64,1,192]{2,1,0:T(1,128)S(1)}, u32[]{:S(2)}, u32[]{:S(2)}) async-start(f32[64,1,192]{2,1,0:T(1,128)} %reshape.301), calls=%async_computation.1 | async-start | bytes 131072 | tf_op jit(solution)/shard_map/all_to_all | solution.py:34
  28.8 8.6 %all-to-all-done.1 = f32[64,1,192]{2,1,0:T(1,128)S(1)} async-done(((f32[64,1,192]{2,1,0:T(1,128)}), f32[64,1,192]{2,1,0:T(1,128)S(1)}, u32[]{:S(2)}, u32[]{:S(2)}) %all-to-all-start.1) | async-done | bytes 49184 | tf_op jit(solution)/shard_map/all_to_all | solution.py:34
  37.4 0.8 reduce.37
  38.6 175.1 %while.18 = (s32[]{:T(128)}, f32[526,4096]{1,0:T(8,128)}, f32[3,4096]{1,0:T(4,128)S(1)}, f32[8]{0:T(128)S(1)}, bf16[8]{0:T(256)(128)(2,1)S(1)}, /*index=5*/s32[]...) while((s32[]{:T(128)}, f32[526,4096]{1,0:T(8,128)}, f32[3,4096]{1,0:T(4,128)S(1)}, ...), condition=%wide.region_5.6_spmd.clone, body=%wide.region_4.5_spmd.clone.sunk | while | flops 2273700864 | bytes 18414876 | solution.py:176
  39.0 1.6 fusion.259
  41.2 17.3 %select_add_fusion.2 = f32[526,4096]{1,0:T(8,128)} fusion(f32[526,4096]{1,0:T(8,128)} %get-tuple-element.356, pred[]{:T(512)S(6)} %compare.38, s32[512]{0:T(512)S(1)} %get-tuple-element.312, bf16[]{:T(256)} %bitcast.130, bf16[]{:T(256)} %bitcast.131, bf16[]{:T(256)} %bitcast.132, bf16[]{:T(256)} %bitcast.133, bf16[]{:T(256)} %bitcast.134, ...), kind=kOutput, calls=%fused_computation.4.clone.1 | convolution fusion | flops 2270310400 | bytes 17776656 | tf_op jit(solution)/shard_map/while/body/eval_jaxpr/dot_general | solution.py:143
  58.9 1.6 fusion.259
  61.2 19.5 %select_add_fusion.2 = f32[526,4096]{1,0:T(8,128)} fusion(f32[526,4096]{1,0:T(8,128)} %get-tuple-element.356, pred[]{:T(512)S(6)} %compare.38, s32[512]{0:T(512)S(1)} %get-tuple-element.312, bf16[]{:T(256)} %bitcast.130, bf16[]{:T(256)} %bitcast.131, bf16[]{:T(256)} %bitcast.132, bf16[]{:T(256)} %bitcast.133, bf16[]{:T(256)} %bitcast.134, ...), kind=kOutput, calls=%fused_computation.4.clone.1 | convolution fusion | flops 2270310400 | bytes 17776656 | tf_op jit(solution)/shard_map/while/body/eval_jaxpr/dot_general | solution.py:143
  81.1 1.6 fusion.259
  83.4 19.5 %select_add_fusion.2 = f32[526,4096]{1,0:T(8,128)} fusion(f32[526,4096]{1,0:T(8,128)} %get-tuple-element.356, pred[]{:T(512)S(6)} %compare.38, s32[512]{0:T(512)S(1)} %get-tuple-element.312, bf16[]{:T(256)} %bitcast.130, bf16[]{:T(256)} %bitcast.131, bf16[]{:T(256)} %bitcast.132, bf16[]{:T(256)} %bitcast.133, bf16[]{:T(256)} %bitcast.134, ...), kind=kOutput, calls=%fused_computation.4.clone.1 | convolution fusion | flops 2270310400 | bytes 17776656 | tf_op jit(solution)/shard_map/while/body/eval_jaxpr/dot_general | solution.py:143
  103.3 1.6 fusion.259
  105.5 19.5 %select_add_fusion.2 = f32[526,4096]{1,0:T(8,128)} fusion(f32[526,4096]{1,0:T(8,128)} %get-tuple-element.356, pred[]{:T(512)S(6)} %compare.38, s32[512]{0:T(512)S(1)} %get-tuple-element.312, bf16[]{:T(256)} %bitcast.130, bf16[]{:T(256)} %bitcast.131, bf16[]{:T(256)} %bitcast.132, bf16[]{:T(256)} %bitcast.133, bf16[]{:T(256)} %bitcast.134, ...), kind=kOutput, calls=%fused_computation.4.clone.1 | convolution fusion | flops 2270310400 | bytes 17776656 | tf_op jit(solution)/shard_map/while/body/eval_jaxpr/dot_general | solution.py:143
  125.4 1.6 fusion.259
  127.7 19.5 %select_add_fusion.2 = f32[526,4096]{1,0:T(8,128)} fusion(f32[526,4096]{1,0:T(8,128)} %get-tuple-element.356, pred[]{:T(512)S(6)} %compare.38, s32[512]{0:T(512)S(1)} %get-tuple-element.312, bf16[]{:T(256)} %bitcast.130, bf16[]{:T(256)} %bitcast.131, bf16[]{:T(256)} %bitcast.132, bf16[]{:T(256)} %bitcast.133, bf16[]{:T(256)} %bitcast.134, ...), kind=kOutput, calls=%fused_computation.4.clone.1 | convolution fusion | flops 2270310400 | bytes 17776656 | tf_op jit(solution)/shard_map/while/body/eval_jaxpr/dot_general | solution.py:143
  147.6 1.6 fusion.259
  149.9 19.5 %select_add_fusion.2 = f32[526,4096]{1,0:T(8,128)} fusion(f32[526,4096]{1,0:T(8,128)} %get-tuple-element.356, pred[]{:T(512)S(6)} %compare.38, s32[512]{0:T(512)S(1)} %get-tuple-element.312, bf16[]{:T(256)} %bitcast.130, bf16[]{:T(256)} %bitcast.131, bf16[]{:T(256)} %bitcast.132, bf16[]{:T(256)} %bitcast.133, bf16[]{:T(256)} %bitcast.134, ...), kind=kOutput, calls=%fused_computation.4.clone.1 | convolution fusion | flops 2270310400 | bytes 17776656 | tf_op jit(solution)/shard_map/while/body/eval_jaxpr/dot_general | solution.py:143
  169.8 1.6 fusion.259
  172.0 19.5 %select_add_fusion.2 = f32[526,4096]{1,0:T(8,128)} fusion(f32[526,4096]{1,0:T(8,128)} %get-tuple-element.356, pred[]{:T(512)S(6)} %compare.38, s32[512]{0:T(512)S(1)} %get-tuple-element.312, bf16[]{:T(256)} %bitcast.130, bf16[]{:T(256)} %bitcast.131, bf16[]{:T(256)} %bitcast.132, bf16[]{:T(256)} %bitcast.133, bf16[]{:T(256)} %bitcast.134, ...), kind=kOutput, calls=%fused_computation.4.clone.1 | convolution fusion | flops 2270310400 | bytes 17776656 | tf_op jit(solution)/shard_map/while/body/eval_jaxpr/dot_general | solution.py:143
  191.9 1.6 fusion.259
  194.2 19.5 %select_add_fusion.2 = f32[526,4096]{1,0:T(8,128)} fusion(f32[526,4096]{1,0:T(8,128)} %get-tuple-element.356, pred[]{:T(512)S(6)} %compare.38, s32[512]{0:T(512)S(1)} %get-tuple-element.312, bf16[]{:T(256)} %bitcast.130, bf16[]{:T(256)} %bitcast.131, bf16[]{:T(256)} %bitcast.132, bf16[]{:T(256)} %bitcast.133, bf16[]{:T(256)} %bitcast.134, ...), kind=kOutput, calls=%fused_computation.4.clone.1 | convolution fusion | flops 2270310400 | bytes 17776656 | tf_op jit(solution)/shard_map/while/body/eval_jaxpr/dot_general | solution.py:143
  213.7 7.6 %reshape.264 = f32[2,263,4096]{2,1,0:T(8,128)} reshape(f32[526,4096]{1,0:T(8,128)} %get-tuple-element.158) | data formatting | bytes 17235968 | tf_op jit(solution)/shard_map/reshape | solution.py:177
  221.3 1.0 slice.407
  222.3 2.0 collective-permute-start
  224.4 7.6 %slice.405 = f32[2,256,4096]{2,1,0:T(8,128)} slice(f32[2,263,4096]{2,1,0:T(8,128)} %reshape.264), slice={[0:2], [0:256], [0:4096]} | slice | bytes 16777216 | tf_op jit(solution)/shard_map/slice | solution.py:179
  232.0 1.0 slice_add_fusion
  233.0 2.2 scatter-add.4
  235.1 4.0 slice_bitcast_fusion
  239.9 4.0 fusion.150
  243.9 4.0 fusion.156
  247.9 0.8 copy.95
  248.7 4.3 convolution_add_fusion
  253.0 5.1 subtract_bitcast_fusion.1
  258.1 6.2 %fusion.84 = f32[128,256,32]{1,0,2:T(8,128)S(1)} fusion(f32[256,32,128]{2,1,0:T(8,128)S(1)} %get-tuple-element.234), kind=kOutput, calls=%fused_computation.135 | convolution fusion | flops 1610842112 | bytes 8388608 | tf_op jit(solution)/shard_map/rkb,bq->rqk/dot_general | solution.py:90
  264.3 6.2 %fusion.82 = f32[128,256,32]{1,0,2:T(8,128)S(1)} fusion(f32[256,32,128]{2,1,0:T(8,128)S(1)} %get-tuple-element.234), kind=kOutput, calls=%fused_computation.133 | convolution fusion | flops 1610842112 | bytes 8388608 | tf_op jit(solution)/shard_map/rkb,bq->rqk/dot_general | solution.py:93
  270.6 6.8 %subtract_bitcast_fusion = f32[256,128,32]{0,1,2:T(8,128)S(1)} fusion(f32[128,256,32]{1,0,2:T(8,128)S(1)} %fusion.84, f32[256,32,128]{2,1,0:T(8,128)S(1)} %get-tuple-element.233), kind=kOutput, calls=%fused_computation.114 | convolution fusion | flops 1611890688 | bytes 12582912 | tf_op jit(solution)/shard_map/rkb,bq->rqk/dot_general | solution.py:90
  277.3 2.4 copy.76
  279.8 6.1 %add_bitcast_fusion = f32[256,128,32]{0,1,2:T(8,128)S(1)} fusion(f32[128,256,32]{1,0,2:T(8,128)S(1)} %fusion.82, f32[256,32,128]{2,1,0:T(8,128)S(1)} %get-tuple-element.233), kind=kOutput, calls=%fused_computation.113 | convolution fusion | flops 1611890688 | bytes 12582912 | tf_op jit(solution)/shard_map/rkb,bq->rqk/dot_general | solution.py:93
  285.9 2.4 copy.79
  288.3 1.0 pad_maximum_fusion
  289.4 3.8 copy.80
  293.2 5.0 all-to-all-start.2
  299.0 111.6 %all-to-all-done.2 = f32[2,256,16,256]{1,3,0,2:T(8,128)} async-done(((f32[2,256,16,256]{1,3,0,2:T(8,128)}), f32[2,256,16,256]{1,3,0,2:T(8,128)}, u32[]{:S(2)}, u32[]{:S(2)}) %all-to-all-start.2) | async-done | bytes 8388640 | tf_op jit(solution)/shard_map/all_to_all | solution.py:182
  410.6 8.7 %copy.81 = f32[2,256,16,256]{3,1,2,0:T(8,128)} copy(f32[2,256,16,256]{1,3,0,2:T(8,128)} %all-to-all-done.2) | data formatting | bytes 16777216 | tf_op jit(solution)/shard_map/all_to_all | solution.py:182
  419.3 4.0 fusion.247
  423.3 5.9 %fusion.76 = f32[32,128,256]{2,0,1:T(8,128)S(1)} fusion(f32[32,128,256]{2,1,0:T(8,128)S(1)} %bitcast.146), kind=kOutput, calls=%fused_computation.127 | convolution fusion | flops 402667520 | bytes 8388608 | tf_op jit(solution)/shard_map/abc,ak->kbc/dot_general | solution.py:105
  429.2 6.6 %fusion.74 = f32[32,128,256]{2,0,1:T(8,128)S(1)} fusion(f32[32,128,256]{2,1,0:T(8,128)S(1)} %bitcast.147), kind=kOutput, calls=%fused_computation.125 | convolution fusion | flops 402667520 | bytes 8388608 | tf_op jit(solution)/shard_map/abc,ak->kbc/dot_general | solution.py:108
  435.8 6.2 %fusion.94 = f32[32,128,256]{2,0,1:T(8,128)S(1)} fusion(f32[32,128,256]{2,0,1:T(8,128)S(1)} %fusion.76, f32[32,128,256]{2,1,0:T(8,128)S(1)} %bitcast.142), kind=kOutput, calls=%fused_computation.141 | convolution fusion | flops 403716096 | bytes 12582912 | tf_op jit(solution)/shard_map/abc,ak->kbc/dot_general | solution.py:105
  441.9 7.9 %multiply_subtract_fusion = (f32[32,128,256]{2,0,1:T(8,128)S(1)}, f32[32,128,256]{2,0,1:T(8,128)S(1)}) fusion(f32[32,128,256]{2,0,1:T(8,128)S(1)} %fusion.94, f32[32,128]{0,1:T(8,128)S(1)} %copy.87, f32[32,128]{0,1:T(8,128)S(1)} %copy.84, f32[32,128,256]{2,0,1:T(8,128)S(1)} %fusion.74, f32[32,128,256]{2,1,0:T(8,128)S(1)} %bitcast.143), kind=kOutput, calls=%fused_computation.112 | convolution fusion | flops 410007552 | bytes 21004288 | tf_op jit(solution)/shard_map/abc,ak->kbc/dot_general | solution.py:108
  449.9 6.0 %fusion.68 = f32[128,32,256]{2,0,1:T(8,128)S(1)} fusion(f32[32,128,256]{2,0,1:T(8,128)S(1)} %get-tuple-element.232), kind=kOutput, calls=%fused_computation.119 | convolution fusion | flops 1610842112 | bytes 8388608 | tf_op jit(solution)/shard_map/kbc,bq->qkc/dot_general | solution.py:115
  455.9 6.5 %fusion.66 = f32[128,32,256]{2,0,1:T(8,128)S(1)} fusion(f32[32,128,256]{2,0,1:T(8,128)S(1)} %get-tuple-element.232), kind=kOutput, calls=%fused_computation.117 | convolution fusion | flops 1610842112 | bytes 8388608 | tf_op jit(solution)/shard_map/kbc,bq->qkc/dot_general | solution.py:118
  462.4 6.0 %fusion.100 = f32[128,32,256]{2,0,1:T(8,128)S(1)} fusion(f32[128,32,256]{2,0,1:T(8,128)S(1)} %fusion.68, f32[32,128,256]{2,0,1:T(8,128)S(1)} %get-tuple-element.231), kind=kOutput, calls=%fused_computation.143 | convolution fusion | flops 1611890688 | bytes 12582912 | tf_op jit(solution)/shard_map/kbc,bq->qkc/dot_general | solution.py:115
  468.4 2.4 copy.90
  470.8 6.5 %fusion.103 = f32[128,32,256]{2,0,1:T(8,128)S(1)} fusion(f32[128,32,256]{2,0,1:T(8,128)S(1)} %fusion.66, f32[32,128,256]{2,0,1:T(8,128)S(1)} %get-tuple-element.231), kind=kOutput, calls=%fused_computation.144 | convolution fusion | flops 1611890688 | bytes 12582912 | tf_op jit(solution)/shard_map/kbc,bq->qkc/dot_general | solution.py:118
  477.4 2.4 copy.93
  479.8 16.9 %fusion.65 = f32[8,512,256]{2,1,0:T(8,128)S(1)} fusion(f32[256]{0:T(256)S(1)} %fusion.179, f32[8,512]{1,0:T(8,128)S(1)} %fusion.141, f32[]{:T(128)} %bitcast, f32[8,512,256]{2,1,0:T(8,128)S(1)} %bitcast.150, f32[8,512,256]{2,1,0:T(8,128)S(1)} %bitcast.149), kind=kLoop, calls=%fused_computation.109 | loop fusion | flops 6291456 | bytes 12600324 | tf_op jit(solution)/shard_map/sub | solution.py:197
  496.8 54.3 %all_to_all.31 = f32[8,512,256]{2,1,0:T(8,128)} all-to-all(f32[8,512,256]{2,1,0:T(8,128)S(1)} %fusion.65), channel_id=1, replica_groups=mesh['plane_0'=2,'plane_1'=4,'tile_0'=2,'tile_1'=4,'tile_2'=2] {'plane_0..., dimensions={0} | all-to-all | bytes 8388608 | tf_op jit(solution)/shard_map/all_to_all | solution.py:51
  551.1 2.5 reduce_sum.19
  553.6 0.8 broadcast_multiply_fusion
  (93 shorter events, 12.7 us)
Async XLA Ops:
  0.0 1.7 copy-start
  0.0 2.4 copy-start.3
  0.0 2.4 copy-start.1
  1.7 27.1 %copy-start.2 = (f32[8]{0:T(128)S(1)}, f32[8]{0:T(128)}, u32[]{:S(2)}) copy-start(f32[8]{0:T(128)} %param.12) | copy-start | bytes 100
  17.3 20.1 %all-to-all-start.1 = ((f32[64,1,192]{2,1,0:T(1,128)}), f32[64,1,192]{2,1,0:T(1,128)S(1)}, u32[]{:S(2)}, u32[]{:S(2)}) async-start(f32[64,1,192]{2,1,0:T(1,128)} %reshape.301), calls=%async_computation.1 | async-start | bytes 131072 | tf_op jit(solution)/shard_map/all_to_all | solution.py:34
  222.3 9.7 %collective-permute-start = (f32[2,7,4096]{2,1,0:T(8,128)S(1)}, f32[2,7,4096]{2,1,0:T(8,128)S(1)}, u32[]{:S(2)}, u32[]{:S(2)}) collective-permute-start(f32[2,7,4096]{2,1,0:T(8,128)S(1)} %slice.407), channel_id=1, source_target_pairs={{0,1},{1,2},{2,3},{3,4},{4,5},{5,6},{6,7},{7,8},{8,9},{9,10},{10,1... | collective-permute-start | bytes 688136 | tf_op jit(solution)/shard_map/ppermute | solution.py:46
  293.2 117.4 %all-to-all-start.2 = ((f32[2,256,16,256]{1,3,0,2:T(8,128)}), f32[2,256,16,256]{1,3,0,2:T(8,128)}, u32[]{:S(2)}, u32[]{:S(2)}) async-start(f32[2,256,16,256]{1,3,0,2:T(8,128)} %copy.80), calls=%async_computation.2 | async-start | bytes 16777216 | tf_op jit(solution)/shard_map/all_to_all | solution.py:182
where the time goes:
time: 561 us; the launch traced here: 555 us
  matrix products  248 us (44%)
  waiting for transfers between devices  120 us (21%)
  local copies, waits for them, and re-layouts  67.9 us (12%)
  blocking collectives  59.1 us (11%)
  other arithmetic  39.3 us (7%)
  starting transfers between devices  18.4 us (3%)
    dot_general x8, matrix products, grid_block(): lax.dot_general(row_table, col_table, (((0,), (0,)), ((), ())), preferred...  154 us
    all_to_all x1, waiting for transfers between devices, local(): lax.all_to_all(stacked, TILE, split_axis=2, concat_axis=1, tiled=True)  112 us
    all_to_all x1, blocking collectives, summed_on_arrival(): lax.all_to_all(blocks, axis, split_axis=0, concat_axis=0, tiled=True)  54.3 us
    sub x1, other arithmetic, local(): screened = jnp.cos(phase) * image_parts[0] - jnp.sin(phase) * image_parts[1]  16.9 us
    select_n x8, other arithmetic, grid_block(): jnp.where(rel_row == tap_index, weight_re[:, tap_index:tap_index + 1], ro...  12.7 us
    all_to_all x1, starting transfers between devices, moved_by_axis(): lax.all_to_all(blocks, axes[k], split_axis=k, concat_axis=k, tiled=True)  11.5 us
  transfers between devices with their start and end apart: 3, of which 2 were waited for; matrix products, arithmetic and copies ran while one was open for 1% of the time, Pallas kernels for 0%

commit v1 on v0

v1 whole, which is shorter than its diff:
```python
import math

import jax
import jax.numpy as jnp
import numpy as np
from jax import lax
from jax.experimental import pallas as pl
from jax.experimental.pallas import tpu as pltpu
from jax.sharding import Mesh
from jax.sharding import PartitionSpec as P

G = 4096
TILE = ("tile_0", "tile_1", "tile_2")
PLANE = ("plane_0", "plane_1")
PLANE_TILE = PLANE + TILE
BANDS = 16
CAP = 32
PAIR = 2
COLS = 128
SETS = PAIR * BANDS
GROUPS = 32

SIN = (6.283183359351797, -41.341456456971535, 81.59688036372165, -76.58598132852413,
       41.227609837804344, -12.302204294679466)
COS = (0.9999996601928737, -19.739032170917408, 64.93001305163173, -85.28516993938109,
       58.84794870978477, -21.158227293307913)


def horner(u, coefs):
    total = jnp.full_like(u, coefs[-1])
    for c in coefs[-2::-1]:
        total = total * u + c
    return total


def cis(turn):
    u = turn * turn
    return horner(u, COS), turn * horner(u, SIN)


def cis_int(k):
    return cis((((k + 2048) & 4095) - 2048).astype(jnp.float32) * (1.0 / 4096))


def mul(a, b):
    return a[0] * b[0] - a[1] * b[1], a[0] * b[1] + a[1] * b[0]


def add(a, b):
    return a[0] + b[0], a[1] + b[1]


def sub(a, b):
    return a[0] - b[0], a[1] - b[1]


def turned(a, k, n):
    k = k % n
    if k == 0:
        return a
    if 4 * k == n:
        return -a[1], a[0]
    if 8 * k == n:
        h = math.sqrt(0.5)
        return (a[0] - a[1]) * h, (a[0] + a[1]) * h
    if 8 * k == 3 * n:
        h = math.sqrt(0.5)
        return (-a[0] - a[1]) * h, (a[0] - a[1]) * h
    c, s = math.cos(2 * math.pi * k / n), math.sin(2 * math.pi * k / n)
    return a[0] * c - a[1] * s, a[0] * s + a[1] * c


def fft(xs):
    n = len(xs)
    if n == 1:
        return xs
    even, odd = fft(xs[0::2]), fft(xs[1::2])
    odd = [turned(o, k, n) for k, o in enumerate(odd)]
    return [add(e, o) for e, o in zip(even, odd)] + [sub(e, o) for e, o in zip(even, odd)]


def dft_matrix():
    n = 256
    k = np.outer(np.arange(n), np.arange(n)) % n
    w = np.concatenate([np.cos(2 * np.pi * k / n), np.sin(2 * np.pi * k / n)]).astype(np.float32)
    hi = w.astype(jnp.bfloat16)
    lo = (w - hi.astype(np.float32)).astype(jnp.bfloat16)
    return np.concatenate([hi, lo, hi], axis=1)


def kernel(first_ref, w_ref, taps_ref, vis_ref, dft_ref, out_ref, p_ref, q_ref, o_ref, e_ref, h_ref, y_ref):
    first = first_ref[0]

    def set_step(s, carry):
        off = vis_ref[2, s].astype(jnp.int32)
        col = off & (G - 1)
        row = off >> 12
        place = ((row & 15) << 4) | (row >> 4)
        p_ref[16] = place.astype(jnp.float32)
        base = (vis_ref[0, s], vis_ref[1, s])
        one = cis_int(col)
        base = mul(base, cis_int(col * first))
        power = one
        q_ref[0] = jnp.ones((GROUPS, 128), jnp.float32)
        q_ref[16] = jnp.zeros((GROUPS, 128), jnp.float32)
        for k in range(1, 16):
            q_ref[k] = power[0]
            q_ref[16 + k] = power[1]
            power = mul(power, one)
        for k in range(8):
            p_ref[k] = base[0]
            p_ref[8 + k] = base[1]
            if k < 7:
                base = mul(base, power)

        rows = lax.broadcasted_iota(jnp.int32, (256, 128), 0).astype(jnp.float32)

        def group_step(g, c):
            lanes = pl.ds(pl.multiple_of(g * 128, 128), 128)
            here = p_ref[16, pl.ds(g, 1), :]
            o_ref[:, lanes] = jnp.where(rows == here, 1.0, 0.0).astype(jnp.bfloat16)
            qr = q_ref[0:16, pl.ds(g, 1), :].reshape(16, 128)
            qi = q_ref[16:32, pl.ds(g, 1), :].reshape(16, 128)
            for k in range(8):
                pr = p_ref[k, pl.ds(g, 1), :]
                pi = p_ref[8 + k, pl.ds(g, 1), :]
                e_ref[16 * k : 16 * k + 16, lanes] = (pr * qr - pi * qi).astype(jnp.bfloat16)
                e_ref[128 + 16 * k : 144 + 16 * k, lanes] = (pr * qi + pi * qr).astype(jnp.bfloat16)
            return c

        lax.fori_loop(0, GROUPS, group_step, 0)
        acc = lax.dot_general(
            o_ref[...], e_ref[...], (((1,), (1,)), ((), ())), preferred_element_type=jnp.float32
        )
        plane = s // BANDS
        at = pl.ds(pl.multiple_of((s % BANDS) * 16, 16), 16)
        for k in range(16):
            h_ref[plane * 16 + k, at, :] = acc[16 * k : 16 * k + 16, :]
        return carry

    lax.fori_loop(0, SETS, set_step, 0)

    def dft_step(k, carry):
        x = h_ref[k]
        hi = x.astype(jnp.bfloat16)
        lo = (x - hi.astype(jnp.float32)).astype(jnp.bfloat16)
        both = jnp.concatenate([hi, hi, lo], axis=0)
        r = jnp.dot(dft_ref[...], both, preferred_element_type=jnp.float32)
        y_ref[k, :, 0:128] = r[:256, :128] - r[256:, 128:]
        y_ref[k, :, 128:256] = r[:256, 128:] + r[256:, :128]
        return carry

    lax.fori_loop(0, PAIR * 16, dft_step, 0)

    lane = lax.broadcasted_iota(jnp.int32, (8, 128), 1) + first
    sub_row = lax.broadcasted_iota(jnp.int32, (8, 128), 0)
    step = cis_int(lane)
    weight = [taps_ref[k].astype(jnp.bfloat16).astype(jnp.float32) * (1.0 / 512) for k in range(8)]
    b = (jnp.full((8, 128), weight[7]), jnp.zeros((8, 128), jnp.float32))
    for k in range(6, -1, -1):
        b = mul(b, step)
        b = (b[0] + weight[k], b[1])

    def cosine(index):
        return (((index + 2048) & 4095) - 2048).astype(jnp.float32) * (0.5 / G)

    y2 = cosine(lane)
    y2 = y2 * y2

    def tile_step(t, carry):
        at = pl.ds(pl.multiple_of(t * 8, 8), 8)
        line = sub_row + t * 8
        tw = [None, cis_int(line)]
        for k in range(2, 16):
            tw.append(mul(tw[k // 2], tw[k - k // 2]))
        sums = None
        for q in range(PAIR):
            xs = []
            for k in range(16):
                x = (y_ref[q * 16 + k, at, 0:128], y_ref[q * 16 + k, at, 128:256])
                xs.append(x if k == 0 else mul(x, tw[k]))
            f = fft(xs)
            new = []
            for j in range(16):
                x2 = cosine(line + 256 * j)
                s = x2 * x2 + y2
                n = -s / (1.0 + jnp.sqrt(1.0 - s))
                turn = w_ref[q] * n
                turn = turn - jnp.round(turn)
                term = mul(f[j], cis(turn))
                new.append(term if sums is None else add(sums[j], term))
            sums = new
        zero = jnp.zeros((8, 128), jnp.float32)
        ts = [(jnp.full((8, 128), taps_ref[0]), zero)]
        ts += [(tw[k][0] * taps_ref[k], tw[k][1] * taps_ref[k]) for k in range(1, 8)]
        ts += [(zero, zero)] * 8
        a = fft(ts)
        for j in range(16):
            ab = mul(a[j], b)
            out_ref[pl.ds(pl.multiple_of(t * 8 + 256 * j, 8), 8), :] = sums[j][0] * ab[0] - sums[j][1] * ab[1]
        return carry

    lax.fori_loop(0, 32, tile_step, 0)


def part_image(first, w, taps, vis, interpret=False):
    smem = pl.BlockSpec(memory_space=pltpu.SMEM)
    vmem = pl.BlockSpec(memory_space=pltpu.VMEM)
    return pl.pallas_call(
        kernel,
        out_shape=jax.ShapeDtypeStruct((G, COLS), jnp.float32),
        in_specs=[smem, smem, smem, vmem, vmem],
        out_specs=vmem,
        scratch_shapes=[
            pltpu.VMEM((17, GROUPS, 128), jnp.float32),
            pltpu.VMEM((32, GROUPS, 128), jnp.float32),
            pltpu.VMEM((256, GROUPS * 128), jnp.bfloat16),
            pltpu.VMEM((256, GROUPS * 128), jnp.bfloat16),
            pltpu.VMEM((PAIR * 16, 256, 256), jnp.float32),
            pltpu.VMEM((PAIR * 16, 256, 256), jnp.float32),
        ],
        compiler_params=pltpu.CompilerParams(vmem_limit_bytes=56 * 1024 * 1024),
        interpret=interpret,
    )(first, w, taps, vis, dft_matrix())


def local(visibility, target, offset, taps, w_plane):
    dest = target[:, 0]
    onehot = (dest[:, None] == jnp.arange(128, dtype=jnp.int32)[None, :]).astype(jnp.int32)
    rank = jnp.sum(jnp.cumsum(onehot, axis=0) * onehot, axis=1) - 1
    plane, band = dest // BANDS, dest % BANDS
    bucket = ((plane % 4) * 2 + plane // 4) * BANDS + band
    slot = bucket * CAP + rank
    payload = jnp.stack([visibility[0], visibility[1], offset.astype(jnp.float32)])
    outgoing = jnp.zeros((3, 128 * CAP), jnp.float32).at[:, slot].set(payload)
    outgoing = outgoing.reshape(3, 4, SETS, CAP).transpose(1, 0, 2, 3).reshape(4, 3 * SETS, CAP)
    mine = lax.all_to_all(outgoing, "plane_1", split_axis=0, concat_axis=0, tiled=True)
    mine = mine.transpose(1, 0, 2).reshape(3 * SETS, 4 * CAP)
    mine = jnp.concatenate([mine, jnp.broadcast_to(w_plane[0], (8, 128))])
    everyone = lax.all_gather(mine, ("plane_0",) + TILE, axis=0)
    w = everyone[:, 3 * SETS, 0].reshape(2, 16)[:, 0]
    vis = everyone[:, : 3 * SETS].transpose(1, 0, 2).reshape(3, SETS, GROUPS, 128)
    first = lax.axis_index(TILE) * 256 + lax.axis_index("plane_0") * COLS
    part = part_image(first.reshape(1).astype(jnp.int32), w, taps, vis)
    arrived = lax.all_to_all(part, PLANE, split_axis=0, concat_axis=0, tiled=True)
    total = arrived.reshape(2, 4, 512, COLS).sum(axis=1)
    return jnp.concatenate([total[0], total[1]], axis=1)


def solution(mesh):
    finer = Mesh(
        mesh.devices.reshape(2, 4, 2, 4, 2), ("plane_0", "plane_1", "tile_0", "tile_1", "tile_2")
    )
    return jax.shard_map(
        local,
        mesh=finer,
        in_specs=(P(None, PLANE_TILE), P(PLANE_TILE, None), P(PLANE_TILE), P(), P(PLANE)),
        out_specs=P(PLANE, TILE),
        check_vma=False,
    )
```

time: 561 us -> 231 us (0.41)
  matrix products: 248 us -> 0 us
  Pallas kernels: 0 us -> 108 us
  waiting for transfers between devices: 120 us -> 49.6 us
  local copies, waits for them, and re-layouts: 67.9 us -> 16.1 us
  other arithmetic: 39.3 us -> 2.86 us
  blocking collectives: 59.1 us -> 34.5 us
  starting transfers between devices: 18.4 us -> 4.83 us
  between operations: 1.52 us -> 14.2 us
    dot_general x24 -> x0, matrix products: 248 us -> none  [the longest x8 154 us: grid_block(): lax.dot_general(row_table, col_table, (((0,), (0,)), ((), ())), preferred...]
    all_to_all x2 -> x1, waiting for transfers between devices: 120 us -> 3.82 us  [local(): lax.all_to_all(outgoing, 'plane_1', split_axis=0, concat_axis=0, tiled=True)]
    pallas_call x0 -> x1, Pallas kernels: none -> 108 us  [part_image(): pl.pallas_call(kernel, out_shape=jax.ShapeDtypeStruct((G, COLS), jnp.floa...]
    all_gather x0 -> x1, waiting for transfers between devices: none -> 45.8 us  [local(): everyone = lax.all_gather(mine, ('plane_0',) + TILE, axis=0)]
    all_to_all x2 -> x1, blocking collectives: 59.1 us -> 34.5 us  [local(): lax.all_to_all(part, PLANE, split_axis=0, concat_axis=0, tiled=True)]
    slice x27 -> x2, local copies, waits for them, and re-layouts: 19.4 us -> 1.85 us  [local(): w = everyone[:, 3 * SETS, 0].reshape(2, 16)[:, 0]]
    sub x2 -> x0, other arithmetic: 17 us -> none  [the longest x1 16.9 us: local(): screened = jnp.cos(phase) * image_parts[0] - jnp.sin(phase) * image_parts[1]]
    select_n x17 -> x1, other arithmetic: 12.8 us -> 0.14 us  [local(): outgoing = jnp.zeros((3, 128 * CAP), jnp.float32).at[:, slot].set(payload)]
  transfers between devices with their start and end apart: 3 -> 2, of which waited for: 2 -> 2; matrix products, arithmetic and copies ran while one was open for 1% -> 0% of each run, Pallas kernels for 0% -> 0%
where the time goes in v1:
time: 231 us; the launch traced here: 230 us
  Pallas kernels  108 us (47%)
  waiting for transfers between devices  49.6 us (21%)
  blocking collectives  34.5 us (15%)
  local copies, waits for them, and re-layouts  16.1 us (7%)
  between operations  14.2 us (6%)
  starting transfers between devices  4.83 us (2%)
  other arithmetic  2.86 us (1%)
    pallas_call x1, Pallas kernels, part_image(): pl.pallas_call(kernel, out_shape=jax.ShapeDtypeStruct((G, COLS), jnp.floa...  108 us
    all_gather x1, waiting for transfers between devices, local(): everyone = lax.all_gather(mine, ('plane_0',) + TILE, axis=0)  45.8 us
    all_to_all x1, blocking collectives, local(): lax.all_to_all(part, PLANE, split_axis=0, concat_axis=0, tiled=True)  34.5 us
    scatter x1, local copies, waits for them, and re-layouts, local(): outgoing = jnp.zeros((3, 128 * CAP), jnp.float32).at[:, slot].set(payload)  6.1 us
    all_to_all x1, starting transfers between devices, local(): lax.all_to_all(outgoing, 'plane_1', split_axis=0, concat_axis=0, tiled=True)  4.83 us
  transfers between devices with their start and end apart: 2, of which 2 were waited for; matrix products, arithmetic and copies ran while one was open for 0% of the time, Pallas kernels for 0%

profile of v1, /device:TPU:1, one launch (start us, length us, event | category | flops | bytes accessed | tf_op | source)
XLA Modules:
  0.0 230.1 jit_solution(15168699077894161976)
XLA Ops:
  6.5 0.7 convert_element_type.9
  7.2 0.8 copy.22
  8.0 0.3 fusion.1
  8.4 0.0 copy-start
  8.4 0.1 broadcast_add_fusion
  8.5 0.0 copy-start.1
  8.5 0.3 copy.23
  8.9 0.2 copy-done
  9.1 0.6 fusion
  9.8 0.1 compare_select_fusion
  9.9 0.0 copy-done.1
  9.9 0.4 copy.24
  10.3 6.1 %scatter_custom_fusion = f32[3,4096]{0,1:T(8,128)S(1)} fusion(s32[2048]{0:T(1024)S(1)} %bitcast.48, f32[2048,3]{1,0:T(8,128)S(1)} %copy.24, f32[]{:T(128)} %constant.78.clone.1), kind=kCustom, calls=%fused_computation.9 | custom fusion | bytes 49156 | tf_op jit(solution)/shard_map/scatter | solution.py:235
  16.4 1.2 copy.25
  17.7 0.8 reshape.49
  18.5 4.8 %all-to-all-start = ((f32[4,96,32]{1,2,0:T(8,128)}), f32[4,96,32]{1,2,0:T(8,128)S(1)}, u32[]{:S(2)}, u32[]{:S(2)}) async-start(f32[4,96,32]{1,2,0:T(8,128)} %reshape.49), calls=%async_computation | async-start | bytes 131072 | tf_op jit(solution)/shard_map/all_to_all | solution.py:237
  23.3 0.0 all-gather.3.cloned.1.call-start
  23.9 3.8 %all-to-all-done = f32[4,96,32]{1,2,0:T(8,128)S(1)} async-done(((f32[4,96,32]{1,2,0:T(8,128)}), f32[4,96,32]{1,2,0:T(8,128)S(1)}, u32[]{:S(2)}, u32[]{:S(2)}) %all-to-all-start) | async-done | bytes 49184 | tf_op jit(solution)/shard_map/all_to_all | solution.py:237
  27.8 0.1 copy.28
  27.8 0.6 concatenate.6.clone
  28.5 0.0 all-gather.3.cloned.1.call-update
  28.5 45.8 %all-gather.3.cloned.1.call-done = f32[3328,128]{1,0:T(8,128)} async-done(((f32[104,128]{1,0:T(8,128)}), f32[3328,128]{1,0:T(8,128)}) %all-gather.3.cloned.1.call-update) | async-done | bytes 1703952 | tf_op jit(solution)/shard_map/all_gather | solution.py:240
  74.3 1.2 slice_reduce_fusion
  75.5 1.5 slice_bitcast_fusion
  77.1 2.1 copy.27
  79.1 0.1 reshape_squeeze.3
  79.2 0.6 slice_reduce_fusion.1.w_ref
  79.8 107.9 %shard_map.64 = f32[4096,128]{1,0:T(8,128)} custom-call(s32[1]{0:T(128)} %bitcast.first_ref, f32[2]{0:T(128)} %slice_reduce_fusion.1.w_ref, f32[8]{0:T(128)} %taps_ref.1, f32[3,32,32,128]{3,2,1,0:T(8,128)} %bitcast.39, bf16[512,768]{1,0:T(8,128)(2,1)} %constant.88.clone.dft_ref), custom_call_target="tpu_custom_call" | custom-call | tf_op jit(solution)/shard_map/pallas_call | solution.py:209
  187.8 34.5 %all_to_all.14 = f32[8,512,128]{2,1,0:T(8,128)S(1)} all-to-all(f32[8,512,128]{2,1,0:T(8,128)} %bitcast.38), channel_id=1, replica_groups=mesh['plane_0'=2,'plane_1'=4,'tile_0'=2,'tile_1'=4,'tile_2'=2] {'plane_0..., dimensions={0} | all-to-all | bytes 4194304 | tf_op jit(solution)/shard_map/all_to_all | solution.py:245
  222.2 0.1 bitcast_reduce_fusion
  222.4 0.8 pad_maximum_fusion
  (6 shorter events, 0.1 us)
Async XLA Ops:
  8.4 0.7 copy-start
  8.5 1.4 copy-start.1
  18.5 9.3 %all-to-all-start = ((f32[4,96,32]{1,2,0:T(8,128)}), f32[4,96,32]{1,2,0:T(8,128)S(1)}, u32[]{:S(2)}, u32[]{:S(2)}) async-start(f32[4,96,32]{1,2,0:T(8,128)} %reshape.49), calls=%async_computation | async-start | bytes 131072 | tf_op jit(solution)/shard_map/all_to_all | solution.py:237
  23.3 51.0 %all-gather.3.cloned.1.call-start = ((), (), s32[]{:S(2)}) async-start(), calls=%async_computation.2 | async-start | bytes 1757184 | tf_op jit(solution)/shard_map/all_gather | solution.py:240
Sparse Core Ops, SparseCore 0:
  28.6 45.6 all-gather.2

commit v2 on v1

v2 whole, which is shorter than its diff:
```python
import math

import jax
import jax.numpy as jnp
import numpy as np
from jax import lax
from jax.experimental import pallas as pl
from jax.experimental.pallas import tpu as pltpu
from jax.sharding import Mesh
from jax.sharding import PartitionSpec as P

G = 4096
TILE = ("tile_0", "tile_1", "tile_2")
PLANE = ("plane_0", "plane_1")
PLANE_TILE = PLANE + TILE
BANDS = 16
CAP = 32
PAIR = 2
COLS = 128
SETS = PAIR * BANDS
UNROLL = 32
SKIP = 33
ROWS = 3 * 32 + 8
GROUPS = 32

SIN = (6.283183359351797, -41.341456456971535, 81.59688036372165, -76.58598132852413,
       41.227609837804344, -12.302204294679466)
COS = (0.9999996601928737, -19.739032170917408, 64.93001305163173, -85.28516993938109,
       58.84794870978477, -21.158227293307913)


def horner(u, coefs):
    total = jnp.full_like(u, coefs[-1])
    for c in coefs[-2::-1]:
        total = total * u + c
    return total


def cis(turn):
    u = turn * turn
    return horner(u, COS), turn * horner(u, SIN)


def cis_int(k):
    return cis((((k + 2048) & 4095) - 2048).astype(jnp.float32) * (1.0 / 4096))


def cis_half(k):
    return cis((((k + 4096) & 8191) - 4096).astype(jnp.float32) * (1.0 / 8192))


def mul(a, b):
    return a[0] * b[0] - a[1] * b[1], a[0] * b[1] + a[1] * b[0]


def add(a, b):
    return a[0] + b[0], a[1] + b[1]


def sub(a, b):
    return a[0] - b[0], a[1] - b[1]


def turned(a, k, n):
    k = k % n
    if k == 0:
        return a
    if 4 * k == n:
        return -a[1], a[0]
    if 8 * k == n:
        h = math.sqrt(0.5)
        return (a[0] - a[1]) * h, (a[0] + a[1]) * h
    if 8 * k == 3 * n:
        h = math.sqrt(0.5)
        return (-a[0] - a[1]) * h, (a[0] - a[1]) * h
    c, s = math.cos(2 * math.pi * k / n), math.sin(2 * math.pi * k / n)
    return a[0] * c - a[1] * s, a[0] * s + a[1] * c


def fft(xs):
    n = len(xs)
    if n == 1:
        return xs
    even, odd = fft(xs[0::2]), fft(xs[1::2])
    odd = [turned(o, k, n) for k, o in enumerate(odd)]
    return [add(e, o) for e, o in zip(even, odd)] + [sub(e, o) for e, o in zip(even, odd)]


def dft_matrix():
    n = 256
    k = np.outer(np.arange(n), np.arange(n)) % n
    w = np.concatenate([np.cos(2 * np.pi * k / n), np.sin(2 * np.pi * k / n)]).astype(np.float32)
    hi = w.astype(jnp.bfloat16)
    lo = (w - hi.astype(np.float32)).astype(jnp.bfloat16)
    return np.concatenate([hi, lo, hi], axis=1)


def kernel(
    first_ref, taps_ref, *refs
):
    vis_refs, refs = refs[:8], refs[8:]
    dft_ref, out_ref, p0_ref, p1_ref, q0_ref, q1_ref, acc_ref, h_ref, y_ref = refs

    def values(v, s):
        rows = pl.ds(pl.multiple_of(4 * (v * SETS + s), 4), 4)
        return jnp.concatenate([ref[rows, :] for ref in vis_refs])

    first = first_ref[0]

    def tables(s, p_ref, q_ref):
        off = values(2, s).astype(jnp.int32)
        col = off & (G - 1)
        row = off >> 12
        p_ref[pl.ds(16 * GROUPS, GROUPS), :] = (row & 15).astype(jnp.float32)
        p_ref[pl.ds(17 * GROUPS, GROUPS), :] = (row >> 4).astype(jnp.float32)
        half = cis_half(col)
        one = mul(half, half)
        base = mul((values(0, s), values(1, s)), cis_half(col * (2 * first + 15)))
        power = half
        for k in range(8):
            q_ref[pl.ds(k * SKIP, GROUPS), :] = power[0]
            q_ref[pl.ds((8 + k) * SKIP, GROUPS), :] = power[1]
            if k < 7:
                power = mul(power, one)
        step = one
        for k in range(4):
            step = mul(step, step)
        for k in range(8):
            p_ref[pl.ds(k * GROUPS, GROUPS), :] = base[0]
            p_ref[pl.ds((8 + k) * GROUPS, GROUPS), :] = base[1]
            if k < 7:
                base = mul(base, step)

    sub16 = lax.broadcasted_iota(jnp.int32, (16, 128), 0).astype(jnp.float32).astype(jnp.bfloat16)
    yes = jnp.ones((16, 128), jnp.bfloat16)
    no = jnp.zeros((16, 128), jnp.bfloat16)

    def made(g, p_ref, q_ref):
        def spread(row):
            return jnp.broadcast_to(p_ref[pl.ds(row * GROUPS + g, 1), :], (16, 128)).astype(jnp.bfloat16)

        high = jnp.where(spread(17) == sub16, spread(16), -yes)
        o = [jnp.where(high == jnp.bfloat16(k), yes, no) for k in range(16)]
        qr = q_ref[pl.ds(g, 8, stride=SKIP), :]
        qi = q_ref[pl.ds(8 * SKIP + g, 8, stride=SKIP), :]
        products = []
        for part, q in ((0, qr), (8, qi), (0, qi), (8, qr)):
            for k in range(0, 8, 2):
                two = [p_ref[pl.ds((part + k + j) * GROUPS + g, 1), :] * q for j in range(2)]
                products.append(jnp.concatenate(two).astype(jnp.bfloat16))
        return jnp.concatenate(o), jnp.concatenate(products)

    def phase(used, later, s):
        def chunk(k, c):
            parts = [made(k * UNROLL + j, *used) for j in range(UNROLL)]
            o = jnp.concatenate([x[0] for x in parts], axis=1)
            e = jnp.concatenate([x[1] for x in parts], axis=1)
            part = lax.dot_general(o, e, (((1,), (1,)), ((), ())), preferred_element_type=jnp.float32)
            if UNROLL == GROUPS:
                put(part)
            else:
                acc_ref[...] += part
            return c

        plane = s // BANDS
        at = pl.ds(pl.multiple_of((s % BANDS) * 16, 16), 16)

        def put(part):
            for k in range(16):
                h_ref[plane * 16 + k, at, :] = part[16 * k : 16 * k + 16, :]

        tables(jnp.minimum(s + 1, SETS - 1), *later)
        if UNROLL == GROUPS:
            chunk(0, 0)
        else:
            acc_ref[...] = jnp.zeros((256, 256), jnp.float32)
            lax.fori_loop(0, GROUPS // UNROLL, chunk, 0)
            put(acc_ref[...])

    buf0, buf1 = (p0_ref, q0_ref), (p1_ref, q1_ref)
    tables(0, *buf0)

    def two_sets(i, c):
        phase(buf0, buf1, 2 * i)
        phase(buf1, buf0, 2 * i + 1)
        return c

    lax.fori_loop(0, SETS // 2, two_sets, 0)

    sign = jnp.where(lax.broadcasted_iota(jnp.int32, (256, 128), 1) < 64, -1.0, 1.0)

    def dft_step(i, carry):
        for j in range(2):
            k = 2 * i + j
            re, im = h_ref[k, :, 0:128], h_ref[k, :, 128:256]
            re = re + sign * pltpu.roll(re, 64, 1)
            im = im - sign * pltpu.roll(im, 64, 1)
            x = jnp.concatenate([re, im], axis=1)
            hi = x.astype(jnp.bfloat16)
            lo = (x - hi.astype(jnp.float32)).astype(jnp.bfloat16)
            both = jnp.concatenate([hi, hi, lo], axis=0)
            r = jnp.dot(dft_ref[...], both, preferred_element_type=jnp.float32)
            y_ref[k, :, 0:128] = r[:256, :128] - r[256:, 128:]
            y_ref[k, :, 128:256] = r[:256, 128:] + r[256:, :128]
        return carry

    lax.fori_loop(0, PAIR * 8, dft_step, 0)

    place = lax.broadcasted_iota(jnp.int32, (8, 128), 1)
    lower = place & 63
    lane = 2 * (lower - (lower & 7)) + jnp.where(place < 64, 8 + (lower & 7), 7 - (lower & 7))
    inner = place & 15
    source = ((place - inner) >> 1) + jnp.where(inner < 8, 71 - inner, inner - 8)
    lane = lane + first
    sub_row = lax.broadcasted_iota(jnp.int32, (8, 128), 0)
    step = cis_int(lane)
    weight = [taps_ref[k].astype(jnp.bfloat16).astype(jnp.float32) * (1.0 / 512) for k in range(8)]
    b = (jnp.full((8, 128), weight[7]), jnp.zeros((8, 128), jnp.float32))
    for k in range(6, -1, -1):
        b = mul(b, step)
        b = (b[0] + weight[k], b[1])

    def cosine(index):
        return (((index + 2048) & 4095) - 2048).astype(jnp.float32) * (0.5 / G)

    y2 = cosine(lane)
    y2 = y2 * y2
    w_row = sum(ref[pl.ds(4 * 3 * SETS, 1), :] for ref in vis_refs[:4]) * 0.5
    w = [jnp.broadcast_to(w_row[:, q : q + 1], (8, 128)) for q in range(PAIR)]

    def tile_step(t, carry):
        at = pl.ds(pl.multiple_of(t * 8, 8), 8)
        line = sub_row + t * 8
        tw = [None, cis_int(line)]
        for k in range(2, 16):
            tw.append(mul(tw[k // 2], tw[k - k // 2]))
        sums = None
        for q in range(PAIR):
            xs = []
            for k in range(16):
                x = (y_ref[q * 16 + k, at, 0:128], y_ref[q * 16 + k, at, 128:256])
                xs.append(x if k == 0 else mul(x, tw[k]))
            f = fft(xs)
            new = []
            for j in range(16):
                x2 = cosine(line + 256 * j)
                s = x2 * x2 + y2
                n = -s / (1.0 + jnp.sqrt(1.0 - s))
                turn = w[q] * n
                turn = turn - jnp.round(turn)
                term = mul(f[j], cis(turn))
                new.append(term if sums is None else add(sums[j], term))
            sums = new
        zero = jnp.zeros((8, 128), jnp.float32)
        ts = [(jnp.full((8, 128), taps_ref[0]), zero)]
        ts += [(tw[k][0] * taps_ref[k], tw[k][1] * taps_ref[k]) for k in range(1, 8)]
        ts += [(zero, zero)] * 8
        a = fft(ts)
        for j in range(16):
            ab = mul(a[j], b)
            pixel = sums[j][0] * ab[0] - sums[j][1] * ab[1]
            rows = pl.ds(pl.multiple_of(t * 8 + 256 * j, 8), 8)
            out_ref[rows, :] = jnp.take_along_axis(pixel, source, axis=1)
        return carry

    lax.fori_loop(0, 32, tile_step, 0)


def part_image(first, taps, *vis, interpret=False):
    smem = pl.BlockSpec(memory_space=pltpu.SMEM)
    vmem = pl.BlockSpec(memory_space=pltpu.VMEM)
    return pl.pallas_call(
        kernel,
        out_shape=jax.ShapeDtypeStruct((G, COLS), jnp.float32),
        in_specs=[smem, smem] + [vmem] * 9,
        out_specs=vmem,
        scratch_shapes=[
            pltpu.VMEM((18 * GROUPS, 128), jnp.float32),
            pltpu.VMEM((18 * GROUPS, 128), jnp.float32),
            pltpu.VMEM((16 * SKIP, 128), jnp.float32),
            pltpu.VMEM((16 * SKIP, 128), jnp.float32),
            pltpu.VMEM((256, 256), jnp.float32),
            pltpu.VMEM((PAIR * 16, 256, 256), jnp.float32),
            pltpu.VMEM((PAIR * 16, 256, 256), jnp.float32),
        ],
        compiler_params=pltpu.CompilerParams(vmem_limit_bytes=56 * 1024 * 1024),
        interpret=interpret,
    )(first, taps, *vis, dft_matrix())


def shifted(x, axis, by):
    length = lax.axis_size(axis)
    return lax.ppermute(x, axis, [(i, (i + by) % length) for i in range(length)])


def local(visibility, target, offset, taps, w_plane):
    dest = target[:, 0]
    onehot = (dest[:, None] == jnp.arange(128, dtype=jnp.int32)[None, :]).astype(jnp.int32)
    rank = jnp.sum(jnp.cumsum(onehot, axis=0) * onehot, axis=1) - 1
    plane, band = dest // BANDS, dest % BANDS
    bucket = ((plane % 4) * 2 + plane // 4) * BANDS + band
    slot = bucket * CAP + rank
    payload = jnp.stack([visibility[0], visibility[1], offset.astype(jnp.float32)])
    outgoing = jnp.zeros((3, 128 * CAP), jnp.float32).at[:, slot].set(payload)
    outgoing = outgoing.reshape(3, 4, SETS, CAP).transpose(1, 0, 2, 3).reshape(4, 3 * SETS, CAP)
    here = lax.axis_index("plane_1")
    mine = []
    for by in range(4):
        block = lax.dynamic_index_in_dim(outgoing, (here + by) % 4, 0, keepdims=False)
        mine.append(block if by == 0 else shifted(block, "plane_1", by))
    mine = jnp.concatenate(mine, axis=1)
    half = lax.axis_index("plane_0")
    w_row = jnp.where(jnp.arange(128) == half, w_plane[0], 0.0)
    mine = jnp.concatenate([mine, jnp.broadcast_to(w_row, (8, 128))])
    line = [mine] + [shifted(mine, "tile_1", by) for by in (1, 2, 3)]
    line = jnp.stack(line, axis=1).reshape(ROWS * 4, 128)
    area = [line] + [shifted(line, ("plane_0", "tile_0"), by) for by in (1, 2, 3)]
    area = area + [shifted(x, "tile_2", 1) for x in area]
    first = lax.axis_index(TILE) * 256 + half * COLS
    part = part_image(first.reshape(1).astype(jnp.int32), taps, *area)
    arrived = lax.all_to_all(part, PLANE, split_axis=0, concat_axis=0, tiled=True)
    total = arrived.reshape(2, 4, 512, COLS).sum(axis=1)
    return jnp.concatenate([total[0], total[1]], axis=1)


def solution(mesh):
    finer = Mesh(
        mesh.devices.reshape(2, 4, 2, 4, 2), ("plane_0", "plane_1", "tile_0", "tile_1", "tile_2")
    )
    return jax.shard_map(
        local,
        mesh=finer,
        in_specs=(P(None, PLANE_TILE), P(PLANE_TILE, None), P(PLANE_TILE), P(), P(PLANE)),
        out_specs=P(PLANE, TILE),
        check_vma=False,
    )
```

time: 231 us -> 131 us (0.57)
  Pallas kernels: 108 us -> 50.8 us
  waiting for transfers between devices: 49.6 us -> 6.78 us
  starting transfers between devices: 4.83 us -> 26.6 us
  between operations: 14.2 us -> 0.92 us
  local copies, waits for them, and re-layouts: 16.1 us -> 10.2 us
  blocking collectives: 34.5 us -> 32.1 us
    pallas_call x1, Pallas kernels: 108 us -> 50.8 us  [part_image(): pl.pallas_call(kernel, out_shape=jax.ShapeDtypeStruct((G, COLS), jnp.floa...]
    all_gather x1 -> x0, waiting for transfers between devices: 45.8 us -> none  [local(): everyone = lax.all_gather(mine, ('plane_0',) + TILE, axis=0)]
    ppermute x0 -> x13, starting transfers between devices: none -> 26.6 us  [shifted(): lax.ppermute(x, axis, [(i, (i + by) % length) for i in range(length)])]
    ppermute x0 -> x13, waiting for transfers between devices: none -> 6.78 us  [shifted(): lax.ppermute(x, axis, [(i, (i + by) % length) for i in range(length)])]
    all_to_all x1 -> x0, starting transfers between devices: 4.83 us -> none  [local(): lax.all_to_all(outgoing, 'plane_1', split_axis=0, concat_axis=0, tiled=True)]
    all_to_all x1 -> x0, waiting for transfers between devices: 3.82 us -> none  [local(): lax.all_to_all(outgoing, 'plane_1', split_axis=0, concat_axis=0, tiled=True)]
    transpose x2 -> x0, local copies, waits for them, and re-layouts: 3.58 us -> none  [local(): everyone[:, :3 * SETS].transpose(1, 0, 2).reshape(3, SETS, GROUPS, 128)]
    all_to_all x1, blocking collectives: 34.5 us -> 32.1 us  [local(): lax.all_to_all(part, PLANE, split_axis=0, concat_axis=0, tiled=True)]
  transfers between devices with their start and end apart: 2 -> 13, of which waited for: 2 -> 5; matrix products, arithmetic and copies ran while one was open for 0% -> 0% of each run, Pallas kernels for 0% -> 0%
where the time goes in v2:
time: 131 us; the launch traced here: 130 us
  Pallas kernels  50.8 us (39%)
  blocking collectives  32.1 us (25%)
  starting transfers between devices  26.6 us (20%)
  local copies, waits for them, and re-layouts  10.2 us (8%)
  waiting for transfers between devices  6.78 us (5%)
  other arithmetic  2.97 us (2%)
    pallas_call x1, Pallas kernels, part_image(): pl.pallas_call(kernel, out_shape=jax.ShapeDtypeStruct((G, COLS), jnp.floa...  50.8 us
    all_to_all x1, blocking collectives, local(): lax.all_to_all(part, PLANE, split_axis=0, concat_axis=0, tiled=True)  32.1 us
    ppermute x13, starting transfers between devices, shifted(): lax.ppermute(x, axis, [(i, (i + by) % length) for i in range(length)])  26.6 us
    ppermute x13, waiting for transfers between devices, shifted(): lax.ppermute(x, axis, [(i, (i + by) % length) for i in range(length)])  6.78 us
    scatter x1, local copies, waits for them, and re-layouts, local(): outgoing = jnp.zeros((3, 128 * CAP), jnp.float32).at[:, slot].set(payload)  6.1 us
  transfers between devices with their start and end apart: 13, of which 5 were waited for; matrix products, arithmetic and copies ran while one was open for 0% of the time, Pallas kernels for 0%

profile of v2, /device:TPU:1, one launch (start us, length us, event | category | flops | bytes accessed | tf_op | source)
XLA Modules:
  0.0 130.3 jit_solution(6051669400433242977)
XLA Ops:
  0.0 0.7 convert_element_type.9
  0.7 0.8 copy.19
  1.5 0.3 fusion.1
  1.9 0.0 copy-start.8
  1.9 0.1 broadcast_add_fusion
  2.0 0.0 copy-start.9
  2.0 0.3 copy.20
  2.3 0.2 copy-done.8
  2.6 0.6 fusion
  3.2 0.1 compare_select_fusion
  3.4 0.0 copy-done.9
  3.4 0.4 copy.21
  3.8 6.1 %scatter_custom_fusion = f32[3,4096]{0,1:T(8,128)S(1)} fusion(s32[2048]{0:T(1024)S(1)} %bitcast.59, f32[2048,3]{1,0:T(8,128)S(1)} %copy.21, f32[]{:T(128)} %constant.111.clone.1), kind=kCustom, calls=%fused_computation.8 | custom fusion | bytes 49156 | tf_op jit(solution)/shard_map/scatter | solution.py:304
  9.9 1.2 copy.22
  11.1 0.1 reshape.46
  11.3 3.4 %collective-permute-start.2 = (f32[96,32]{0,1:T(8,128)S(1)}, f32[96,32]{0,1:T(8,128)S(1)}, u32[]{:S(2)}, u32[]{:S(2)}) collective-permute-start(f32[96,32]{0,1:T(8,128)S(1)} %get-tuple-element.10), channel_id=1, source_target_pairs={{0,48},{16,0},{32,16},{48,32},{1,49},{17,1},{33,17},{49,33},{2,50}... | collective-permute-start | bytes 36872 | tf_op jit(solution)/shard_map/ppermute | solution.py:293
  14.7 0.5 collective-permute-start.1
  15.2 0.6 collective-permute-start
  16.5 0.0 collective-permute-done.2
  16.5 2.3 %collective-permute-done.1 = f32[96,32]{0,1:T(8,128)S(1)} collective-permute-done((f32[96,32]{0,1:T(8,128)S(1)}, f32[96,32]{0,1:T(8,128)S(1)}, u32[]{:S(2)}, u32[]{:S(2)}) %collective-permute-start.1) | collective-permute-done | bytes 12320 | tf_op jit(solution)/shard_map/ppermute | solution.py:293
  18.8 0.2 collective-permute-done
  19.0 0.1 broadcast_in_dim.19
  19.1 0.1 fusion.9
  19.2 3.0 %collective-permute-start.4 = (f32[104,128]{0,1:T(8,128)S(1)}, f32[104,128]{0,1:T(8,128)S(1)}, u32[]{:S(2)}, u32[]{:S(2)}) collective-permute-start(f32[104,128]{0,1:T(8,128)S(1)} %get-tuple-element.8), channel_id=1, source_target_pairs={{0,4},{2,6},{4,0},{6,2},{1,5},{3,7},{5,1},{7,3},{8,12},{10,14},{12... | collective-permute-start | bytes 159752 | tf_op jit(solution)/shard_map/ppermute | solution.py:293
  22.2 0.4 collective-permute-start.3
  22.6 2.3 %collective-permute-start.5 = (f32[104,128]{0,1:T(8,128)S(1)}, f32[104,128]{0,1:T(8,128)S(1)}, u32[]{:S(2)}, u32[]{:S(2)}) collective-permute-start(f32[104,128]{0,1:T(8,128)S(1)} %get-tuple-element.8), channel_id=1, source_target_pairs={{0,6},{2,0},{4,2},{6,4},{1,7},{3,1},{5,3},{7,5},{8,14},{10,8},{12,... | collective-permute-start | bytes 159752 | tf_op jit(solution)/shard_map/ppermute | solution.py:293
  24.9 0.0 collective-permute-done.4
  24.9 2.3 %collective-permute-done.3 = f32[104,128]{0,1:T(8,128)S(1)} collective-permute-done((f32[104,128]{0,1:T(8,128)S(1)}, f32[104,128]{0,1:T(8,128)S(1)}, u32[]{:S(2)}, u32[]{:S(2)}) %collective-permute-start.3) | collective-permute-done | bytes 53280 | tf_op jit(solution)/shard_map/ppermute | solution.py:293
  27.2 0.0 collective-permute-done.5
  27.2 0.1 copy.23
  27.4 0.0 copy-start
  27.4 3.8 %collective-permute-start.8 = (f32[416,128]{1,0:T(8,128)S(1)}, f32[416,128]{1,0:T(8,128)S(1)}, u32[]{:S(2)}, u32[]{:S(2)}) collective-permute-start(f32[416,128]{1,0:T(8,128)S(1)} %bitcast.47), channel_id=1, source_target_pairs={{0,72},{8,0},{64,8},{72,64},{1,73},{9,1},{65,9},{73,65},{2,74},{10... | collective-permute-start | bytes 638984 | tf_op jit(solution)/shard_map/ppermute | solution.py:293
  31.2 0.0 collective-permute-start.7
  31.2 0.7 collective-permute-start.6
  31.9 4.0 %collective-permute-start.9 = (f32[416,128]{1,0:T(8,128)S(1)}, f32[416,128]{1,0:T(8,128)S(1)}, u32[]{:S(2)}, u32[]{:S(2)}) collective-permute-start(f32[416,128]{1,0:T(8,128)S(1)} %bitcast.50), channel_id=1, source_target_pairs={{0,1},{1,0},{2,3},{3,2},{4,5},{5,4},{6,7},{7,6},{8,9},{9,8},{10,11... | collective-permute-start | bytes 638984 | tf_op jit(solution)/shard_map/ppermute | solution.py:293
  35.9 0.8 collective-permute-done.8.refs_3_
  36.7 0.0 copy-start.1
  36.7 4.5 %collective-permute-start.12 = (f32[416,128]{1,0:T(8,128)S(1)}, f32[416,128]{1,0:T(8,128)S(1)}, u32[]{:S(2)}, u32[]{:S(2)}) collective-permute-start(f32[416,128]{1,0:T(8,128)S(1)} %collective-permute-done.8.refs_3_), channel_id=1, source_target_pairs={{0,1},{1,0},{2,3},{3,2},{4,5},{5,4},{6,7},{7,6},{8,9},{9,8},{10,11... | collective-permute-start | bytes 638984 | tf_op jit(solution)/shard_map/ppermute | solution.py:293
  41.3 0.0 collective-permute-done.7.refs_2_
  41.3 0.0 copy-start.2
  41.3 1.6 %collective-permute-start.11 = (f32[416,128]{1,0:T(8,128)S(1)}, f32[416,128]{1,0:T(8,128)S(1)}, u32[]{:S(2)}, u32[]{:S(2)}) collective-permute-start(f32[416,128]{1,0:T(8,128)S(1)} %collective-permute-done.7.refs_2_), channel_id=1, source_target_pairs={{0,1},{1,0},{2,3},{3,2},{4,5},{5,4},{6,7},{7,6},{8,9},{9,8},{10,11... | collective-permute-start | bytes 638984 | tf_op jit(solution)/shard_map/ppermute | solution.py:293
  42.8 0.0 collective-permute-done.6.refs_1_
  42.8 0.0 copy-start.3
  42.8 1.8 %collective-permute-start.10 = (f32[416,128]{1,0:T(8,128)S(1)}, f32[416,128]{1,0:T(8,128)S(1)}, u32[]{:S(2)}, u32[]{:S(2)}) collective-permute-start(f32[416,128]{1,0:T(8,128)S(1)} %collective-permute-done.6.refs_1_), channel_id=1, source_target_pairs={{0,1},{1,0},{2,3},{3,2},{4,5},{5,4},{6,7},{7,6},{8,9},{9,8},{10,11... | collective-permute-start | bytes 638984 | tf_op jit(solution)/shard_map/ppermute | solution.py:293
  44.7 0.0 collective-permute-done.9.refs_4_
  44.7 0.0 copy-start.4
  44.7 0.0 collective-permute-done.12.refs_7_
  44.7 0.0 copy-start.5
  44.7 0.0 collective-permute-done.11.refs_6_
  44.7 0.0 copy-start.6
  44.7 1.1 collective-permute-done.10.refs_5_
  45.8 0.0 copy-start.7
  45.8 0.0 copy-done
  45.8 0.0 copy-done.1
  45.8 0.0 copy-done.2
  45.8 0.0 copy-done.3
  45.8 0.0 copy-done.4
  45.8 0.0 copy-done.5
  45.8 0.0 copy-done.6
  45.8 0.6 copy-done.7
  46.5 50.8 %shard_map.64 = f32[4096,128]{1,0:T(8,128)} custom-call(s32[1]{0:T(128)} %bitcast.first_ref, f32[8]{0:T(128)} %taps_ref.1, f32[416,128]{1,0:T(8,128)} %bitcast.51, f32[416,128]{1,0:T(8,128)} %copy-done.3, f32[416,128]{1,0:T(8,128)} %copy-done.2, f32[416,128]{1,0:T(8,128)} %copy-done.1, f32[416,128]{1,0:T(8,128)} %copy-done.4, f32[416,128]{1,0:T(8,128)} %copy-done.7, ...), custom_call_target="tpu_custom_call" | custom-call | tf_op jit(solution)/shard_map/pallas_call | solution.py:272
  97.3 32.1 %all_to_all.9 = f32[8,512,128]{2,1,0:T(8,128)S(1)} all-to-all(f32[8,512,128]{2,1,0:T(8,128)} %bitcast.44), channel_id=1, replica_groups=mesh['plane_0'=2,'plane_1'=4,'tile_0'=2,'tile_1'=4,'tile_2'=2] {'plane_0..., dimensions={0} | all-to-all | bytes 4194304 | tf_op jit(solution)/shard_map/all_to_all | solution.py:321
  129.4 0.1 bitcast_reduce_fusion
  129.5 0.8 pad_maximum_fusion
  (9 shorter events, 0.1 us)
Async XLA Ops:
  1.9 0.7 copy-start.8
  2.0 1.4 %copy-start.9 = (f32[2,2048]{1,0:T(2,128)S(1)}, f32[2,2048]{1,0:T(2,128)}, u32[]{:S(2)}) copy-start(f32[2,2048]{1,0:T(2,128)} %param.6) | copy-start | bytes 49156
  11.3 5.2 %collective-permute-start.2 = (f32[96,32]{0,1:T(8,128)S(1)}, f32[96,32]{0,1:T(8,128)S(1)}, u32[]{:S(2)}, u32[]{:S(2)}) collective-permute-start(f32[96,32]{0,1:T(8,128)S(1)} %get-tuple-element.10), channel_id=1, source_target_pairs={{0,48},{16,0},{32,16},{48,32},{1,49},{17,1},{33,17},{49,33},{2,50}... | collective-permute-start | bytes 36872 | tf_op jit(solution)/shard_map/ppermute | solution.py:293
  14.7 4.1 %collective-permute-start.1 = (f32[96,32]{0,1:T(8,128)S(1)}, f32[96,32]{0,1:T(8,128)S(1)}, u32[]{:S(2)}, u32[]{:S(2)}) collective-permute-start(f32[96,32]{0,1:T(8,128)S(1)} %get-tuple-element.11), channel_id=1, source_target_pairs={{0,32},{16,48},{32,0},{48,16},{1,33},{17,49},{33,1},{49,17},{2,34}... | collective-permute-start | bytes 36872 | tf_op jit(solution)/shard_map/ppermute | solution.py:293
  15.2 3.8 %collective-permute-start = (f32[96,32]{0,1:T(8,128)S(1)}, f32[96,32]{0,1:T(8,128)S(1)}, u32[]{:S(2)}, u32[]{:S(2)}) collective-permute-start(f32[96,32]{0,1:T(8,128)S(1)} %get-tuple-element.12), channel_id=1, source_target_pairs={{0,16},{16,32},{32,48},{48,0},{1,17},{17,33},{33,49},{49,1},{2,18}... | collective-permute-start | bytes 36872 | tf_op jit(solution)/shard_map/ppermute | solution.py:293
  19.2 5.7 %collective-permute-start.4 = (f32[104,128]{0,1:T(8,128)S(1)}, f32[104,128]{0,1:T(8,128)S(1)}, u32[]{:S(2)}, u32[]{:S(2)}) collective-permute-start(f32[104,128]{0,1:T(8,128)S(1)} %get-tuple-element.8), channel_id=1, source_target_pairs={{0,4},{2,6},{4,0},{6,2},{1,5},{3,7},{5,1},{7,3},{8,12},{10,14},{12... | collective-permute-start | bytes 159752 | tf_op jit(solution)/shard_map/ppermute | solution.py:293
  22.2 5.0 %collective-permute-start.3 = (f32[104,128]{0,1:T(8,128)S(1)}, f32[104,128]{0,1:T(8,128)S(1)}, u32[]{:S(2)}, u32[]{:S(2)}) collective-permute-start(f32[104,128]{0,1:T(8,128)S(1)} %get-tuple-element.8), channel_id=1, source_target_pairs={{0,2},{2,4},{4,6},{6,0},{1,3},{3,5},{5,7},{7,1},{8,10},{10,12},{12... | collective-permute-start | bytes 159752 | tf_op jit(solution)/shard_map/ppermute | solution.py:293
  22.6 4.6 %collective-permute-start.5 = (f32[104,128]{0,1:T(8,128)S(1)}, f32[104,128]{0,1:T(8,128)S(1)}, u32[]{:S(2)}, u32[]{:S(2)}) collective-permute-start(f32[104,128]{0,1:T(8,128)S(1)} %get-tuple-element.8), channel_id=1, source_target_pairs={{0,6},{2,0},{4,2},{6,4},{1,7},{3,1},{5,3},{7,5},{8,14},{10,8},{12,... | collective-permute-start | bytes 159752 | tf_op jit(solution)/shard_map/ppermute | solution.py:293
  27.4 18.4 %copy-start = (f32[104,4,128]{2,1,0:T(4,128)}, f32[104,4,128]{2,1,0:T(4,128)S(1)}, u32[]{:S(2)}) copy-start(f32[104,4,128]{2,1,0:T(4,128)S(1)} %copy.23) | copy-start | bytes 638980
  27.4 9.3 %collective-permute-start.8 = (f32[416,128]{1,0:T(8,128)S(1)}, f32[416,128]{1,0:T(8,128)S(1)}, u32[]{:S(2)}, u32[]{:S(2)}) collective-permute-start(f32[416,128]{1,0:T(8,128)S(1)} %bitcast.47), channel_id=1, source_target_pairs={{0,72},{8,0},{64,8},{72,64},{1,73},{9,1},{65,9},{73,65},{2,74},{10... | collective-permute-start | bytes 638984 | tf_op jit(solution)/shard_map/ppermute | solution.py:293
  31.2 10.0 %collective-permute-start.7 = (f32[416,128]{1,0:T(8,128)S(1)}, f32[416,128]{1,0:T(8,128)S(1)}, u32[]{:S(2)}, u32[]{:S(2)}) collective-permute-start(f32[416,128]{1,0:T(8,128)S(1)} %bitcast.48), channel_id=1, source_target_pairs={{0,64},{8,72},{64,0},{72,8},{1,65},{9,73},{65,1},{73,9},{2,66},{10... | collective-permute-start | bytes 638984 | tf_op jit(solution)/shard_map/ppermute | solution.py:293
  31.2 11.6 %collective-permute-start.6 = (f32[416,128]{1,0:T(8,128)S(1)}, f32[416,128]{1,0:T(8,128)S(1)}, u32[]{:S(2)}, u32[]{:S(2)}) collective-permute-start(f32[416,128]{1,0:T(8,128)S(1)} %bitcast.49), channel_id=1, source_target_pairs={{0,8},{8,64},{64,72},{72,0},{1,9},{9,65},{65,73},{73,1},{2,10},{10... | collective-permute-start | bytes 638984 | tf_op jit(solution)/shard_map/ppermute | solution.py:293
  31.9 12.7 %collective-permute-start.9 = (f32[416,128]{1,0:T(8,128)S(1)}, f32[416,128]{1,0:T(8,128)S(1)}, u32[]{:S(2)}, u32[]{:S(2)}) collective-permute-start(f32[416,128]{1,0:T(8,128)S(1)} %bitcast.50), channel_id=1, source_target_pairs={{0,1},{1,0},{2,3},{3,2},{4,5},{5,4},{6,7},{7,6},{8,9},{9,8},{10,11... | collective-permute-start | bytes 638984 | tf_op jit(solution)/shard_map/ppermute | solution.py:293
  36.7 9.0 %copy-start.1 = (f32[416,128]{1,0:T(8,128)}, f32[416,128]{1,0:T(8,128)S(1)}, u32[]{:S(2)}) copy-start(f32[416,128]{1,0:T(8,128)S(1)} %collective-permute-done.8.refs_3_) | copy-start | bytes 638980
  36.7 8.0 %collective-permute-start.12 = (f32[416,128]{1,0:T(8,128)S(1)}, f32[416,128]{1,0:T(8,128)S(1)}, u32[]{:S(2)}, u32[]{:S(2)}) collective-permute-start(f32[416,128]{1,0:T(8,128)S(1)} %collective-permute-done.8.refs_3_), channel_id=1, source_target_pairs={{0,1},{1,0},{2,3},{3,2},{4,5},{5,4},{6,7},{7,6},{8,9},{9,8},{10,11... | collective-permute-start | bytes 638984 | tf_op jit(solution)/shard_map/ppermute | solution.py:293
  41.3 4.5 %copy-start.2 = (f32[416,128]{1,0:T(8,128)}, f32[416,128]{1,0:T(8,128)S(1)}, u32[]{:S(2)}) copy-start(f32[416,128]{1,0:T(8,128)S(1)} %collective-permute-done.7.refs_2_) | copy-start | bytes 638980
  41.3 3.4 %collective-permute-start.11 = (f32[416,128]{1,0:T(8,128)S(1)}, f32[416,128]{1,0:T(8,128)S(1)}, u32[]{:S(2)}, u32[]{:S(2)}) collective-permute-start(f32[416,128]{1,0:T(8,128)S(1)} %collective-permute-done.7.refs_2_), channel_id=1, source_target_pairs={{0,1},{1,0},{2,3},{3,2},{4,5},{5,4},{6,7},{7,6},{8,9},{9,8},{10,11... | collective-permute-start | bytes 638984 | tf_op jit(solution)/shard_map/ppermute | solution.py:293
  42.8 3.0 %copy-start.3 = (f32[416,128]{1,0:T(8,128)}, f32[416,128]{1,0:T(8,128)S(1)}, u32[]{:S(2)}) copy-start(f32[416,128]{1,0:T(8,128)S(1)} %collective-permute-done.6.refs_1_) | copy-start | bytes 638980
  42.8 2.9 %collective-permute-start.10 = (f32[416,128]{1,0:T(8,128)S(1)}, f32[416,128]{1,0:T(8,128)S(1)}, u32[]{:S(2)}, u32[]{:S(2)}) collective-permute-start(f32[416,128]{1,0:T(8,128)S(1)} %collective-permute-done.6.refs_1_), channel_id=1, source_target_pairs={{0,1},{1,0},{2,3},{3,2},{4,5},{5,4},{6,7},{7,6},{8,9},{9,8},{10,11... | collective-permute-start | bytes 638984 | tf_op jit(solution)/shard_map/ppermute | solution.py:293
  44.7 1.1 copy-start.4
  44.7 1.1 copy-start.5
  44.7 1.1 copy-start.6
  45.8 0.7 copy-start.7

commit v3 on v2

--- a/solution.py
+++ b/solution.py
@@ -18,8 +18,8 @@
 PAIR = 2
 COLS = 128
 SETS = PAIR * BANDS
-UNROLL = 32
 SKIP = 33
+DFTS = 4
 ROWS = 3 * 32 + 8
 GROUPS = 32
 
@@ -27,6 +27,10 @@
        41.227609837804344, -12.302204294679466)
 COS = (0.9999996601928737, -19.739032170917408, 64.93001305163173, -85.28516993938109,
        58.84794870978477, -21.158227293307913)
+
+
+SIN4 = (6.283080178478066, -41.332270740282254, 81.3803723363611, -74.5450983459368, 32.89453310276785)
+COS4 = (0.9999814280910587, -19.732589155128917, 64.69856260154607, -82.54685792407774, 45.912495330496334)
 
 
 def horner(u, coefs):
@@ -41,6 +45,11 @@
     return horner(u, COS), turn * horner(u, SIN)
 
 
+def cis4(turn):
+    u = turn * turn
+    return horner(u, COS4), turn * horner(u, SIN4)
+
+
 def cis_int(k):
     return cis((((k + 2048) & 4095) - 2048).astype(jnp.float32) * (1.0 / 4096))
 
@@ -54,16 +63,20 @@
 
 
 def add(a, b):
+    if b is None:
+        return a
     return a[0] + b[0], a[1] + b[1]
 
 
 def sub(a, b):
+    if b is None:
+        return a
     return a[0] - b[0], a[1] - b[1]
 
 
 def turned(a, k, n):
     k = k % n
-    if k == 0:
+    if a is None or k == 0:
         return a
     if 4 * k == n:
         return -a[1], a[0]
@@ -95,17 +108,76 @@
     return np.concatenate([hi, lo, hi], axis=1)
 
 
-def kernel(
-    first_ref, taps_ref, *refs
-):
+def bucket_kernel(here_ref, dest_ref, off_ref, vis_ref, *out_refs):
+    dest = dest_ref[...]
+    plane, band = dest >> 4, dest & 15
+    spot = (((plane - here_ref[0]) & 3) * 2 + (plane >> 2)) * BANDS + band
+    low, high = (spot & 15).astype(jnp.float32), (spot >> 4).astype(jnp.float32)
+    off = off_ref[...]
+    pieces = []
+    for v in range(2):
+        x = vis_ref[v]
+        top = x.astype(jnp.bfloat16).astype(jnp.float32)
+        pieces += [top, x - top]
+    pieces += [(off >> 12).astype(jnp.float32), ((off >> 4) & 255).astype(jnp.float32), (off & 15).astype(jnp.float32)]
+    sub16 = lax.broadcasted_iota(jnp.int32, (16, 128), 0).astype(jnp.float32).astype(jnp.bfloat16)
+    yes, no = jnp.ones((16, 128), jnp.bfloat16), jnp.zeros((16, 128), jnp.bfloat16)
+    first = lax.broadcasted_iota(jnp.int32, (256, 256), 0) <= lax.broadcasted_iota(jnp.int32, (256, 256), 1)
+    upto = jnp.where(first, 1.0, 0.0).astype(jnp.bfloat16)
+    upto = jnp.concatenate([upto, jnp.ones((256, 256), jnp.bfloat16)])
+
+    def spread(x, i):
+        return jnp.broadcast_to(x[i : i + 1], (16, 128)).astype(jnp.bfloat16)
+
+    ones = []
+    for i in range(16):
+        code = jnp.where(spread(low, i) == sub16, spread(high, i), -yes)
+        ones.append([jnp.where(code == jnp.bfloat16(k), yes, no) for k in range(8)])
+    slots = lax.broadcasted_iota(jnp.int32, (32, 256), 0).astype(jnp.float32)
+    before = jnp.zeros((128, 256), jnp.bfloat16)
+    ranked = []
+    for i in range(8):
+        one = jnp.concatenate([jnp.concatenate(ones[2 * i]), jnp.concatenate(ones[2 * i + 1])], axis=1)
+        count = jnp.dot(jnp.concatenate([one, before], axis=1), upto, preferred_element_type=jnp.float32)
+        before = before + one
+        rank = jnp.sum(count * one.astype(jnp.float32), axis=0, keepdims=True) - 1.0
+        ranked.append(jnp.where(slots == rank, 1.0, 0.0).astype(jnp.bfloat16))
+    ranked = jnp.concatenate(ranked, axis=1)
+    held = []
+    for x in pieces:
+        held.append(
+            jnp.concatenate([jnp.concatenate([o * spread(x, i) for o in ones[i]]) for i in range(16)], axis=1)
+        )
+    r = lax.dot_general(
+        jnp.concatenate(held), ranked, (((1,), (1,)), ((), ())), preferred_element_type=jnp.float32
+    )
+    r = [r[128 * k : 128 * k + 128] for k in range(7)]
+    both = (r[0] + r[1], r[2] + r[3], r[4] * 4096.0 + r[5] * 16.0 + r[6])
+    for x in range(4):
+        for v in range(3):
+            out_refs[x][SETS * v : SETS * v + SETS, :] = both[v][SETS * x : SETS * x + SETS]
+
+
+def buckets(here, dest, off, vis, interpret=False):
+    smem = pl.BlockSpec(memory_space=pltpu.SMEM)
+    vmem = pl.BlockSpec(memory_space=pltpu.VMEM)
+    return pl.pallas_call(
+        bucket_kernel,
+        out_shape=[jax.ShapeDtypeStruct((3 * SETS, CAP), jnp.float32)] * 4,
+        in_specs=[smem, vmem, vmem, vmem],
+        out_specs=[vmem] * 4,
+        interpret=interpret,
+    )(here, dest, off, vis)
+
+
+def first_kernel(first_ref, taps_ref, *refs):
     vis_refs, refs = refs[:8], refs[8:]
-    dft_ref, out_ref, p0_ref, p1_ref, q0_ref, q1_ref, acc_ref, h_ref, y_ref = refs
+    dft_ref, out_ref, p0_ref, p1_ref, q0_ref, q1_ref, h_ref, y_ref = refs
+    first = first_ref[0]
 
     def values(v, s):
         rows = pl.ds(pl.multiple_of(4 * (v * SETS + s), 4), 4)
         return jnp.concatenate([ref[rows, :] for ref in vis_refs])
-
-    first = first_ref[0]
 
     def tables(s, p_ref, q_ref):
         off = values(2, s).astype(jnp.int32)
@@ -151,31 +223,15 @@
         return jnp.concatenate(o), jnp.concatenate(products)
 
     def phase(used, later, s):
-        def chunk(k, c):
-            parts = [made(k * UNROLL + j, *used) for j in range(UNROLL)]
-            o = jnp.concatenate([x[0] for x in parts], axis=1)
-            e = jnp.concatenate([x[1] for x in parts], axis=1)
-            part = lax.dot_general(o, e, (((1,), (1,)), ((), ())), preferred_element_type=jnp.float32)
-            if UNROLL == GROUPS:
-                put(part)
-            else:
-                acc_ref[...] += part
-            return c
-
+        tables(jnp.minimum(s + 1, SETS - 1), *later)
+        parts = [made(g, *used) for g in range(GROUPS)]
+        o = jnp.concatenate([x[0] for x in parts], axis=1)
+        e = jnp.concatenate([x[1] for x in parts], axis=1)
+        part = lax.dot_general(o, e, (((1,), (1,)), ((), ())), preferred_element_type=jnp.float32)
         plane = s // BANDS
         at = pl.ds(pl.multiple_of((s % BANDS) * 16, 16), 16)
-
-        def put(part):
-            for k in range(16):
-                h_ref[plane * 16 + k, at, :] = part[16 * k : 16 * k + 16, :]
-
-        tables(jnp.minimum(s + 1, SETS - 1), *later)
-        if UNROLL == GROUPS:
-            chunk(0, 0)
-        else:
-            acc_ref[...] = jnp.zeros((256, 256), jnp.float32)
-            lax.fori_loop(0, GROUPS // UNROLL, chunk, 0)
-            put(acc_ref[...])
+        for k in range(16):
+            h_ref[plane * 16 + k, at, :] = part[16 * k : 16 * k + 16, :]
 
     buf0, buf1 = (p0_ref, q0_ref), (p1_ref, q1_ref)
     tables(0, *buf0)
@@ -187,11 +243,16 @@
 
     lax.fori_loop(0, SETS // 2, two_sets, 0)
 
+    w_row = sum(ref[pl.ds(4 * 3 * SETS, 1), :] for ref in vis_refs[:4]) * 0.5
+    rows_of_image(first, taps_ref, w_row, dft_ref, h_ref, out_ref, y_ref)
+
+
+def rows_of_image(first, taps_ref, w_row, dft_ref, h_ref, out_ref, y_ref):
     sign = jnp.where(lax.broadcasted_iota(jnp.int32, (256, 128), 1) < 64, -1.0, 1.0)
 
     def dft_step(i, carry):
-        for j in range(2):
-            k = 2 * i + j
+        for j in range(DFTS):
+            k = DFTS * i + j
             re, im = h_ref[k, :, 0:128], h_ref[k, :, 128:256]
             re = re + sign * pltpu.roll(re, 64, 1)
             im = im - sign * pltpu.roll(im, 64, 1)
@@ -204,7 +265,7 @@
             y_ref[k, :, 128:256] = r[:256, 128:] + r[256:, :128]
         return carry
 
-    lax.fori_loop(0, PAIR * 8, dft_step, 0)
+    lax.fori_loop(0, PAIR * 16 // DFTS, dft_step, 0)
 
     place = lax.broadcasted_iota(jnp.int32, (8, 128), 1)
     lower = place & 63
@@ -220,12 +281,9 @@
         b = mul(b, step)
         b = (b[0] + weight[k], b[1])
 
-    def cosine(index):
-        return (((index + 2048) & 4095) - 2048).astype(jnp.float32) * (0.5 / G)
-
-    y2 = cosine(lane)
-    y2 = y2 * y2
-    w_row = sum(ref[pl.ds(4 * 3 * SETS, 1), :] for ref in vis_refs[:4]) * 0.5
+    scale = 0.5 / G
+    y = (((lane + 2048) & 4095) - 2048).astype(jnp.float32) * scale
+    rest = 1.0 - y * y
     w = [jnp.broadcast_to(w_row[:, q : q + 1], (8, 128)) for q in range(PAIR)]
 
     def tile_step(t, carry):
@@ -234,6 +292,7 @@
         tw = [None, cis_int(line)]
         for k in range(2, 16):
             tw.append(mul(tw[k // 2], tw[k - k // 2]))
+        x0 = line.astype(jnp.float32) * scale
         sums = None
         for q in range(PAIR):
             xs = []
@@ -243,35 +302,33 @@
             f = fft(xs)
             new = []
             for j in range(16):
-                x2 = cosine(line + 256 * j)
-                s = x2 * x2 + y2
-                n = -s / (1.0 + jnp.sqrt(1.0 - s))
-                turn = w[q] * n
+                x = x0 + (256 * j if j < 8 else 256 * j - G) * scale
+                z = rest - x * x
+                turn = w[q] * (z * lax.rsqrt(z)) - w[q]
                 turn = turn - jnp.round(turn)
-                term = mul(f[j], cis(turn))
+                term = mul(f[j], cis4(turn))
                 new.append(term if sums is None else add(sums[j], term))
             sums = new
         zero = jnp.zeros((8, 128), jnp.float32)
         ts = [(jnp.full((8, 128), taps_ref[0]), zero)]
         ts += [(tw[k][0] * taps_ref[k], tw[k][1] * taps_ref[k]) for k in range(1, 8)]
-        ts += [(zero, zero)] * 8
+        ts += [None] * 8
         a = fft(ts)
         for j in range(16):
             ab = mul(a[j], b)
             pixel = sums[j][0] * ab[0] - sums[j][1] * ab[1]
-            rows = pl.ds(pl.multiple_of(t * 8 + 256 * j, 8), 8)
-            out_ref[rows, :] = jnp.take_along_axis(pixel, source, axis=1)
+            out_ref[j, at, :] = jnp.take_along_axis(pixel, source, axis=1)
         return carry
 
-    lax.fori_loop(0, 32, tile_step, 0)
+    lax.fori_loop(0, 256 // 8, tile_step, 0)
 
 
 def part_image(first, taps, *vis, interpret=False):
     smem = pl.BlockSpec(memory_space=pltpu.SMEM)
     vmem = pl.BlockSpec(memory_space=pltpu.VMEM)
     return pl.pallas_call(
-        kernel,
-        out_shape=jax.ShapeDtypeStruct((G, COLS), jnp.float32),
+        first_kernel,
+        out_shape=jax.ShapeDtypeStruct((16, 256, COLS), jnp.float32),
         in_specs=[smem, smem] + [vmem] * 9,
         out_specs=vmem,
         scratch_shapes=[
@@ -279,7 +336,6 @@
             pltpu.VMEM((18 * GROUPS, 128), jnp.float32),
             pltpu.VMEM((16 * SKIP, 128), jnp.float32),
             pltpu.VMEM((16 * SKIP, 128), jnp.float32),
-            pltpu.VMEM((256, 256), jnp.float32),
             pltpu.VMEM((PAIR * 16, 256, 256), jnp.float32),
             pltpu.VMEM((PAIR * 16, 256, 256), jnp.float32),
         ],
@@ -294,20 +350,9 @@
 
 
 def local(visibility, target, offset, taps, w_plane):
-    dest = target[:, 0]
-    onehot = (dest[:, None] == jnp.arange(128, dtype=jnp.int32)[None, :]).astype(jnp.int32)
-    rank = jnp.sum(jnp.cumsum(onehot, axis=0) * onehot, axis=1) - 1
-    plane, band = dest // BANDS, dest % BANDS
-    bucket = ((plane % 4) * 2 + plane // 4) * BANDS + band
-    slot = bucket * CAP + rank
-    payload = jnp.stack([visibility[0], visibility[1], offset.astype(jnp.float32)])
-    outgoing = jnp.zeros((3, 128 * CAP), jnp.float32).at[:, slot].set(payload)
-    outgoing = outgoing.reshape(3, 4, SETS, CAP).transpose(1, 0, 2, 3).reshape(4, 3 * SETS, CAP)
-    here = lax.axis_index("plane_1")
-    mine = []
-    for by in range(4):
-        block = lax.dynamic_index_in_dim(outgoing, (here + by) % 4, 0, keepdims=False)
-        mine.append(block if by == 0 else shifted(block, "plane_1", by))
+    here = lax.axis_index("plane_1").reshape(1).astype(jnp.int32)
+    blocks = buckets(here, target.reshape(16, 128), offset.reshape(16, 128), visibility.reshape(2, 16, 128))
+    mine = [blocks[0]] + [shifted(blocks[by], "plane_1", by) for by in (1, 2, 3)]
     mine = jnp.concatenate(mine, axis=1)
     half = lax.axis_index("plane_0")
     w_row = jnp.where(jnp.arange(128) == half, w_plane[0], 0.0)
@@ -317,7 +362,8 @@
     area = [line] + [shifted(line, ("plane_0", "tile_0"), by) for by in (1, 2, 3)]
     area = area + [shifted(x, "tile_2", 1) for x in area]
     first = lax.axis_index(TILE) * 256 + half * COLS
-    part = part_image(first.reshape(1).astype(jnp.int32), taps, *area)
+    first = first.reshape(1).astype(jnp.int32)
+    part = part_image(first, taps, *area).reshape(G, COLS)
     arrived = lax.all_to_all(part, PLANE, split_axis=0, concat_axis=0, tiled=True)
     total = arrived.reshape(2, 4, 512, COLS).sum(axis=1)
     return jnp.concatenate([total[0], total[1]], axis=1)

time: 131 us -> 120 us (0.916)
  local copies, waits for them, and re-layouts: 10.2 us -> 2.06 us
  Pallas kernels: 50.8 us -> 49.4 us
    scatter x1 -> x0, local copies, waits for them, and re-layouts: 6.1 us -> none  [local(): outgoing = jnp.zeros((3, 128 * CAP), jnp.float32).at[:, slot].set(payload)]
    pallas_call x1 -> x2, Pallas kernels: 50.8 us -> 49.4 us  [the longest x1 46.6 us: part_image(): pl.pallas_call(first_kernel, out_shape=jax.ShapeDtypeStruct((16, 256, COL...]
    reshape x2 -> x0, local copies, waits for them, and re-layouts: 1.39 us -> none  [local(): outgoing.reshape(3, 4, SETS, CAP).transpose(1, 0, 2, 3)]
  transfers between devices with their start and end apart: 13 -> 13, of which waited for: 5 -> 7; matrix products, arithmetic and copies ran while one was open for 0% -> 0% of each run, Pallas kernels for 0% -> 0%
where the time goes in v3:
time: 120 us
  Pallas kernels  49.4 us (41%)
  blocking collectives  32.1 us (27%)
  starting transfers between devices  26.3 us (22%)
  waiting for transfers between devices  7.2 us (6%)
  local copies, waits for them, and re-layouts  2.06 us (2%)
  other arithmetic  1.84 us (2%)
    pallas_call x1, Pallas kernels, part_image(): pl.pallas_call(first_kernel, out_shape=jax.ShapeDtypeStruct((16, 256, COL...  46.6 us
    all_to_all x1, blocking collectives, local(): lax.all_to_all(part, PLANE, split_axis=0, concat_axis=0, tiled=True)  32.1 us
    ppermute x13, starting transfers between devices, shifted(): lax.ppermute(x, axis, [(i, (i + by) % length) for i in range(length)])  26.3 us
    ppermute x13, waiting for transfers between devices, shifted(): lax.ppermute(x, axis, [(i, (i + by) % length) for i in range(length)])  7.2 us
    pallas_call x1, Pallas kernels, buckets(): pl.pallas_call(bucket_kernel, out_shape=[jax.ShapeDtypeStruct((3 * SETS,...  2.85 us
  transfers between devices with their start and end apart: 13, of which 7 were waited for; matrix products, arithmetic and copies ran while one was open for 0% of the time, Pallas kernels for 0%

profile of v3, /device:TPU:1, one launch (start us, length us, event | category | flops | bytes accessed | tf_op | source)
XLA Modules:
  0.0 119.7 jit_solution(5325000295721469651)
XLA Ops:
  0.0 1.3 %copy.10 = f32[1,2,16,128]{3,2,1,0:T(8,128)} copy(f32[1,2,16,128]{3,1,2,0:T(2,128)} %bitcast.33) | data formatting | bytes 32768
  1.3 2.8 %shard_map.64 = (f32[96,32]{1,0:T(8,128)}, f32[96,32]{1,0:T(8,128)}, f32[96,32]{1,0:T(8,128)}, f32[96,32]{1,0:T(8,128)}) custom-call(s32[1]{0:T(128)} %bitcast.1.here_ref, s32[16,128]{1,0:T(8,128)} %bitcast.34, s32[16,128]{1,0:T(8,128)} %bitcast.35, f32[2,16,128]{2,1,0:T(8,128)} %bitcast.29), custom_call_target="tpu_custom_call" | custom-call | tf_op jit(solution)/shard_map/pallas_call | solution.py:164
  4.2 2.0 %collective-permute-start = (f32[96,32]{1,0:T(8,128)}, f32[96,32]{1,0:T(8,128)S(1)}, u32[]{:S(2)}, u32[]{:S(2)}) collective-permute-start(f32[96,32]{1,0:T(8,128)} %get-tuple-element.10), channel_id=1, source_target_pairs={{0,16},{16,32},{32,48},{48,0},{1,17},{17,33},{33,49},{49,1},{2,18}... | collective-permute-start | bytes 36872 | tf_op jit(solution)/shard_map/ppermute | solution.py:349
  6.2 2.5 %collective-permute-start.1 = (f32[96,32]{1,0:T(8,128)}, f32[96,32]{1,0:T(8,128)S(1)}, u32[]{:S(2)}, u32[]{:S(2)}) collective-permute-start(f32[96,32]{1,0:T(8,128)} %get-tuple-element.11), channel_id=1, source_target_pairs={{0,32},{16,48},{32,0},{48,16},{1,33},{17,49},{33,1},{49,17},{2,34}... | collective-permute-start | bytes 36872 | tf_op jit(solution)/shard_map/ppermute | solution.py:349
  8.6 1.2 collective-permute-start.2
  10.5 0.0 collective-permute-done
  10.5 0.4 collective-permute-done.1
  10.9 1.2 collective-permute-done.2
  12.1 0.9 pad_maximum_fusion.2
  13.0 2.9 %collective-permute-start.5 = (f32[104,128]{1,0:T(8,128)S(1)}, f32[104,128]{1,0:T(8,128)S(1)}, u32[]{:S(2)}, u32[]{:S(2)}) collective-permute-start(f32[104,128]{1,0:T(8,128)S(1)} %pad_maximum_fusion.2), channel_id=1, source_target_pairs={{0,6},{2,0},{4,2},{6,4},{1,7},{3,1},{5,3},{7,5},{8,14},{10,8},{12,... | collective-permute-start | bytes 159752 | tf_op jit(solution)/shard_map/ppermute | solution.py:349
  15.9 0.3 collective-permute-start.4
  16.2 0.7 collective-permute-start.3
  16.9 0.2 collective-permute-done.5
  17.1 3.3 %collective-permute-done.4 = f32[104,128]{1,0:T(8,128)S(1)} collective-permute-done((f32[104,128]{1,0:T(8,128)S(1)}, f32[104,128]{1,0:T(8,128)S(1)}, u32[]{:S(2)}, u32[]{:S(2)}) %collective-permute-start.4) | collective-permute-done | bytes 53280 | tf_op jit(solution)/shard_map/ppermute | solution.py:349
  20.4 0.5 collective-permute-done.3
  21.0 0.1 copy.7
  21.0 0.0 copy-start
  21.0 3.8 %collective-permute-start.8 = (f32[416,128]{1,0:T(8,128)S(1)}, f32[416,128]{1,0:T(8,128)S(1)}, u32[]{:S(2)}, u32[]{:S(2)}) collective-permute-start(f32[416,128]{1,0:T(8,128)S(1)} %bitcast.23), channel_id=1, source_target_pairs={{0,72},{8,0},{64,8},{72,64},{1,73},{9,1},{65,9},{73,65},{2,74},{10... | collective-permute-start | bytes 638984 | tf_op jit(solution)/shard_map/ppermute | solution.py:349
  24.9 0.0 collective-permute-start.7
  24.9 0.7 collective-permute-start.6
  25.6 4.3 %collective-permute-start.9 = (f32[416,128]{1,0:T(8,128)S(1)}, f32[416,128]{1,0:T(8,128)S(1)}, u32[]{:S(2)}, u32[]{:S(2)}) collective-permute-start(f32[416,128]{1,0:T(8,128)S(1)} %bitcast.26), channel_id=1, source_target_pairs={{0,1},{1,0},{2,3},{3,2},{4,5},{5,4},{6,7},{7,6},{8,9},{9,8},{10,11... | collective-permute-start | bytes 638984 | tf_op jit(solution)/shard_map/ppermute | solution.py:349
  29.8 0.5 collective-permute-done.8.refs_3_
  30.3 0.0 copy-start.1
  30.3 4.5 %collective-permute-start.12 = (f32[416,128]{1,0:T(8,128)S(1)}, f32[416,128]{1,0:T(8,128)S(1)}, u32[]{:S(2)}, u32[]{:S(2)}) collective-permute-start(f32[416,128]{1,0:T(8,128)S(1)} %collective-permute-done.8.refs_3_), channel_id=1, source_target_pairs={{0,1},{1,0},{2,3},{3,2},{4,5},{5,4},{6,7},{7,6},{8,9},{9,8},{10,11... | collective-permute-start | bytes 638984 | tf_op jit(solution)/shard_map/ppermute | solution.py:349
  34.9 0.0 collective-permute-done.7.refs_2_
  34.9 0.0 copy-start.2
  34.9 1.6 %collective-permute-start.11 = (f32[416,128]{1,0:T(8,128)S(1)}, f32[416,128]{1,0:T(8,128)S(1)}, u32[]{:S(2)}, u32[]{:S(2)}) collective-permute-start(f32[416,128]{1,0:T(8,128)S(1)} %collective-permute-done.7.refs_2_), channel_id=1, source_target_pairs={{0,1},{1,0},{2,3},{3,2},{4,5},{5,4},{6,7},{7,6},{8,9},{9,8},{10,11... | collective-permute-start | bytes 638984 | tf_op jit(solution)/shard_map/ppermute | solution.py:349
  36.5 0.0 collective-permute-done.6.refs_1_
  36.5 0.0 copy-start.3
  36.5 1.8 %collective-permute-start.10 = (f32[416,128]{1,0:T(8,128)S(1)}, f32[416,128]{1,0:T(8,128)S(1)}, u32[]{:S(2)}, u32[]{:S(2)}) collective-permute-start(f32[416,128]{1,0:T(8,128)S(1)} %collective-permute-done.6.refs_1_), channel_id=1, source_target_pairs={{0,1},{1,0},{2,3},{3,2},{4,5},{5,4},{6,7},{7,6},{8,9},{9,8},{10,11... | collective-permute-start | bytes 638984 | tf_op jit(solution)/shard_map/ppermute | solution.py:349
  38.3 0.0 collective-permute-done.9.refs_4_
  38.3 0.0 copy-start.4
  38.3 0.0 collective-permute-done.12.refs_7_
  38.3 0.0 copy-start.5
  38.3 0.0 collective-permute-done.11.refs_6_
  38.3 0.0 copy-start.6
  38.3 1.1 collective-permute-done.10.refs_5_
  39.4 0.0 copy-start.7
  39.4 0.0 copy-done
  39.4 0.0 copy-done.1
  39.4 0.0 copy-done.2
  39.4 0.0 copy-done.3
  39.4 0.0 copy-done.4
  39.4 0.0 copy-done.5
  39.4 0.0 copy-done.6
  39.4 0.6 copy-done.7
  40.1 46.6 %shard_map.65 = f32[16,256,128]{2,1,0:T(8,128)} custom-call(s32[1]{0:T(128)} %bitcast.first_ref, f32[8]{0:T(128)} %taps_ref.1, f32[416,128]{1,0:T(8,128)} %bitcast.27, f32[416,128]{1,0:T(8,128)} %copy-done.3, f32[416,128]{1,0:T(8,128)} %copy-done.2, f32[416,128]{1,0:T(8,128)} %copy-done.1, f32[416,128]{1,0:T(8,128)} %copy-done.4, f32[416,128]{1,0:T(8,128)} %copy-done.7, ...), custom_call_target="tpu_custom_call" | custom-call | tf_op jit(solution)/shard_map/pallas_call | solution.py:329
  86.6 32.1 %all_to_all.9 = f32[8,512,128]{2,1,0:T(8,128)S(1)} all-to-all(f32[8,512,128]{2,1,0:T(8,128)} %bitcast.22), channel_id=1, replica_groups=mesh['plane_0'=2,'plane_1'=4,'tile_0'=2,'tile_1'=4,'tile_2'=2] {'plane_0..., dimensions={0} | all-to-all | bytes 4194304 | tf_op jit(solution)/shard_map/all_to_all | solution.py:367
  118.7 0.1 bitcast_reduce_fusion
  118.9 0.8 pad_maximum_fusion
  (4 shorter events, 0.1 us)
Async XLA Ops:
  4.2 6.3 %collective-permute-start = (f32[96,32]{1,0:T(8,128)}, f32[96,32]{1,0:T(8,128)S(1)}, u32[]{:S(2)}, u32[]{:S(2)}) collective-permute-start(f32[96,32]{1,0:T(8,128)} %get-tuple-element.10), channel_id=1, source_target_pairs={{0,16},{16,32},{32,48},{48,0},{1,17},{17,33},{33,49},{49,1},{2,18}... | collective-permute-start | bytes 36872 | tf_op jit(solution)/shard_map/ppermute | solution.py:349
  6.2 4.7 %collective-permute-start.1 = (f32[96,32]{1,0:T(8,128)}, f32[96,32]{1,0:T(8,128)S(1)}, u32[]{:S(2)}, u32[]{:S(2)}) collective-permute-start(f32[96,32]{1,0:T(8,128)} %get-tuple-element.11), channel_id=1, source_target_pairs={{0,32},{16,48},{32,0},{48,16},{1,33},{17,49},{33,1},{49,17},{2,34}... | collective-permute-start | bytes 36872 | tf_op jit(solution)/shard_map/ppermute | solution.py:349
  8.6 3.4 %collective-permute-start.2 = (f32[96,32]{1,0:T(8,128)}, f32[96,32]{1,0:T(8,128)S(1)}, u32[]{:S(2)}, u32[]{:S(2)}) collective-permute-start(f32[96,32]{1,0:T(8,128)} %get-tuple-element.12), channel_id=1, source_target_pairs={{0,48},{16,0},{32,16},{48,32},{1,49},{17,1},{33,17},{49,33},{2,50}... | collective-permute-start | bytes 36872 | tf_op jit(solution)/shard_map/ppermute | solution.py:349
  13.0 4.1 %collective-permute-start.5 = (f32[104,128]{1,0:T(8,128)S(1)}, f32[104,128]{1,0:T(8,128)S(1)}, u32[]{:S(2)}, u32[]{:S(2)}) collective-permute-start(f32[104,128]{1,0:T(8,128)S(1)} %pad_maximum_fusion.2), channel_id=1, source_target_pairs={{0,6},{2,0},{4,2},{6,4},{1,7},{3,1},{5,3},{7,5},{8,14},{10,8},{12,... | collective-permute-start | bytes 159752 | tf_op jit(solution)/shard_map/ppermute | solution.py:349
  15.9 4.5 %collective-permute-start.4 = (f32[104,128]{1,0:T(8,128)S(1)}, f32[104,128]{1,0:T(8,128)S(1)}, u32[]{:S(2)}, u32[]{:S(2)}) collective-permute-start(f32[104,128]{1,0:T(8,128)S(1)} %pad_maximum_fusion.2), channel_id=1, source_target_pairs={{0,4},{2,6},{4,0},{6,2},{1,5},{3,7},{5,1},{7,3},{8,12},{10,14},{12... | collective-permute-start | bytes 159752 | tf_op jit(solution)/shard_map/ppermute | solution.py:349
  16.2 4.7 %collective-permute-start.3 = (f32[104,128]{1,0:T(8,128)S(1)}, f32[104,128]{1,0:T(8,128)S(1)}, u32[]{:S(2)}, u32[]{:S(2)}) collective-permute-start(f32[104,128]{1,0:T(8,128)S(1)} %pad_maximum_fusion.2), channel_id=1, source_target_pairs={{0,2},{2,4},{4,6},{6,0},{1,3},{3,5},{5,7},{7,1},{8,10},{10,12},{12... | collective-permute-start | bytes 159752 | tf_op jit(solution)/shard_map/ppermute | solution.py:349
  21.0 18.4 %copy-start = (f32[104,4,128]{2,1,0:T(4,128)}, f32[104,4,128]{2,1,0:T(4,128)S(1)}, u32[]{:S(2)}) copy-start(f32[104,4,128]{2,1,0:T(4,128)S(1)} %copy.7) | copy-start | bytes 638980
  21.0 9.3 %collective-permute-start.8 = (f32[416,128]{1,0:T(8,128)S(1)}, f32[416,128]{1,0:T(8,128)S(1)}, u32[]{:S(2)}, u32[]{:S(2)}) collective-permute-start(f32[416,128]{1,0:T(8,128)S(1)} %bitcast.23), channel_id=1, source_target_pairs={{0,72},{8,0},{64,8},{72,64},{1,73},{9,1},{65,9},{73,65},{2,74},{10... | collective-permute-start | bytes 638984 | tf_op jit(solution)/shard_map/ppermute | solution.py:349
  24.9 10.0 %collective-permute-start.7 = (f32[416,128]{1,0:T(8,128)S(1)}, f32[416,128]{1,0:T(8,128)S(1)}, u32[]{:S(2)}, u32[]{:S(2)}) collective-permute-start(f32[416,128]{1,0:T(8,128)S(1)} %bitcast.24), channel_id=1, source_target_pairs={{0,64},{8,72},{64,0},{72,8},{1,65},{9,73},{65,1},{73,9},{2,66},{10... | collective-permute-start | bytes 638984 | tf_op jit(solution)/shard_map/ppermute | solution.py:349
  24.9 11.6 %collective-permute-start.6 = (f32[416,128]{1,0:T(8,128)S(1)}, f32[416,128]{1,0:T(8,128)S(1)}, u32[]{:S(2)}, u32[]{:S(2)}) collective-permute-start(f32[416,128]{1,0:T(8,128)S(1)} %bitcast.25), channel_id=1, source_target_pairs={{0,8},{8,64},{64,72},{72,0},{1,9},{9,65},{65,73},{73,1},{2,10},{10... | collective-permute-start | bytes 638984 | tf_op jit(solution)/shard_map/ppermute | solution.py:349
  25.6 12.7 %collective-permute-start.9 = (f32[416,128]{1,0:T(8,128)S(1)}, f32[416,128]{1,0:T(8,128)S(1)}, u32[]{:S(2)}, u32[]{:S(2)}) collective-permute-start(f32[416,128]{1,0:T(8,128)S(1)} %bitcast.26), channel_id=1, source_target_pairs={{0,1},{1,0},{2,3},{3,2},{4,5},{5,4},{6,7},{7,6},{8,9},{9,8},{10,11... | collective-permute-start | bytes 638984 | tf_op jit(solution)/shard_map/ppermute | solution.py:349
  30.3 9.1 %copy-start.1 = (f32[416,128]{1,0:T(8,128)}, f32[416,128]{1,0:T(8,128)S(1)}, u32[]{:S(2)}) copy-start(f32[416,128]{1,0:T(8,128)S(1)} %collective-permute-done.8.refs_3_) | copy-start | bytes 638980
  30.3 8.0 %collective-permute-start.12 = (f32[416,128]{1,0:T(8,128)S(1)}, f32[416,128]{1,0:T(8,128)S(1)}, u32[]{:S(2)}, u32[]{:S(2)}) collective-permute-start(f32[416,128]{1,0:T(8,128)S(1)} %collective-permute-done.8.refs_3_), channel_id=1, source_target_pairs={{0,1},{1,0},{2,3},{3,2},{4,5},{5,4},{6,7},{7,6},{8,9},{9,8},{10,11... | collective-permute-start | bytes 638984 | tf_op jit(solution)/shard_map/ppermute | solution.py:349
  34.9 4.5 %copy-start.2 = (f32[416,128]{1,0:T(8,128)}, f32[416,128]{1,0:T(8,128)S(1)}, u32[]{:S(2)}) copy-start(f32[416,128]{1,0:T(8,128)S(1)} %collective-permute-done.7.refs_2_) | copy-start | bytes 638980
  34.9 3.4 %collective-permute-start.11 = (f32[416,128]{1,0:T(8,128)S(1)}, f32[416,128]{1,0:T(8,128)S(1)}, u32[]{:S(2)}, u32[]{:S(2)}) collective-permute-start(f32[416,128]{1,0:T(8,128)S(1)} %collective-permute-done.7.refs_2_), channel_id=1, source_target_pairs={{0,1},{1,0},{2,3},{3,2},{4,5},{5,4},{6,7},{7,6},{8,9},{9,8},{10,11... | collective-permute-start | bytes 638984 | tf_op jit(solution)/shard_map/ppermute | solution.py:349
  36.5 3.0 %copy-start.3 = (f32[416,128]{1,0:T(8,128)}, f32[416,128]{1,0:T(8,128)S(1)}, u32[]{:S(2)}) copy-start(f32[416,128]{1,0:T(8,128)S(1)} %collective-permute-done.6.refs_1_) | copy-start | bytes 638980
  36.5 2.9 %collective-permute-start.10 = (f32[416,128]{1,0:T(8,128)S(1)}, f32[416,128]{1,0:T(8,128)S(1)}, u32[]{:S(2)}, u32[]{:S(2)}) collective-permute-start(f32[416,128]{1,0:T(8,128)S(1)} %collective-permute-done.6.refs_1_), channel_id=1, source_target_pairs={{0,1},{1,0},{2,3},{3,2},{4,5},{5,4},{6,7},{7,6},{8,9},{9,8},{10,11... | collective-permute-start | bytes 638984 | tf_op jit(solution)/shard_map/ppermute | solution.py:349
  38.3 1.1 copy-start.4
  38.3 1.1 copy-start.5
  38.3 1.1 copy-start.6
  39.4 0.7 copy-start.7

commit v4 on v3

v4 whole, which is shorter than its diff:
```python
import math

import jax
import jax.numpy as jnp
import numpy as np
from jax import lax
from jax.experimental import pallas as pl
from jax.experimental.pallas import tpu as pltpu
from jax.sharding import Mesh
from jax.sharding import PartitionSpec as P

G = 4096
TILE = ("tile_0", "tile_1", "tile_2")
PLANE = ("plane_0", "plane_1")
PLANE_TILE = PLANE + TILE
BANDS = 16
CAP = 32
PAIR = 2
COLS = 128
SETS = PAIR * BANDS
SKIP = 33
STEPS = 2
GROUPS = 32

SIN = (6.283183359351797, -41.341456456971535, 81.59688036372165, -76.58598132852413,
       41.227609837804344, -12.302204294679466)
COS = (0.9999996601928737, -19.739032170917408, 64.93001305163173, -85.28516993938109,
       58.84794870978477, -21.158227293307913)


SIN4 = (6.283080178478066, -41.332270740282254, 81.3803723363611, -74.5450983459368, 32.89453310276785)
COS4 = (0.9999814280910587, -19.732589155128917, 64.69856260154607, -82.54685792407774, 45.912495330496334)


def horner(u, coefs):
    total = jnp.full_like(u, coefs[-1])
    for c in coefs[-2::-1]:
        total = total * u + c
    return total


def cis(turn):
    u = turn * turn
    return horner(u, COS), turn * horner(u, SIN)


def cis4(turn):
    u = turn * turn
    return horner(u, COS4), turn * horner(u, SIN4)


def cis_int(k):
    return cis((((k + 2048) & 4095) - 2048).astype(jnp.float32) * (1.0 / 4096))


def cis_half(k):
    return cis((((k + 4096) & 8191) - 4096).astype(jnp.float32) * (1.0 / 8192))


def mul(a, b):
    return a[0] * b[0] - a[1] * b[1], a[0] * b[1] + a[1] * b[0]


def add(a, b):
    if b is None:
        return a
    return a[0] + b[0], a[1] + b[1]


def sub(a, b):
    if b is None:
        return a
    return a[0] - b[0], a[1] - b[1]


def turned(a, k, n):
    k = k % n
    if a is None or k == 0:
        return a
    if 4 * k == n:
        return -a[1], a[0]
    if 8 * k == n:
        h = math.sqrt(0.5)
        return (a[0] - a[1]) * h, (a[0] + a[1]) * h
    if 8 * k == 3 * n:
        h = math.sqrt(0.5)
        return (-a[0] - a[1]) * h, (a[0] - a[1]) * h
    c, s = math.cos(2 * math.pi * k / n), math.sin(2 * math.pi * k / n)
    return a[0] * c - a[1] * s, a[0] * s + a[1] * c


def fft(xs):
    n = len(xs)
    if n == 1:
        return xs
    even, odd = fft(xs[0::2]), fft(xs[1::2])
    odd = [turned(o, k, n) for k, o in enumerate(odd)]
    return [add(e, o) for e, o in zip(even, odd)] + [sub(e, o) for e, o in zip(even, odd)]


def bucket_kernel(dest_ref, off_ref, vis_ref, out_ref):
    dest = jnp.concatenate([dest_ref[0:1, 128 * i : 128 * i + 128] for i in range(16)])
    plane, band = dest >> 4, dest & 15
    spot = ((plane & 3) * 2 + (plane >> 2)) * BANDS + band
    low, high = (spot & 15).astype(jnp.float32), (spot >> 4).astype(jnp.float32)
    off = off_ref[...]
    pieces = []
    for v in range(2):
        x = jnp.concatenate([vis_ref[v : v + 1, 128 * i : 128 * i + 128] for i in range(16)])
        top = x.astype(jnp.bfloat16).astype(jnp.float32)
        pieces += [top, x - top]
    pieces += [(off >> 12).astype(jnp.float32), ((off >> 4) & 255).astype(jnp.float32), (off & 15).astype(jnp.float32)]
    sub16 = lax.broadcasted_iota(jnp.int32, (16, 128), 0).astype(jnp.float32).astype(jnp.bfloat16)
    yes, no = jnp.ones((16, 128), jnp.bfloat16), jnp.zeros((16, 128), jnp.bfloat16)
    first = lax.broadcasted_iota(jnp.int32, (256, 256), 0) <= lax.broadcasted_iota(jnp.int32, (256, 256), 1)
    upto = jnp.where(first, 1.0, 0.0).astype(jnp.bfloat16)
    upto = jnp.concatenate([upto, jnp.ones((256, 256), jnp.bfloat16)])

    def spread(x, i):
        return jnp.broadcast_to(x[i : i + 1], (16, 128)).astype(jnp.bfloat16)

    ones = []
    for i in range(16):
        code = jnp.where(spread(low, i) == sub16, spread(high, i), -yes)
        ones.append([jnp.where(code == jnp.bfloat16(k), yes, no) for k in range(8)])
    quarter = ((spot & 3) * CAP).astype(jnp.float32)
    places = lax.broadcasted_iota(jnp.int32, (128, 256), 0).astype(jnp.float32)
    before = jnp.zeros((128, 256), jnp.bfloat16)
    placed = []
    for i in range(8):
        one = jnp.concatenate([jnp.concatenate(ones[2 * i]), jnp.concatenate(ones[2 * i + 1])], axis=1)
        count = jnp.dot(jnp.concatenate([one, before], axis=1), upto, preferred_element_type=jnp.float32)
        before = before + one
        rank = jnp.sum(count * one.astype(jnp.float32), axis=0, keepdims=True) - 1.0
        rank = rank + jnp.concatenate([quarter[2 * i : 2 * i + 1], quarter[2 * i + 1 : 2 * i + 2]], axis=1)
        placed.append(jnp.where(places == rank, 1.0, 0.0).astype(jnp.bfloat16))
    placed = jnp.concatenate(placed, axis=1)
    fours = (spot >> 2).astype(jnp.float32)
    rows = [[jnp.where(spread(fours, i) == sub16 + jnp.bfloat16(16 * k), yes, no) for k in range(2)] for i in range(16)]
    held = []
    for x in pieces:
        held.append(jnp.concatenate([jnp.concatenate([o * spread(x, i) for o in rows[i]]) for i in range(16)], axis=1))
    r = lax.dot_general(
        jnp.concatenate(held), placed, (((1,), (1,)), ((), ())), preferred_element_type=jnp.float32
    )
    r = [r[32 * k : 32 * k + 32] for k in range(7)]
    both = (r[0] + r[1], r[2] + r[3], r[4] * 4096.0 + r[5] * 16.0 + r[6])
    for i in range(16):
        x = i // 4
        for v in range(3):
            out_ref[i, 8 * v : 8 * v + 8, :] = both[v][8 * x : 8 * x + 8]


def buckets(dest, off, vis, interpret=False):
    vmem = pl.BlockSpec(memory_space=pltpu.VMEM)
    return pl.pallas_call(
        bucket_kernel,
        out_shape=jax.ShapeDtypeStruct((16, 24, 128), jnp.float32),
        in_specs=[vmem, vmem, vmem],
        out_specs=vmem,
        interpret=interpret,
    )(dest, off, vis)


def image_kernel(first_ref, *refs):
    own_refs, other_refs, refs = refs[:4], refs[4:8], refs[8:]
    out_ref, p0_ref, p1_ref, q0_ref, q1_ref, h0_ref, h1_ref, y0_ref, y1_ref, sum_ref, dft_ref, vis_ref = refs
    first = first_ref[0]
    segment = lax.broadcasted_iota(jnp.int32, (16, 128), 1) >> 5
    odd, upper = (segment & 1) == 1, segment >= 2

    def swapped(a, b, mask, by):
        return jnp.where(mask, pltpu.roll(b, by, 1), a), jnp.where(mask, b, pltpu.roll(a, 128 - by, 1))

    def regroup(step, c):
        for i in [step * 6 + k for k in range(6)]:
            for half, area in enumerate((own_refs, other_refs)):
                x = [ref[pl.ds(i, 16, stride=24), :] for ref in area]
                x[0], x[1] = swapped(x[0], x[1], odd, 32)
                x[2], x[3] = swapped(x[2], x[3], odd, 32)
                x[0], x[2] = swapped(x[0], x[2], upper, 64)
                x[1], x[3] = swapped(x[1], x[3], upper, 64)
                for j in range(4):
                    vis_ref[pl.ds(pl.multiple_of((4 * i + j) * GROUPS + 16 * half, 16), 16), :] = x[j]
        return c

    lax.fori_loop(0, 4, regroup, 0)

    def values(v, s):
        return vis_ref[pl.ds(pl.multiple_of((v * SETS + s) * GROUPS, GROUPS), GROUPS), :]

    def make_dft(i):
        k = 2 * (lax.broadcasted_iota(jnp.int32, (16, 256), 0) + 16 * i) + 1
        k = k * lax.broadcasted_iota(jnp.int32, (16, 256), 1) * 16
        for j, x in enumerate(cis_half(k)):
            rows = pl.ds(pl.multiple_of(128 * j + 16 * i, 16), 16)
            hi = x.astype(jnp.bfloat16)
            dft_ref[rows, 0:256] = hi
            dft_ref[rows, 256:512] = (x - hi.astype(jnp.float32)).astype(jnp.bfloat16)
            dft_ref[rows, 512:768] = hi

    def tables(s, p_ref, q_ref):
        off = values(2, s).astype(jnp.int32)
        col = off & (G - 1)
        row = off >> 12
        p_ref[pl.ds(16 * GROUPS, GROUPS), :] = (row & 15).astype(jnp.float32)
        p_ref[pl.ds(17 * GROUPS, GROUPS), :] = (row >> 4).astype(jnp.float32)
        half = cis_half(col)
        one = mul(half, half)
        base = mul((values(0, s), values(1, s)), cis_half(col * (2 * first + 15) - 16 * (row >> 4) - 256 * (s % BANDS)))
        power = half
        for k in range(8):
            q_ref[pl.ds(k * SKIP, GROUPS), :] = power[0]
            q_ref[pl.ds((8 + k) * SKIP, GROUPS), :] = power[1]
            if k < 7:
                power = mul(power, one)
        step = one
        for k in range(4):
            step = mul(step, step)
        for k in range(8):
            p_ref[pl.ds(k * GROUPS, GROUPS), :] = base[0]
            p_ref[pl.ds((8 + k) * GROUPS, GROUPS), :] = base[1]
            if k < 7:
                base = mul(base, step)

    sub16 = lax.broadcasted_iota(jnp.int32, (16, 128), 0).astype(jnp.float32).astype(jnp.bfloat16)
    yes = jnp.ones((16, 128), jnp.bfloat16)
    no = jnp.zeros((16, 128), jnp.bfloat16)

    def made(g, p_ref, q_ref):
        def spread(row):
            return jnp.broadcast_to(p_ref[pl.ds(row * GROUPS + g, 1), :], (16, 128)).astype(jnp.bfloat16)

        high = jnp.where(spread(17) == sub16, spread(16), -yes)
        o = [jnp.where(high == jnp.bfloat16(k), yes, no) for k in range(16)]
        qr = q_ref[pl.ds(g, 8, stride=SKIP), :]
        qi = q_ref[pl.ds(8 * SKIP + g, 8, stride=SKIP), :]
        products = []
        for part, q in ((0, qr), (8, qi), (0, qi), (8, qr)):
            for k in range(0, 8, 2):
                two = [p_ref[pl.ds((part + k + j) * GROUPS + g, 1), :] * q for j in range(2)]
                products.append(jnp.concatenate(two).astype(jnp.bfloat16))
        return jnp.concatenate(o), jnp.concatenate(products)

    def phase(used, later, s, h_ref):
        tables(jnp.minimum(s + 1, SETS - 1), *later)
        parts = [made(g, *used) for g in range(GROUPS)]
        o = jnp.concatenate([x[0] for x in parts], axis=1)
        e = jnp.concatenate([x[1] for x in parts], axis=1)
        part = lax.dot_general(o, e, (((1,), (1,)), ((), ())), preferred_element_type=jnp.float32)
        at = pl.ds(pl.multiple_of((s % BANDS) * 16, 16), 16)
        for k in range(16):
            h_ref[k, at, :] = part[16 * k : 16 * k + 16, :]

    sign = jnp.where(lax.broadcasted_iota(jnp.int32, (256, 128), 1) < 64, -1.0, 1.0)

    def dft(k, h_ref, y_ref):
        re, im = h_ref[k, :, 0:128], h_ref[k, :, 128:256]
        re = re + sign * pltpu.roll(re, 64, 1)
        im = im - sign * pltpu.roll(im, 64, 1)
        x = jnp.concatenate([re, im], axis=1)
        hi = x.astype(jnp.bfloat16)
        lo = (x - hi.astype(jnp.float32)).astype(jnp.bfloat16)
        both = jnp.concatenate([hi, hi, lo], axis=0)
        r = jnp.dot(dft_ref[...], both, preferred_element_type=jnp.float32)
        c_re, c_im, s_re, s_im = r[:128, :128], r[:128, 128:], r[128:, :128], r[128:, 128:]
        y_ref[k, 0:128, 0:128] = c_re - s_im
        y_ref[k, 0:128, 128:256] = c_im + s_re
        y_ref[k, 128:256, 0:128] = c_re + s_im
        y_ref[k, 128:256, 128:256] = c_im - s_re

    place = lax.broadcasted_iota(jnp.int32, (8, 128), 1)
    lower = place & 63
    lane = 2 * (lower - (lower & 7)) + jnp.where(place < 64, 8 + (lower & 7), 7 - (lower & 7))
    inner = place & 15
    source = ((place - inner) >> 1) + jnp.where(inner < 8, 71 - inner, inner - 8)
    lane = lane + first
    sub_row = lax.broadcasted_iota(jnp.int32, (8, 128), 0)
    scale = 0.5 / G
    y = (((lane + 2048) & 4095) - 2048).astype(jnp.float32) * scale
    rest = 1.0 - y * y
    def spread8(row, k):
        return jnp.broadcast_to(row[:, k : k + 1], (8, 128))

    w_row = sum(ref[384:385, :] for ref in own_refs) * 0.5
    taps_row = own_refs[0][385:386, :]

    def twiddles(line):
        tw = [None, cis_int(line)]
        for k in range(2, 16):
            tw.append(mul(tw[k // 2], tw[k - k // 2]))
        return tw

    def half_tile(t, half):
        line = sub_row + t * 8
        return pl.ds(pl.multiple_of(t * 8 + 128 * half, 8), 8), 255 - line if half else line

    def terms(at, line, tw, w, y_ref):
        xs = []
        for k in range(16):
            x = (y_ref[k, at, 0:128], y_ref[k, at, 128:256])
            xs.append(x if k == 0 else mul(x, tw[k]))
        f = fft(xs)
        x0 = line.astype(jnp.float32) * scale
        result = []
        for j in range(16):
            x = x0 + (256 * j if j < 8 else 256 * j - G) * scale
            z = rest - x * x
            turn = w * (z * lax.rsqrt(z)) - w
            turn = turn - jnp.round(turn)
            result.append(mul(f[j], cis4(turn)))
        return result

    buf0, buf1 = (p0_ref, q0_ref), (p1_ref, q1_ref)
    tables(0, *buf0)

    def sets_of_first(i, c):
        phase(buf0, buf1, 2 * i, h0_ref)
        phase(buf1, buf0, 2 * i + 1, h0_ref)
        make_dft(i)
        return c

    lax.fori_loop(0, BANDS // 2, sets_of_first, 0)

    def sets_of_second(i, c):
        phase(buf0, buf1, BANDS + 2 * i, h1_ref)
        dft(2 * i, h0_ref, y0_ref)
        phase(buf1, buf0, BANDS + 2 * i + 1, h1_ref)
        dft(2 * i + 1, h0_ref, y0_ref)
        return c

    lax.fori_loop(0, BANDS // 2, sets_of_second, 0)
    w0 = spread8(w_row, 0)

    def tiles_of_first(i, c):
        for k in range(STEPS):
            dft(STEPS * i + k, h1_ref, y1_ref)
        for k in range(STEPS):
            for half in range(2):
                at, line = half_tile(STEPS * i + k, half)
                for j, x in enumerate(terms(at, line, twiddles(line), w0, y0_ref)):
                    sum_ref[j, at, 0:128] = x[0]
                    sum_ref[j, at, 128:256] = x[1]
        return c

    lax.fori_loop(0, 16 // STEPS, tiles_of_first, 0)
    w1 = spread8(w_row, 1)
    taps = [spread8(taps_row, k) for k in range(8)]
    step = cis_int(lane)
    weight = [x.astype(jnp.bfloat16).astype(jnp.float32) * (1.0 / 512) for x in taps]
    b = (weight[7], jnp.zeros((8, 128), jnp.float32))
    for k in range(6, -1, -1):
        b = mul(b, step)
        b = (b[0] + weight[k], b[1])

    def tiles_of_second(t, c):
        for half in range(2):
            at, line = half_tile(t, half)
            tw = twiddles(line)
            ts = [(taps[0], jnp.zeros((8, 128), jnp.float32))]
            ts += [(tw[k][0] * taps[k], tw[k][1] * taps[k]) for k in range(1, 8)]
            a = fft(ts + [None] * 8)
            place = pl.ds(pl.multiple_of(248 - t * 8 if half else t * 8, 8), 8)
            for j, x in enumerate(terms(at, line, tw, w1, y1_ref)):
                x = add(x, (sum_ref[j, at, 0:128], sum_ref[j, at, 128:256]))
                ab = mul(a[j], b)
                pixel = jnp.take_along_axis(x[0] * ab[0] - x[1] * ab[1], source, axis=1)
                if half:
                    pixel = jnp.take_along_axis(pixel, 7 - sub_row, axis=0)
                out_ref[j, place, :] = pixel
        return c

    lax.fori_loop(0, 16, tiles_of_second, 0)


def part_image(first, *area, interpret=False):
    smem = pl.BlockSpec(memory_space=pltpu.SMEM)
    vmem = pl.BlockSpec(memory_space=pltpu.VMEM)
    return pl.pallas_call(
        image_kernel,
        out_shape=jax.ShapeDtypeStruct((16, 256, COLS), jnp.float32),
        in_specs=[smem] + [vmem] * 8,
        out_specs=vmem,
        scratch_shapes=[
            pltpu.VMEM((18 * GROUPS, 128), jnp.float32),
            pltpu.VMEM((18 * GROUPS, 128), jnp.float32),
            pltpu.VMEM((16 * SKIP, 128), jnp.float32),
            pltpu.VMEM((16 * SKIP, 128), jnp.float32),
            pltpu.VMEM((16, 256, 256), jnp.float32),
            pltpu.VMEM((16, 256, 256), jnp.float32),
            pltpu.VMEM((16, 256, 256), jnp.float32),
            pltpu.VMEM((16, 256, 256), jnp.float32),
            pltpu.VMEM((16, 256, 256), jnp.float32),
            pltpu.VMEM((256, 768), jnp.bfloat16),
            pltpu.VMEM((3 * SETS * GROUPS, 128), jnp.float32),
        ],
        compiler_params=pltpu.CompilerParams(vmem_limit_bytes=56 * 1024 * 1024),
        interpret=interpret,
    )(first, *area)


def shifted(x, axis, by):
    length = lax.axis_size(axis)
    return lax.ppermute(x, axis, [(i, (i + by) % length) for i in range(length)])


def local(visibility, target, offset, taps, w_plane):
    half = lax.axis_index("plane_0")
    out = buckets(target.reshape(1, 2048), offset.reshape(16, 128), visibility)
    own = lax.all_to_all(out, ("plane_1", "tile_1"), split_axis=0, concat_axis=0, tiled=True).reshape(384, 128)
    w_row = jnp.where(jnp.arange(128) == half, w_plane[0], 0.0)
    own = jnp.concatenate([own, w_row[None], jnp.pad(taps, (0, 120))[None], jnp.zeros((6, 128), jnp.float32)])
    area = [own] + [shifted(own, ("plane_0", "tile_0"), by) for by in (1, 2, 3)]
    area = area + [shifted(x, "tile_2", 1) for x in area]
    first = lax.axis_index(TILE) * 256 + half * COLS
    first = first.reshape(1).astype(jnp.int32)
    part = part_image(first, *area).reshape(G, COLS)
    arrived = lax.all_to_all(part, PLANE, split_axis=0, concat_axis=0, tiled=True)
    total = arrived.reshape(2, 4, 512, COLS).sum(axis=1)
    return jnp.concatenate([total[0], total[1]], axis=1)


def solution(mesh):
    finer = Mesh(
        mesh.devices.reshape(2, 4, 2, 4, 2), ("plane_0", "plane_1", "tile_0", "tile_1", "tile_2")
    )
    return jax.shard_map(
        local,
        mesh=finer,
        in_specs=(P(None, PLANE_TILE), P(PLANE_TILE, None), P(PLANE_TILE), P(), P(PLANE)),
        out_specs=P(PLANE, TILE),
        check_vma=False,
    )
```

time: 120 us -> 114 us (0.950)
  starting transfers between devices: 26.3 us -> 19.4 us
  waiting for transfers between devices: 7.2 us -> 11.7 us
  Pallas kernels: 49.4 us -> 46.9 us
    ppermute x13 -> x7, starting transfers between devices: 26.3 us -> 11.9 us  [shifted(): lax.ppermute(x, axis, [(i, (i + by) % length) for i in range(length)])]
    all_to_all x0 -> x1, starting transfers between devices: none -> 7.56 us  [local(): lax.all_to_all(out, ('plane_1', 'tile_1'), split_axis=0, concat_axis=0, t...]
    all_to_all x0 -> x1, waiting for transfers between devices: none -> 5.73 us  [local(): lax.all_to_all(out, ('plane_1', 'tile_1'), split_axis=0, concat_axis=0, t...]
    pallas_call x2, Pallas kernels: 49.4 us -> 46.9 us  [the longest x1 44.7 us: part_image(): pl.pallas_call(image_kernel, out_shape=jax.ShapeDtypeStruct((16, 256, COL...]
    unnamed x17 -> x16, local copies, waits for them, and re-layouts: 1.97 us -> 0.66 us
    ppermute x13 -> x7, waiting for transfers between devices: 7.2 us -> 5.95 us  [shifted(): lax.ppermute(x, axis, [(i, (i + by) % length) for i in range(length)])]
  transfers between devices with their start and end apart: 13 -> 8, of which waited for: 7 -> 4; matrix products, arithmetic and copies ran while one was open for 0% -> 1% of each run, Pallas kernels for 0% -> 0%
where the time goes in v4:
time: 114 us; the launch traced here: 113 us
  Pallas kernels  46.9 us (41%)
  blocking collectives  32.1 us (28%)
  starting transfers between devices  19.4 us (17%)
  waiting for transfers between devices  11.7 us (10%)
  local copies, waits for them, and re-layouts  1.43 us (1%)
    pallas_call x1, Pallas kernels, part_image(): pl.pallas_call(image_kernel, out_shape=jax.ShapeDtypeStruct((16, 256, COL...  44.7 us
    all_to_all x1, blocking collectives, local(): lax.all_to_all(part, PLANE, split_axis=0, concat_axis=0, tiled=True)  32.1 us
    ppermute x7, starting transfers between devices, shifted(): lax.ppermute(x, axis, [(i, (i + by) % length) for i in range(length)])  11.9 us
    all_to_all x1, starting transfers between devices, local(): lax.all_to_all(out, ('plane_1', 'tile_1'), split_axis=0, concat_axis=0, t...  7.56 us
    ppermute x7, waiting for transfers between devices, shifted(): lax.ppermute(x, axis, [(i, (i + by) % length) for i in range(length)])  5.95 us
    all_to_all x1, waiting for transfers between devices, local(): lax.all_to_all(out, ('plane_1', 'tile_1'), split_axis=0, concat_axis=0, t...  5.73 us
  transfers between devices with their start and end apart: 8, of which 4 were waited for; matrix products, arithmetic and copies ran while one was open for 1% of the time, Pallas kernels for 0%

profile of v4, /device:TPU:1, one launch (start us, length us, event | category | flops | bytes accessed | tf_op | source)
XLA Modules:
  0.0 113.4 jit_solution(827286314780493435)
XLA Ops:
  0.0 2.2 %shard_map.55 = f32[16,24,128]{2,1,0:T(8,128)} custom-call(s32[1,2048]{1,0:T(1,128)} %bitcast.17, s32[16,128]{1,0:T(8,128)} %bitcast.18, f32[2,2048]{1,0:T(2,128)} %vis_ref.1), custom_call_target="tpu_custom_call" | custom-call | tf_op jit(solution)/shard_map/pallas_call | solution.py:156
  2.2 7.6 %all-to-all-start = ((f32[16,24,128]{2,1,0:T(8,128)}), f32[16,24,128]{2,1,0:T(8,128)S(1)}, u32[]{:S(2)}, u32[]{:S(2)}) async-start(f32[16,24,128]{2,1,0:T(8,128)} %shard_map.55), calls=%async_computation | async-start | bytes 393216 | tf_op jit(solution)/shard_map/all_to_all | solution.py:410
  10.5 0.1 pad.10.clone
  10.5 0.7 pad_bitcast_fusion
  11.2 5.7 %all-to-all-done = f32[16,24,128]{2,1,0:T(8,128)S(1)} async-done(((f32[16,24,128]{2,1,0:T(8,128)}), f32[16,24,128]{2,1,0:T(8,128)S(1)}, u32[]{:S(2)}, u32[]{:S(2)}) %all-to-all-start) | async-done | bytes 196640 | tf_op jit(solution)/shard_map/all_to_all | solution.py:410
  16.9 0.1 maximum_maximum_fusion.refs_0_
  17.1 0.0 copy-start
  17.1 3.9 %collective-permute-start.2 = (f32[392,128]{1,0:T(8,128)S(1)}, f32[392,128]{1,0:T(8,128)S(1)}, u32[]{:S(2)}, u32[]{:S(2)}) collective-permute-start(f32[392,128]{1,0:T(8,128)S(1)} %maximum_maximum_fusion.refs_0_), channel_id=1, source_target_pairs={{0,72},{8,0},{64,8},{72,64},{1,73},{9,1},{65,9},{73,65},{2,74},{10... | collective-permute-start | bytes 602120 | tf_op jit(solution)/shard_map/ppermute | solution.py:404
  20.9 0.0 collective-permute-start.1
  20.9 0.7 collective-permute-start
  21.6 2.8 %collective-permute-start.3 = (f32[392,128]{1,0:T(8,128)S(1)}, f32[392,128]{1,0:T(8,128)S(1)}, u32[]{:S(2)}, u32[]{:S(2)}) collective-permute-start(f32[392,128]{1,0:T(8,128)S(1)} %maximum_maximum_fusion.refs_0_), channel_id=1, source_target_pairs={{0,1},{1,0},{2,3},{3,2},{4,5},{5,4},{6,7},{7,6},{8,9},{9,8},{10,11... | collective-permute-start | bytes 602120 | tf_op jit(solution)/shard_map/ppermute | solution.py:404
  24.4 4.0 %collective-permute-done.2.refs_3_ = f32[392,128]{1,0:T(8,128)S(1)} collective-permute-done((f32[392,128]{1,0:T(8,128)S(1)}, f32[392,128]{1,0:T(8,128)S(1)}, u32[]{:S(2)}, u32[]{:S(2)}) %collective-permute-start.2) | collective-permute-done | bytes 200736 | tf_op jit(solution)/shard_map/ppermute | solution.py:404
  28.5 0.0 copy-start.1
  28.5 2.0 %collective-permute-start.6 = (f32[392,128]{1,0:T(8,128)S(1)}, f32[392,128]{1,0:T(8,128)S(1)}, u32[]{:S(2)}, u32[]{:S(2)}) collective-permute-start(f32[392,128]{1,0:T(8,128)S(1)} %collective-permute-done.2.refs_3_), channel_id=1, source_target_pairs={{0,1},{1,0},{2,3},{3,2},{4,5},{5,4},{6,7},{7,6},{8,9},{9,8},{10,11... | collective-permute-start | bytes 602120 | tf_op jit(solution)/shard_map/ppermute | solution.py:404
  30.4 0.0 collective-permute-done.1.refs_2_
  30.4 0.0 copy-start.2
  30.4 1.6 %collective-permute-start.5 = (f32[392,128]{1,0:T(8,128)S(1)}, f32[392,128]{1,0:T(8,128)S(1)}, u32[]{:S(2)}, u32[]{:S(2)}) collective-permute-start(f32[392,128]{1,0:T(8,128)S(1)} %collective-permute-done.1.refs_2_), channel_id=1, source_target_pairs={{0,1},{1,0},{2,3},{3,2},{4,5},{5,4},{6,7},{7,6},{8,9},{9,8},{10,11... | collective-permute-start | bytes 602120 | tf_op jit(solution)/shard_map/ppermute | solution.py:404
  32.0 0.9 collective-permute-done.refs_1_
  32.9 0.0 copy-start.3
  32.9 1.0 collective-permute-start.4
  33.8 0.0 collective-permute-done.3.refs_4_
  33.8 0.0 copy-start.4
  33.8 0.0 collective-permute-done.6.refs_7_
  33.8 0.0 copy-start.5
  33.9 0.0 collective-permute-done.5.refs_6_
  33.9 0.0 copy-start.6
  33.9 1.0 collective-permute-done.4.refs_5_
  34.9 0.0 copy-start.7
  34.9 0.0 copy-done
  34.9 0.0 copy-done.1
  34.9 0.0 copy-done.2
  34.9 0.0 copy-done.3
  34.9 0.0 copy-done.4
  34.9 0.0 copy-done.5
  35.0 0.0 copy-done.6
  35.0 0.6 copy-done.7
  35.6 44.7 %shard_map.56 = f32[16,256,128]{2,1,0:T(8,128)} custom-call(s32[1]{0:T(128)} %bitcast.first_ref, f32[392,128]{1,0:T(8,128)} %copy-done, f32[392,128]{1,0:T(8,128)} %copy-done.3, f32[392,128]{1,0:T(8,128)} %copy-done.2, f32[392,128]{1,0:T(8,128)} %copy-done.1, f32[392,128]{1,0:T(8,128)} %copy-done.4, f32[392,128]{1,0:T(8,128)} %copy-done.7, ...), custom_call_target="tpu_custom_call" | custom-call | tf_op jit(solution)/shard_map/pallas_call | solution.py:379
  80.3 32.1 %all_to_all.14 = f32[8,512,128]{2,1,0:T(8,128)S(1)} all-to-all(f32[8,512,128]{2,1,0:T(8,128)} %bitcast.15), channel_id=1, replica_groups=mesh['plane_0'=2,'plane_1'=4,'tile_0'=2,'tile_1'=4,'tile_2'=2] {'plane_0..., dimensions={0} | all-to-all | bytes 4194304 | tf_op jit(solution)/shard_map/all_to_all | solution.py:418
  112.4 0.1 bitcast_reduce_fusion
  112.6 0.8 pad_maximum_fusion
  (3 shorter events, 0.0 us)
Async XLA Ops:
  2.2 14.7 %all-to-all-start = ((f32[16,24,128]{2,1,0:T(8,128)}), f32[16,24,128]{2,1,0:T(8,128)S(1)}, u32[]{:S(2)}, u32[]{:S(2)}) async-start(f32[16,24,128]{2,1,0:T(8,128)} %shard_map.55), calls=%async_computation | async-start | bytes 393216 | tf_op jit(solution)/shard_map/all_to_all | solution.py:410
  17.1 17.9 %copy-start = (f32[392,128]{1,0:T(8,128)}, f32[392,128]{1,0:T(8,128)S(1)}, u32[]{:S(2)}) copy-start(f32[392,128]{1,0:T(8,128)S(1)} %maximum_maximum_fusion.refs_0_) | copy-start | bytes 602116
  17.1 11.4 %collective-permute-start.2 = (f32[392,128]{1,0:T(8,128)S(1)}, f32[392,128]{1,0:T(8,128)S(1)}, u32[]{:S(2)}, u32[]{:S(2)}) collective-permute-start(f32[392,128]{1,0:T(8,128)S(1)} %maximum_maximum_fusion.refs_0_), channel_id=1, source_target_pairs={{0,72},{8,0},{64,8},{72,64},{1,73},{9,1},{65,9},{73,65},{2,74},{10... | collective-permute-start | bytes 602120 | tf_op jit(solution)/shard_map/ppermute | solution.py:404
  20.9 9.5 %collective-permute-start.1 = (f32[392,128]{1,0:T(8,128)S(1)}, f32[392,128]{1,0:T(8,128)S(1)}, u32[]{:S(2)}, u32[]{:S(2)}) collective-permute-start(f32[392,128]{1,0:T(8,128)S(1)} %maximum_maximum_fusion.refs_0_), channel_id=1, source_target_pairs={{0,64},{8,72},{64,0},{72,8},{1,65},{9,73},{65,1},{73,9},{2,66},{10... | collective-permute-start | bytes 602120 | tf_op jit(solution)/shard_map/ppermute | solution.py:404
  20.9 12.0 %collective-permute-start = (f32[392,128]{1,0:T(8,128)S(1)}, f32[392,128]{1,0:T(8,128)S(1)}, u32[]{:S(2)}, u32[]{:S(2)}) collective-permute-start(f32[392,128]{1,0:T(8,128)S(1)} %maximum_maximum_fusion.refs_0_), channel_id=1, source_target_pairs={{0,8},{8,64},{64,72},{72,0},{1,9},{9,65},{65,73},{73,1},{2,10},{10... | collective-permute-start | bytes 602120 | tf_op jit(solution)/shard_map/ppermute | solution.py:404
  21.6 12.2 %collective-permute-start.3 = (f32[392,128]{1,0:T(8,128)S(1)}, f32[392,128]{1,0:T(8,128)S(1)}, u32[]{:S(2)}, u32[]{:S(2)}) collective-permute-start(f32[392,128]{1,0:T(8,128)S(1)} %maximum_maximum_fusion.refs_0_), channel_id=1, source_target_pairs={{0,1},{1,0},{2,3},{3,2},{4,5},{5,4},{6,7},{7,6},{8,9},{9,8},{10,11... | collective-permute-start | bytes 602120 | tf_op jit(solution)/shard_map/ppermute | solution.py:404
  28.5 6.5 %copy-start.1 = (f32[392,128]{1,0:T(8,128)}, f32[392,128]{1,0:T(8,128)S(1)}, u32[]{:S(2)}) copy-start(f32[392,128]{1,0:T(8,128)S(1)} %collective-permute-done.2.refs_3_) | copy-start | bytes 602116
  28.5 5.4 %collective-permute-start.6 = (f32[392,128]{1,0:T(8,128)S(1)}, f32[392,128]{1,0:T(8,128)S(1)}, u32[]{:S(2)}, u32[]{:S(2)}) collective-permute-start(f32[392,128]{1,0:T(8,128)S(1)} %collective-permute-done.2.refs_3_), channel_id=1, source_target_pairs={{0,1},{1,0},{2,3},{3,2},{4,5},{5,4},{6,7},{7,6},{8,9},{9,8},{10,11... | collective-permute-start | bytes 602120 | tf_op jit(solution)/shard_map/ppermute | solution.py:404
  30.4 4.5 %copy-start.2 = (f32[392,128]{1,0:T(8,128)}, f32[392,128]{1,0:T(8,128)S(1)}, u32[]{:S(2)}) copy-start(f32[392,128]{1,0:T(8,128)S(1)} %collective-permute-done.1.refs_2_) | copy-start | bytes 602116
  30.4 3.4 %collective-permute-start.5 = (f32[392,128]{1,0:T(8,128)S(1)}, f32[392,128]{1,0:T(8,128)S(1)}, u32[]{:S(2)}, u32[]{:S(2)}) collective-permute-start(f32[392,128]{1,0:T(8,128)S(1)} %collective-permute-done.1.refs_2_), channel_id=1, source_target_pairs={{0,1},{1,0},{2,3},{3,2},{4,5},{5,4},{6,7},{7,6},{8,9},{9,8},{10,11... | collective-permute-start | bytes 602120 | tf_op jit(solution)/shard_map/ppermute | solution.py:404
  32.9 2.0 %copy-start.3 = (f32[392,128]{1,0:T(8,128)}, f32[392,128]{1,0:T(8,128)S(1)}, u32[]{:S(2)}) copy-start(f32[392,128]{1,0:T(8,128)S(1)} %collective-permute-done.refs_1_) | copy-start | bytes 602116
  32.9 2.0 %collective-permute-start.4 = (f32[392,128]{1,0:T(8,128)S(1)}, f32[392,128]{1,0:T(8,128)S(1)}, u32[]{:S(2)}, u32[]{:S(2)}) collective-permute-start(f32[392,128]{1,0:T(8,128)S(1)} %collective-permute-done.refs_1_), channel_id=1, source_target_pairs={{0,1},{1,0},{2,3},{3,2},{4,5},{5,4},{6,7},{7,6},{8,9},{9,8},{10,11... | collective-permute-start | bytes 602120 | tf_op jit(solution)/shard_map/ppermute | solution.py:404
  33.8 1.1 copy-start.4
  33.8 1.1 copy-start.5
  33.9 1.1 copy-start.6
  34.9 0.7 copy-start.7

commit v5 on v4

--- a/solution.py
+++ b/solution.py
@@ -164,7 +164,7 @@
 
 def image_kernel(first_ref, *refs):
     own_refs, other_refs, refs = refs[:4], refs[4:8], refs[8:]
-    out_ref, p0_ref, p1_ref, q0_ref, q1_ref, h0_ref, h1_ref, y0_ref, y1_ref, sum_ref, dft_ref, vis_ref = refs
+    out_ref, p0_ref, p1_ref, q0_ref, q1_ref, h0_ref, h1_ref, y0_ref, y1_ref, sum_ref, dft_ref, vis0_ref, vis1_ref, tw_ref, r_ref, ab_ref = refs
     first = first_ref[0]
     segment = lax.broadcasted_iota(jnp.int32, (16, 128), 1) >> 5
     odd, upper = (segment & 1) == 1, segment >= 2
@@ -172,22 +172,27 @@
     def swapped(a, b, mask, by):
         return jnp.where(mask, pltpu.roll(b, by, 1), a), jnp.where(mask, b, pltpu.roll(a, 128 - by, 1))
 
-    def regroup(step, c):
-        for i in [step * 6 + k for k in range(6)]:
-            for half, area in enumerate((own_refs, other_refs)):
-                x = [ref[pl.ds(i, 16, stride=24), :] for ref in area]
-                x[0], x[1] = swapped(x[0], x[1], odd, 32)
-                x[2], x[3] = swapped(x[2], x[3], odd, 32)
-                x[0], x[2] = swapped(x[0], x[2], upper, 64)
-                x[1], x[3] = swapped(x[1], x[3], upper, 64)
-                for j in range(4):
-                    vis_ref[pl.ds(pl.multiple_of((4 * i + j) * GROUPS + 16 * half, 16), 16), :] = x[j]
+    def regroup(v, k, plane, vis_ref):
+        for half, area in enumerate((own_refs, other_refs)):
+            x = [ref[pl.ds(8 * v + 4 * plane + k, 16, stride=24), :] for ref in area]
+            x[0], x[1] = swapped(x[0], x[1], odd, 32)
+            x[2], x[3] = swapped(x[2], x[3], odd, 32)
+            x[0], x[2] = swapped(x[0], x[2], upper, 64)
+            x[1], x[3] = swapped(x[1], x[3], upper, 64)
+            for j in range(4):
+                at = (v * BANDS + 4 * k + j) * GROUPS + 16 * half
+                vis_ref[pl.ds(pl.multiple_of(at, 16), 16), :] = x[j]
+
+    def regroup_first(k, c):
+        for j in range(2):
+            for v in range(3):
+                regroup(v, 2 * k + j, 0, vis0_ref)
         return c
 
-    lax.fori_loop(0, 4, regroup, 0)
-
-    def values(v, s):
-        return vis_ref[pl.ds(pl.multiple_of((v * SETS + s) * GROUPS, GROUPS), GROUPS), :]
+    lax.fori_loop(0, 2, regroup_first, 0)
+
+    def values(v, s, vis_ref):
+        return vis_ref[pl.ds(pl.multiple_of((v * BANDS + s) * GROUPS, GROUPS), GROUPS), :]
 
     def make_dft(i):
         k = 2 * (lax.broadcasted_iota(jnp.int32, (16, 256), 0) + 16 * i) + 1
@@ -199,15 +204,15 @@
             dft_ref[rows, 256:512] = (x - hi.astype(jnp.float32)).astype(jnp.bfloat16)
             dft_ref[rows, 512:768] = hi
 
-    def tables(s, p_ref, q_ref):
-        off = values(2, s).astype(jnp.int32)
+    def tables(s, vis_ref, p_ref, q_ref):
+        off = values(2, s, vis_ref).astype(jnp.int32)
         col = off & (G - 1)
         row = off >> 12
         p_ref[pl.ds(16 * GROUPS, GROUPS), :] = (row & 15).astype(jnp.float32)
         p_ref[pl.ds(17 * GROUPS, GROUPS), :] = (row >> 4).astype(jnp.float32)
         half = cis_half(col)
         one = mul(half, half)
-        base = mul((values(0, s), values(1, s)), cis_half(col * (2 * first + 15) - 16 * (row >> 4) - 256 * (s % BANDS)))
+        base = mul((values(0, s, vis_ref), values(1, s, vis_ref)), cis_half(col * (2 * first + 15) - 16 * (row >> 4) - 256 * s))
         power = half
         for k in range(8):
             q_ref[pl.ds(k * SKIP, GROUPS), :] = power[0]
@@ -242,13 +247,13 @@
                 products.append(jnp.concatenate(two).astype(jnp.bfloat16))
         return jnp.concatenate(o), jnp.concatenate(products)
 
-    def phase(used, later, s, h_ref):
-        tables(jnp.minimum(s + 1, SETS - 1), *later)
+    def phase(used, later, s, h_ref, vis_ref):
+        tables(jnp.minimum(s + 1, BANDS - 1), vis_ref, *later)
         parts = [made(g, *used) for g in range(GROUPS)]
         o = jnp.concatenate([x[0] for x in parts], axis=1)
         e = jnp.concatenate([x[1] for x in parts], axis=1)
         part = lax.dot_general(o, e, (((1,), (1,)), ((), ())), preferred_element_type=jnp.float32)
-        at = pl.ds(pl.multiple_of((s % BANDS) * 16, 16), 16)
+        at = pl.ds(pl.multiple_of(s * 16, 16), 16)
         for k in range(16):
             h_ref[k, at, :] = part[16 * k : 16 * k + 16, :]
 
@@ -295,56 +300,22 @@
         line = sub_row + t * 8
         return pl.ds(pl.multiple_of(t * 8 + 128 * half, 8), 8), 255 - line if half else line
 
-    def terms(at, line, tw, w, y_ref):
+    def twist(at, k):
+        return tw_ref[k - 1, at, :], tw_ref[14 + k, at, :]
+
+    def terms(at, w, y_ref):
         xs = []
         for k in range(16):
             x = (y_ref[k, at, 0:128], y_ref[k, at, 128:256])
-            xs.append(x if k == 0 else mul(x, tw[k]))
+            xs.append(x if k == 0 else mul(x, twist(at, k)))
         f = fft(xs)
-        x0 = line.astype(jnp.float32) * scale
         result = []
         for j in range(16):
-            x = x0 + (256 * j if j < 8 else 256 * j - G) * scale
-            z = rest - x * x
-            turn = w * (z * lax.rsqrt(z)) - w
+            turn = w * r_ref[j, at, :] - w
             turn = turn - jnp.round(turn)
             result.append(mul(f[j], cis4(turn)))
         return result
 
-    buf0, buf1 = (p0_ref, q0_ref), (p1_ref, q1_ref)
-    tables(0, *buf0)
-
-    def sets_of_first(i, c):
-        phase(buf0, buf1, 2 * i, h0_ref)
-        phase(buf1, buf0, 2 * i + 1, h0_ref)
-        make_dft(i)
-        return c
-
-    lax.fori_loop(0, BANDS // 2, sets_of_first, 0)
-
-    def sets_of_second(i, c):
-        phase(buf0, buf1, BANDS + 2 * i, h1_ref)
-        dft(2 * i, h0_ref, y0_ref)
-        phase(buf1, buf0, BANDS + 2 * i + 1, h1_ref)
-        dft(2 * i + 1, h0_ref, y0_ref)
-        return c
-
-    lax.fori_loop(0, BANDS // 2, sets_of_second, 0)
-    w0 = spread8(w_row, 0)
-
-    def tiles_of_first(i, c):
-        for k in range(STEPS):
-            dft(STEPS * i + k, h1_ref, y1_ref)
-        for k in range(STEPS):
-            for half in range(2):
-                at, line = half_tile(STEPS * i + k, half)
-                for j, x in enumerate(terms(at, line, twiddles(line), w0, y0_ref)):
-                    sum_ref[j, at, 0:128] = x[0]
-                    sum_ref[j, at, 128:256] = x[1]
-        return c
-
-    lax.fori_loop(0, 16 // STEPS, tiles_of_first, 0)
-    w1 = spread8(w_row, 1)
     taps = [spread8(taps_row, k) for k in range(8)]
     step = cis_int(lane)
     weight = [x.astype(jnp.bfloat16).astype(jnp.float32) * (1.0 / 512) for x in taps]
@@ -353,18 +324,75 @@
         b = mul(b, step)
         b = (b[0] + weight[k], b[1])
 
-    def tiles_of_second(t, c):
+    def prepare(t):
         for half in range(2):
             at, line = half_tile(t, half)
             tw = twiddles(line)
+            for k in range(1, 16):
+                tw_ref[k - 1, at, :] = tw[k][0]
+                tw_ref[14 + k, at, :] = tw[k][1]
             ts = [(taps[0], jnp.zeros((8, 128), jnp.float32))]
             ts += [(tw[k][0] * taps[k], tw[k][1] * taps[k]) for k in range(1, 8)]
             a = fft(ts + [None] * 8)
+            x0 = line.astype(jnp.float32) * scale
+            for j in range(16):
+                x = x0 + (256 * j if j < 8 else 256 * j - G) * scale
+                z = rest - x * x
+                r_ref[j, at, :] = z * lax.rsqrt(z)
+                ab = mul(a[j], b)
+                ab_ref[2 * j, at, :] = ab[0]
+                ab_ref[2 * j + 1, at, :] = ab[1]
+
+    buf0, buf1 = (p0_ref, q0_ref), (p1_ref, q1_ref)
+    tables(0, vis0_ref, *buf0)
+
+    def sets_of_first(i, c):
+        for k in range(0, 4, 2):
+            phase(buf0, buf1, 4 * i + k, h0_ref, vis0_ref)
+            phase(buf1, buf0, 4 * i + k + 1, h0_ref, vis0_ref)
+            make_dft(2 * i + k // 2)
+            prepare(2 * i + k // 2)
+        for v in range(3):
+            regroup(v, i, 1, vis1_ref)
+        return c
+
+    lax.fori_loop(0, 4, sets_of_first, 0)
+    tables(0, vis1_ref, *buf0)
+
+    def sets_of_second(i, c):
+        for k in range(0, 4, 2):
+            phase(buf0, buf1, 4 * i + k, h1_ref, vis1_ref)
+            dft(4 * i + k, h0_ref, y0_ref)
+            phase(buf1, buf0, 4 * i + k + 1, h1_ref, vis1_ref)
+            dft(4 * i + k + 1, h0_ref, y0_ref)
+            prepare(8 + 2 * i + k // 2)
+        return c
+
+    lax.fori_loop(0, 4, sets_of_second, 0)
+    w0 = spread8(w_row, 0)
+
+    def tiles_of_first(i, c):
+        for k in range(STEPS):
+            dft(STEPS * i + k, h1_ref, y1_ref)
+        for k in range(STEPS):
+            for half in range(2):
+                at, _ = half_tile(STEPS * i + k, half)
+                for j, x in enumerate(terms(at, w0, y0_ref)):
+                    sum_ref[j, at, 0:128] = x[0]
+                    sum_ref[j, at, 128:256] = x[1]
+        return c
+
+    lax.fori_loop(0, 16 // STEPS, tiles_of_first, 0)
+    w1 = spread8(w_row, 1)
+
+    def tiles_of_second(t, c):
+        for half in range(2):
+            at, _ = half_tile(t, half)
             place = pl.ds(pl.multiple_of(248 - t * 8 if half else t * 8, 8), 8)
-            for j, x in enumerate(terms(at, line, tw, w1, y1_ref)):
+            for j, x in enumerate(terms(at, w1, y1_ref)):
                 x = add(x, (sum_ref[j, at, 0:128], sum_ref[j, at, 128:256]))
-                ab = mul(a[j], b)
-                pixel = jnp.take_along_axis(x[0] * ab[0] - x[1] * ab[1], source, axis=1)
+                pixel = x[0] * ab_ref[2 * j, at, :] - x[1] * ab_ref[2 * j + 1, at, :]
+                pixel = jnp.take_along_axis(pixel, source, axis=1)
                 if half:
                     pixel = jnp.take_along_axis(pixel, 7 - sub_row, axis=0)
                 out_ref[j, place, :] = pixel
@@ -392,7 +420,11 @@
             pltpu.VMEM((16, 256, 256), jnp.float32),
             pltpu.VMEM((16, 256, 256), jnp.float32),
             pltpu.VMEM((256, 768), jnp.bfloat16),
-            pltpu.VMEM((3 * SETS * GROUPS, 128), jnp.float32),
+            pltpu.VMEM((3 * BANDS * GROUPS, 128), jnp.float32),
+            pltpu.VMEM((3 * BANDS * GROUPS, 128), jnp.float32),
+            pltpu.VMEM((30, 256, 128), jnp.float32),
+            pltpu.VMEM((16, 256, 128), jnp.float32),
+            pltpu.VMEM((32, 256, 128), jnp.float32),
         ],
         compiler_params=pltpu.CompilerParams(vmem_limit_bytes=56 * 1024 * 1024),
         interpret=interpret,

time: 114 us -> 111 us (0.974)
  Pallas kernels: 46.9 us -> 44.3 us
    pallas_call x1, Pallas kernels: 44.7 us -> 42 us  [part_image(): pl.pallas_call(image_kernel, out_shape=jax.ShapeDtypeStruct((16, 256, COL...]
where the time goes in v5:
time: 111 us
  Pallas kernels  44.3 us (40%)
  blocking collectives  32.1 us (29%)
  starting transfers between devices  19.4 us (17%)
  waiting for transfers between devices  11.7 us (11%)
  local copies, waits for them, and re-layouts  1.43 us (1%)
    pallas_call x1, Pallas kernels, part_image(): pl.pallas_call(image_kernel, out_shape=jax.ShapeDtypeStruct((16, 256, COL...  42 us
    all_to_all x1, blocking collectives, local(): lax.all_to_all(part, PLANE, split_axis=0, concat_axis=0, tiled=True)  32.1 us
    ppermute x7, starting transfers between devices, shifted(): lax.ppermute(x, axis, [(i, (i + by) % length) for i in range(length)])  11.9 us
    all_to_all x1, starting transfers between devices, local(): lax.all_to_all(out, ('plane_1', 'tile_1'), split_axis=0, concat_axis=0, t...  7.56 us
    ppermute x7, waiting for transfers between devices, shifted(): lax.ppermute(x, axis, [(i, (i + by) % length) for i in range(length)])  5.95 us
    all_to_all x1, waiting for transfers between devices, local(): lax.all_to_all(out, ('plane_1', 'tile_1'), split_axis=0, concat_axis=0, t...  5.73 us
    pallas_call x1, Pallas kernels, buckets(): pl.pallas_call(bucket_kernel, out_shape=jax.ShapeDtypeStruct((16, 24, 128...  2.22 us
  transfers between devices with their start and end apart: 8, of which 4 were waited for; matrix products, arithmetic and copies ran while one was open for 1% of the time, Pallas kernels for 0%

profile of v5, /device:TPU:1, one launch (start us, length us, event | category | flops | bytes accessed | tf_op | source)
XLA Modules:
  0.0 110.7 jit_solution(17326372111909590589)
XLA Ops:
  0.0 2.2 %shard_map.55 = f32[16,24,128]{2,1,0:T(8,128)} custom-call(s32[1,2048]{1,0:T(1,128)} %bitcast.17, s32[16,128]{1,0:T(8,128)} %bitcast.18, f32[2,2048]{1,0:T(2,128)} %vis_ref.1), custom_call_target="tpu_custom_call" | custom-call | tf_op jit(solution)/shard_map/pallas_call | solution.py:156
  2.2 7.6 %all-to-all-start = ((f32[16,24,128]{2,1,0:T(8,128)}), f32[16,24,128]{2,1,0:T(8,128)S(1)}, u32[]{:S(2)}, u32[]{:S(2)}) async-start(f32[16,24,128]{2,1,0:T(8,128)} %shard_map.55), calls=%async_computation | async-start | bytes 393216 | tf_op jit(solution)/shard_map/all_to_all | solution.py:442
  10.5 0.1 pad.10.clone
  10.5 0.7 pad_bitcast_fusion
  11.2 5.7 %all-to-all-done = f32[16,24,128]{2,1,0:T(8,128)S(1)} async-done(((f32[16,24,128]{2,1,0:T(8,128)}), f32[16,24,128]{2,1,0:T(8,128)S(1)}, u32[]{:S(2)}, u32[]{:S(2)}) %all-to-all-start) | async-done | bytes 196640 | tf_op jit(solution)/shard_map/all_to_all | solution.py:442
  16.9 0.1 maximum_maximum_fusion.refs_0_
  17.1 0.0 copy-start
  17.1 3.9 %collective-permute-start.2 = (f32[392,128]{1,0:T(8,128)S(1)}, f32[392,128]{1,0:T(8,128)S(1)}, u32[]{:S(2)}, u32[]{:S(2)}) collective-permute-start(f32[392,128]{1,0:T(8,128)S(1)} %maximum_maximum_fusion.refs_0_), channel_id=1, source_target_pairs={{0,72},{8,0},{64,8},{72,64},{1,73},{9,1},{65,9},{73,65},{2,74},{10... | collective-permute-start | bytes 602120 | tf_op jit(solution)/shard_map/ppermute | solution.py:436
  20.9 0.0 collective-permute-start.1
  20.9 0.7 collective-permute-start
  21.6 2.8 %collective-permute-start.3 = (f32[392,128]{1,0:T(8,128)S(1)}, f32[392,128]{1,0:T(8,128)S(1)}, u32[]{:S(2)}, u32[]{:S(2)}) collective-permute-start(f32[392,128]{1,0:T(8,128)S(1)} %maximum_maximum_fusion.refs_0_), channel_id=1, source_target_pairs={{0,1},{1,0},{2,3},{3,2},{4,5},{5,4},{6,7},{7,6},{8,9},{9,8},{10,11... | collective-permute-start | bytes 602120 | tf_op jit(solution)/shard_map/ppermute | solution.py:436
  24.4 4.0 %collective-permute-done.2.refs_3_ = f32[392,128]{1,0:T(8,128)S(1)} collective-permute-done((f32[392,128]{1,0:T(8,128)S(1)}, f32[392,128]{1,0:T(8,128)S(1)}, u32[]{:S(2)}, u32[]{:S(2)}) %collective-permute-start.2) | collective-permute-done | bytes 200736 | tf_op jit(solution)/shard_map/ppermute | solution.py:436
  28.5 0.0 copy-start.1
  28.5 2.0 %collective-permute-start.6 = (f32[392,128]{1,0:T(8,128)S(1)}, f32[392,128]{1,0:T(8,128)S(1)}, u32[]{:S(2)}, u32[]{:S(2)}) collective-permute-start(f32[392,128]{1,0:T(8,128)S(1)} %collective-permute-done.2.refs_3_), channel_id=1, source_target_pairs={{0,1},{1,0},{2,3},{3,2},{4,5},{5,4},{6,7},{7,6},{8,9},{9,8},{10,11... | collective-permute-start | bytes 602120 | tf_op jit(solution)/shard_map/ppermute | solution.py:436
  30.4 0.0 collective-permute-done.1.refs_2_
  30.4 0.0 copy-start.2
  30.4 1.6 %collective-permute-start.5 = (f32[392,128]{1,0:T(8,128)S(1)}, f32[392,128]{1,0:T(8,128)S(1)}, u32[]{:S(2)}, u32[]{:S(2)}) collective-permute-start(f32[392,128]{1,0:T(8,128)S(1)} %collective-permute-done.1.refs_2_), channel_id=1, source_target_pairs={{0,1},{1,0},{2,3},{3,2},{4,5},{5,4},{6,7},{7,6},{8,9},{9,8},{10,11... | collective-permute-start | bytes 602120 | tf_op jit(solution)/shard_map/ppermute | solution.py:436
  32.0 0.9 collective-permute-done.refs_1_
  32.9 0.0 copy-start.3
  32.9 1.0 collective-permute-start.4
  33.8 0.0 collective-permute-done.3.refs_4_
  33.8 0.0 copy-start.4
  33.8 0.0 collective-permute-done.6.refs_7_
  33.8 0.0 copy-start.5
  33.9 0.0 collective-permute-done.5.refs_6_
  33.9 0.0 copy-start.6
  33.9 1.0 collective-permute-done.4.refs_5_
  34.9 0.0 copy-start.7
  34.9 0.0 copy-done
  34.9 0.0 copy-done.1
  34.9 0.0 copy-done.2
  34.9 0.0 copy-done.3
  34.9 0.0 copy-done.4
  34.9 0.0 copy-done.5
  35.0 0.0 copy-done.6
  35.0 0.6 copy-done.7
  35.6 42.0 %shard_map.56 = f32[16,256,128]{2,1,0:T(8,128)} custom-call(s32[1]{0:T(128)} %bitcast.first_ref, f32[392,128]{1,0:T(8,128)} %copy-done, f32[392,128]{1,0:T(8,128)} %copy-done.3, f32[392,128]{1,0:T(8,128)} %copy-done.2, f32[392,128]{1,0:T(8,128)} %copy-done.1, f32[392,128]{1,0:T(8,128)} %copy-done.4, f32[392,128]{1,0:T(8,128)} %copy-done.7, ...), custom_call_target="tpu_custom_call" | custom-call | tf_op jit(solution)/shard_map/pallas_call | solution.py:407
  77.6 32.1 %all_to_all.14 = f32[8,512,128]{2,1,0:T(8,128)S(1)} all-to-all(f32[8,512,128]{2,1,0:T(8,128)} %bitcast.15), channel_id=1, replica_groups=mesh['plane_0'=2,'plane_1'=4,'tile_0'=2,'tile_1'=4,'tile_2'=2] {'plane_0..., dimensions={0} | all-to-all | bytes 4194304 | tf_op jit(solution)/shard_map/all_to_all | solution.py:450
  109.7 0.1 bitcast_reduce_fusion
  109.9 0.8 pad_maximum_fusion
  (3 shorter events, 0.0 us)
Async XLA Ops:
  2.2 14.7 %all-to-all-start = ((f32[16,24,128]{2,1,0:T(8,128)}), f32[16,24,128]{2,1,0:T(8,128)S(1)}, u32[]{:S(2)}, u32[]{:S(2)}) async-start(f32[16,24,128]{2,1,0:T(8,128)} %shard_map.55), calls=%async_computation | async-start | bytes 393216 | tf_op jit(solution)/shard_map/all_to_all | solution.py:442
  17.1 17.9 %copy-start = (f32[392,128]{1,0:T(8,128)}, f32[392,128]{1,0:T(8,128)S(1)}, u32[]{:S(2)}) copy-start(f32[392,128]{1,0:T(8,128)S(1)} %maximum_maximum_fusion.refs_0_) | copy-start | bytes 602116
  17.1 11.4 %collective-permute-start.2 = (f32[392,128]{1,0:T(8,128)S(1)}, f32[392,128]{1,0:T(8,128)S(1)}, u32[]{:S(2)}, u32[]{:S(2)}) collective-permute-start(f32[392,128]{1,0:T(8,128)S(1)} %maximum_maximum_fusion.refs_0_), channel_id=1, source_target_pairs={{0,72},{8,0},{64,8},{72,64},{1,73},{9,1},{65,9},{73,65},{2,74},{10... | collective-permute-start | bytes 602120 | tf_op jit(solution)/shard_map/ppermute | solution.py:436
  20.9 9.5 %collective-permute-start.1 = (f32[392,128]{1,0:T(8,128)S(1)}, f32[392,128]{1,0:T(8,128)S(1)}, u32[]{:S(2)}, u32[]{:S(2)}) collective-permute-start(f32[392,128]{1,0:T(8,128)S(1)} %maximum_maximum_fusion.refs_0_), channel_id=1, source_target_pairs={{0,64},{8,72},{64,0},{72,8},{1,65},{9,73},{65,1},{73,9},{2,66},{10... | collective-permute-start | bytes 602120 | tf_op jit(solution)/shard_map/ppermute | solution.py:436
  20.9 12.0 %collective-permute-start = (f32[392,128]{1,0:T(8,128)S(1)}, f32[392,128]{1,0:T(8,128)S(1)}, u32[]{:S(2)}, u32[]{:S(2)}) collective-permute-start(f32[392,128]{1,0:T(8,128)S(1)} %maximum_maximum_fusion.refs_0_), channel_id=1, source_target_pairs={{0,8},{8,64},{64,72},{72,0},{1,9},{9,65},{65,73},{73,1},{2,10},{10... | collective-permute-start | bytes 602120 | tf_op jit(solution)/shard_map/ppermute | solution.py:436
  21.6 12.2 %collective-permute-start.3 = (f32[392,128]{1,0:T(8,128)S(1)}, f32[392,128]{1,0:T(8,128)S(1)}, u32[]{:S(2)}, u32[]{:S(2)}) collective-permute-start(f32[392,128]{1,0:T(8,128)S(1)} %maximum_maximum_fusion.refs_0_), channel_id=1, source_target_pairs={{0,1},{1,0},{2,3},{3,2},{4,5},{5,4},{6,7},{7,6},{8,9},{9,8},{10,11... | collective-permute-start | bytes 602120 | tf_op jit(solution)/shard_map/ppermute | solution.py:436
  28.5 6.5 %copy-start.1 = (f32[392,128]{1,0:T(8,128)}, f32[392,128]{1,0:T(8,128)S(1)}, u32[]{:S(2)}) copy-start(f32[392,128]{1,0:T(8,128)S(1)} %collective-permute-done.2.refs_3_) | copy-start | bytes 602116
  28.5 5.4 %collective-permute-start.6 = (f32[392,128]{1,0:T(8,128)S(1)}, f32[392,128]{1,0:T(8,128)S(1)}, u32[]{:S(2)}, u32[]{:S(2)}) collective-permute-start(f32[392,128]{1,0:T(8,128)S(1)} %collective-permute-done.2.refs_3_), channel_id=1, source_target_pairs={{0,1},{1,0},{2,3},{3,2},{4,5},{5,4},{6,7},{7,6},{8,9},{9,8},{10,11... | collective-permute-start | bytes 602120 | tf_op jit(solution)/shard_map/ppermute | solution.py:436
  30.4 4.5 %copy-start.2 = (f32[392,128]{1,0:T(8,128)}, f32[392,128]{1,0:T(8,128)S(1)}, u32[]{:S(2)}) copy-start(f32[392,128]{1,0:T(8,128)S(1)} %collective-permute-done.1.refs_2_) | copy-start | bytes 602116
  30.4 3.4 %collective-permute-start.5 = (f32[392,128]{1,0:T(8,128)S(1)}, f32[392,128]{1,0:T(8,128)S(1)}, u32[]{:S(2)}, u32[]{:S(2)}) collective-permute-start(f32[392,128]{1,0:T(8,128)S(1)} %collective-permute-done.1.refs_2_), channel_id=1, source_target_pairs={{0,1},{1,0},{2,3},{3,2},{4,5},{5,4},{6,7},{7,6},{8,9},{9,8},{10,11... | collective-permute-start | bytes 602120 | tf_op jit(solution)/shard_map/ppermute | solution.py:436
  32.9 2.0 %copy-start.3 = (f32[392,128]{1,0:T(8,128)}, f32[392,128]{1,0:T(8,128)S(1)}, u32[]{:S(2)}) copy-start(f32[392,128]{1,0:T(8,128)S(1)} %collective-permute-done.refs_1_) | copy-start | bytes 602116
  32.9 2.0 %collective-permute-start.4 = (f32[392,128]{1,0:T(8,128)S(1)}, f32[392,128]{1,0:T(8,128)S(1)}, u32[]{:S(2)}, u32[]{:S(2)}) collective-permute-start(f32[392,128]{1,0:T(8,128)S(1)} %collective-permute-done.refs_1_), channel_id=1, source_target_pairs={{0,1},{1,0},{2,3},{3,2},{4,5},{5,4},{6,7},{7,6},{8,9},{9,8},{10,11... | collective-permute-start | bytes 602120 | tf_op jit(solution)/shard_map/ppermute | solution.py:436
  33.8 1.1 copy-start.4
  33.8 1.1 copy-start.5
  33.9 1.1 copy-start.6
  34.9 0.7 copy-start.7

commit v6 on v5

--- a/solution.py
+++ b/solution.py
@@ -19,7 +19,7 @@
 COLS = 128
 SETS = PAIR * BANDS
 SKIP = 33
-STEPS = 2
+STEPS = 4
 GROUPS = 32
 
 SIN = (6.283183359351797, -41.341456456971535, 81.59688036372165, -76.58598132852413,
@@ -146,7 +146,7 @@
     r = [r[32 * k : 32 * k + 32] for k in range(7)]
     both = (r[0] + r[1], r[2] + r[3], r[4] * 4096.0 + r[5] * 16.0 + r[6])
     for i in range(16):
-        x = i // 4
+        x = i % 4
         for v in range(3):
             out_ref[i, 8 * v : 8 * v + 8, :] = both[v][8 * x : 8 * x + 8]
 
@@ -395,7 +395,7 @@
                 pixel = jnp.take_along_axis(pixel, source, axis=1)
                 if half:
                     pixel = jnp.take_along_axis(pixel, 7 - sub_row, axis=0)
-                out_ref[j, place, :] = pixel
+                out_ref[4 * (j // 2 % 4) + 2 * (j // 8) + j % 2, place, :] = pixel
         return c
 
     lax.fori_loop(0, 16, tiles_of_second, 0)
@@ -439,7 +439,7 @@
 def local(visibility, target, offset, taps, w_plane):
     half = lax.axis_index("plane_0")
     out = buckets(target.reshape(1, 2048), offset.reshape(16, 128), visibility)
-    own = lax.all_to_all(out, ("plane_1", "tile_1"), split_axis=0, concat_axis=0, tiled=True).reshape(384, 128)
+    own = lax.all_to_all(out, ("tile_1", "plane_1"), split_axis=0, concat_axis=0, tiled=True).reshape(384, 128)
     w_row = jnp.where(jnp.arange(128) == half, w_plane[0], 0.0)
     own = jnp.concatenate([own, w_row[None], jnp.pad(taps, (0, 120))[None], jnp.zeros((6, 128), jnp.float32)])
     area = [own] + [shifted(own, ("plane_0", "tile_0"), by) for by in (1, 2, 3)]
@@ -447,8 +447,8 @@
     first = lax.axis_index(TILE) * 256 + half * COLS
     first = first.reshape(1).astype(jnp.int32)
     part = part_image(first, *area).reshape(G, COLS)
-    arrived = lax.all_to_all(part, PLANE, split_axis=0, concat_axis=0, tiled=True)
-    total = arrived.reshape(2, 4, 512, COLS).sum(axis=1)
+    arrived = lax.all_to_all(part, PLANE[::-1], split_axis=0, concat_axis=0, tiled=True)
+    total = arrived.reshape(4, 2, 512, COLS).sum(axis=0)
     return jnp.concatenate([total[0], total[1]], axis=1)
 
 

time: 111 us -> 109 us (0.982)
  no operation moved by 1% of the time
where the time goes in v6:
time: 109 us
  Pallas kernels  43.4 us (40%)
  blocking collectives  31.1 us (29%)
  starting transfers between devices  19.8 us (18%)
  waiting for transfers between devices  11.4 us (10%)
  local copies, waits for them, and re-layouts  1.43 us (1%)
  other arithmetic  1.09 us (1%)
    pallas_call x1, Pallas kernels, part_image(): pl.pallas_call(image_kernel, out_shape=jax.ShapeDtypeStruct((16, 256, COL...  41.2 us
    all_to_all x1, blocking collectives, local(): lax.all_to_all(part, PLANE[::-1], split_axis=0, concat_axis=0, tiled=True)  31.1 us
    ppermute x7, starting transfers between devices, shifted(): lax.ppermute(x, axis, [(i, (i + by) % length) for i in range(length)])  12.2 us
    all_to_all x1, starting transfers between devices, local(): lax.all_to_all(out, ('tile_1', 'plane_1'), split_axis=0, concat_axis=0, t...  7.57 us
    all_to_all x1, waiting for transfers between devices, local(): lax.all_to_all(out, ('tile_1', 'plane_1'), split_axis=0, concat_axis=0, t...  5.79 us
    ppermute x7, waiting for transfers between devices, shifted(): lax.ppermute(x, axis, [(i, (i + by) % length) for i in range(length)])  5.6 us
    pallas_call x1, Pallas kernels, buckets(): pl.pallas_call(bucket_kernel, out_shape=jax.ShapeDtypeStruct((16, 24, 128...  2.21 us
  transfers between devices with their start and end apart: 8, of which 4 were waited for; matrix products, arithmetic and copies ran while one was open for 1% of the time, Pallas kernels for 0%

profile of v6, /device:TPU:1, one launch (start us, length us, event | category | flops | bytes accessed | tf_op | source)
XLA Modules:
  0.0 109.0 jit_solution(5769737450303832698)
XLA Ops:
  0.0 2.2 %shard_map.55 = f32[16,24,128]{2,1,0:T(8,128)} custom-call(s32[1,2048]{1,0:T(1,128)} %bitcast.17, s32[16,128]{1,0:T(8,128)} %bitcast.18, f32[2,2048]{1,0:T(2,128)} %vis_ref.1), custom_call_target="tpu_custom_call" | custom-call | tf_op jit(solution)/shard_map/pallas_call | solution.py:156
  2.2 7.6 %all-to-all-start = ((f32[16,24,128]{2,1,0:T(8,128)}), f32[16,24,128]{2,1,0:T(8,128)S(1)}, u32[]{:S(2)}, u32[]{:S(2)}) async-start(f32[16,24,128]{2,1,0:T(8,128)} %shard_map.55), calls=%async_computation | async-start | bytes 393216 | tf_op jit(solution)/shard_map/all_to_all | solution.py:442
  10.5 0.1 pad.10.clone
  10.5 0.7 pad_bitcast_fusion
  11.2 5.8 %all-to-all-done = f32[16,24,128]{2,1,0:T(8,128)S(1)} async-done(((f32[16,24,128]{2,1,0:T(8,128)}), f32[16,24,128]{2,1,0:T(8,128)S(1)}, u32[]{:S(2)}, u32[]{:S(2)}) %all-to-all-start) | async-done | bytes 196640 | tf_op jit(solution)/shard_map/all_to_all | solution.py:442
  17.0 0.1 maximum_maximum_fusion.refs_0_
  17.1 0.0 copy-start
  17.1 3.8 %collective-permute-start.2 = (f32[392,128]{1,0:T(8,128)S(1)}, f32[392,128]{1,0:T(8,128)S(1)}, u32[]{:S(2)}, u32[]{:S(2)}) collective-permute-start(f32[392,128]{1,0:T(8,128)S(1)} %maximum_maximum_fusion.refs_0_), channel_id=1, source_target_pairs={{0,72},{8,0},{64,8},{72,64},{1,73},{9,1},{65,9},{73,65},{2,74},{10... | collective-permute-start | bytes 602120 | tf_op jit(solution)/shard_map/ppermute | solution.py:436
  21.0 0.0 collective-permute-start.1
  21.0 0.7 collective-permute-start
  21.6 3.0 %collective-permute-start.3 = (f32[392,128]{1,0:T(8,128)S(1)}, f32[392,128]{1,0:T(8,128)S(1)}, u32[]{:S(2)}, u32[]{:S(2)}) collective-permute-start(f32[392,128]{1,0:T(8,128)S(1)} %maximum_maximum_fusion.refs_0_), channel_id=1, source_target_pairs={{0,1},{1,0},{2,3},{3,2},{4,5},{5,4},{6,7},{7,6},{8,9},{9,8},{10,11... | collective-permute-start | bytes 602120 | tf_op jit(solution)/shard_map/ppermute | solution.py:436
  24.6 3.8 %collective-permute-done.2.refs_3_ = f32[392,128]{1,0:T(8,128)S(1)} collective-permute-done((f32[392,128]{1,0:T(8,128)S(1)}, f32[392,128]{1,0:T(8,128)S(1)}, u32[]{:S(2)}, u32[]{:S(2)}) %collective-permute-start.2) | collective-permute-done | bytes 200736 | tf_op jit(solution)/shard_map/ppermute | solution.py:436
  28.4 0.0 copy-start.1
  28.4 2.0 %collective-permute-start.6 = (f32[392,128]{1,0:T(8,128)S(1)}, f32[392,128]{1,0:T(8,128)S(1)}, u32[]{:S(2)}, u32[]{:S(2)}) collective-permute-start(f32[392,128]{1,0:T(8,128)S(1)} %collective-permute-done.2.refs_3_), channel_id=1, source_target_pairs={{0,1},{1,0},{2,3},{3,2},{4,5},{5,4},{6,7},{7,6},{8,9},{9,8},{10,11... | collective-permute-start | bytes 602120 | tf_op jit(solution)/shard_map/ppermute | solution.py:436
  30.5 0.0 collective-permute-done.1.refs_2_
  30.5 0.0 copy-start.2
  30.5 1.6 %collective-permute-start.5 = (f32[392,128]{1,0:T(8,128)S(1)}, f32[392,128]{1,0:T(8,128)S(1)}, u32[]{:S(2)}, u32[]{:S(2)}) collective-permute-start(f32[392,128]{1,0:T(8,128)S(1)} %collective-permute-done.1.refs_2_), channel_id=1, source_target_pairs={{0,1},{1,0},{2,3},{3,2},{4,5},{5,4},{6,7},{7,6},{8,9},{9,8},{10,11... | collective-permute-start | bytes 602120 | tf_op jit(solution)/shard_map/ppermute | solution.py:436
  32.1 0.7 collective-permute-done.refs_1_
  32.8 0.0 copy-start.3
  32.8 1.1 collective-permute-start.4
  33.9 0.0 collective-permute-done.3.refs_4_
  33.9 0.0 copy-start.4
  33.9 0.0 collective-permute-done.6.refs_7_
  33.9 0.0 copy-start.5
  33.9 0.0 collective-permute-done.5.refs_6_
  33.9 0.0 copy-start.6
  33.9 1.0 collective-permute-done.4.refs_5_
  35.0 0.0 copy-start.7
  35.0 0.0 copy-done
  35.0 0.0 copy-done.1
  35.0 0.0 copy-done.2
  35.0 0.0 copy-done.3
  35.0 0.0 copy-done.4
  35.0 0.0 copy-done.5
  35.0 0.0 copy-done.6
  35.0 0.6 copy-done.7
  35.6 41.2 %shard_map.56 = f32[16,256,128]{2,1,0:T(8,128)} custom-call(s32[1]{0:T(128)} %bitcast.first_ref, f32[392,128]{1,0:T(8,128)} %copy-done, f32[392,128]{1,0:T(8,128)} %copy-done.3, f32[392,128]{1,0:T(8,128)} %copy-done.2, f32[392,128]{1,0:T(8,128)} %copy-done.1, f32[392,128]{1,0:T(8,128)} %copy-done.4, f32[392,128]{1,0:T(8,128)} %copy-done.7, ...), custom_call_target="tpu_custom_call" | custom-call | tf_op jit(solution)/shard_map/pallas_call | solution.py:407
  76.9 31.1 %all_to_all.14 = f32[8,512,128]{2,1,0:T(8,128)S(1)} all-to-all(f32[8,512,128]{2,1,0:T(8,128)} %bitcast.14), channel_id=1, replica_groups=mesh['plane_0'=2,'plane_1'=4,'tile_0'=2,'tile_1'=4,'tile_2'=2] {'plane_1..., dimensions={0} | all-to-all | bytes 4194304 | tf_op jit(solution)/shard_map/all_to_all | solution.py:450
  108.0 0.1 reduce_sum.9
  108.2 0.8 pad_maximum_fusion
  (3 shorter events, 0.0 us)
Async XLA Ops:
  2.2 14.8 %all-to-all-start = ((f32[16,24,128]{2,1,0:T(8,128)}), f32[16,24,128]{2,1,0:T(8,128)S(1)}, u32[]{:S(2)}, u32[]{:S(2)}) async-start(f32[16,24,128]{2,1,0:T(8,128)} %shard_map.55), calls=%async_computation | async-start | bytes 393216 | tf_op jit(solution)/shard_map/all_to_all | solution.py:442
  17.1 17.8 %copy-start = (f32[392,128]{1,0:T(8,128)}, f32[392,128]{1,0:T(8,128)S(1)}, u32[]{:S(2)}) copy-start(f32[392,128]{1,0:T(8,128)S(1)} %maximum_maximum_fusion.refs_0_) | copy-start | bytes 602116
  17.1 11.3 %collective-permute-start.2 = (f32[392,128]{1,0:T(8,128)S(1)}, f32[392,128]{1,0:T(8,128)S(1)}, u32[]{:S(2)}, u32[]{:S(2)}) collective-permute-start(f32[392,128]{1,0:T(8,128)S(1)} %maximum_maximum_fusion.refs_0_), channel_id=1, source_target_pairs={{0,72},{8,0},{64,8},{72,64},{1,73},{9,1},{65,9},{73,65},{2,74},{10... | collective-permute-start | bytes 602120 | tf_op jit(solution)/shard_map/ppermute | solution.py:436
  21.0 9.5 %collective-permute-start.1 = (f32[392,128]{1,0:T(8,128)S(1)}, f32[392,128]{1,0:T(8,128)S(1)}, u32[]{:S(2)}, u32[]{:S(2)}) collective-permute-start(f32[392,128]{1,0:T(8,128)S(1)} %maximum_maximum_fusion.refs_0_), channel_id=1, source_target_pairs={{0,64},{8,72},{64,0},{72,8},{1,65},{9,73},{65,1},{73,9},{2,66},{10... | collective-permute-start | bytes 602120 | tf_op jit(solution)/shard_map/ppermute | solution.py:436
  21.0 11.8 %collective-permute-start = (f32[392,128]{1,0:T(8,128)S(1)}, f32[392,128]{1,0:T(8,128)S(1)}, u32[]{:S(2)}, u32[]{:S(2)}) collective-permute-start(f32[392,128]{1,0:T(8,128)S(1)} %maximum_maximum_fusion.refs_0_), channel_id=1, source_target_pairs={{0,8},{8,64},{64,72},{72,0},{1,9},{9,65},{65,73},{73,1},{2,10},{10... | collective-permute-start | bytes 602120 | tf_op jit(solution)/shard_map/ppermute | solution.py:436
  21.6 12.2 %collective-permute-start.3 = (f32[392,128]{1,0:T(8,128)S(1)}, f32[392,128]{1,0:T(8,128)S(1)}, u32[]{:S(2)}, u32[]{:S(2)}) collective-permute-start(f32[392,128]{1,0:T(8,128)S(1)} %maximum_maximum_fusion.refs_0_), channel_id=1, source_target_pairs={{0,1},{1,0},{2,3},{3,2},{4,5},{5,4},{6,7},{7,6},{8,9},{9,8},{10,11... | collective-permute-start | bytes 602120 | tf_op jit(solution)/shard_map/ppermute | solution.py:436
  28.4 6.5 %copy-start.1 = (f32[392,128]{1,0:T(8,128)}, f32[392,128]{1,0:T(8,128)S(1)}, u32[]{:S(2)}) copy-start(f32[392,128]{1,0:T(8,128)S(1)} %collective-permute-done.2.refs_3_) | copy-start | bytes 602116
  28.4 5.4 %collective-permute-start.6 = (f32[392,128]{1,0:T(8,128)S(1)}, f32[392,128]{1,0:T(8,128)S(1)}, u32[]{:S(2)}, u32[]{:S(2)}) collective-permute-start(f32[392,128]{1,0:T(8,128)S(1)} %collective-permute-done.2.refs_3_), channel_id=1, source_target_pairs={{0,1},{1,0},{2,3},{3,2},{4,5},{5,4},{6,7},{7,6},{8,9},{9,8},{10,11... | collective-permute-start | bytes 602120 | tf_op jit(solution)/shard_map/ppermute | solution.py:436
  30.5 4.5 %copy-start.2 = (f32[392,128]{1,0:T(8,128)}, f32[392,128]{1,0:T(8,128)S(1)}, u32[]{:S(2)}) copy-start(f32[392,128]{1,0:T(8,128)S(1)} %collective-permute-done.1.refs_2_) | copy-start | bytes 602116
  30.5 3.4 %collective-permute-start.5 = (f32[392,128]{1,0:T(8,128)S(1)}, f32[392,128]{1,0:T(8,128)S(1)}, u32[]{:S(2)}, u32[]{:S(2)}) collective-permute-start(f32[392,128]{1,0:T(8,128)S(1)} %collective-permute-done.1.refs_2_), channel_id=1, source_target_pairs={{0,1},{1,0},{2,3},{3,2},{4,5},{5,4},{6,7},{7,6},{8,9},{9,8},{10,11... | collective-permute-start | bytes 602120 | tf_op jit(solution)/shard_map/ppermute | solution.py:436
  32.8 2.2 %copy-start.3 = (f32[392,128]{1,0:T(8,128)}, f32[392,128]{1,0:T(8,128)S(1)}, u32[]{:S(2)}) copy-start(f32[392,128]{1,0:T(8,128)S(1)} %collective-permute-done.refs_1_) | copy-start | bytes 602116
  32.8 2.2 %collective-permute-start.4 = (f32[392,128]{1,0:T(8,128)S(1)}, f32[392,128]{1,0:T(8,128)S(1)}, u32[]{:S(2)}, u32[]{:S(2)}) collective-permute-start(f32[392,128]{1,0:T(8,128)S(1)} %collective-permute-done.refs_1_), channel_id=1, source_target_pairs={{0,1},{1,0},{2,3},{3,2},{4,5},{5,4},{6,7},{7,6},{8,9},{9,8},{10,11... | collective-permute-start | bytes 602120 | tf_op jit(solution)/shard_map/ppermute | solution.py:436
  33.9 1.1 %copy-start.4 = (f32[392,128]{1,0:T(8,128)}, f32[392,128]{1,0:T(8,128)S(1)}, u32[]{:S(2)}) copy-start(f32[392,128]{1,0:T(8,128)S(1)} %collective-permute-done.3.refs_4_) | copy-start | bytes 602116
  33.9 1.1 %copy-start.5 = (f32[392,128]{1,0:T(8,128)}, f32[392,128]{1,0:T(8,128)S(1)}, u32[]{:S(2)}) copy-start(f32[392,128]{1,0:T(8,128)S(1)} %collective-permute-done.6.refs_7_) | copy-start | bytes 602116
  33.9 1.1 copy-start.6
  35.0 0.7 copy-start.7

commit v7 on v6

--- a/solution.py
+++ b/solution.py
@@ -442,7 +442,7 @@
     own = lax.all_to_all(out, ("tile_1", "plane_1"), split_axis=0, concat_axis=0, tiled=True).reshape(384, 128)
     w_row = jnp.where(jnp.arange(128) == half, w_plane[0], 0.0)
     own = jnp.concatenate([own, w_row[None], jnp.pad(taps, (0, 120))[None], jnp.zeros((6, 128), jnp.float32)])
-    area = [own] + [shifted(own, ("plane_0", "tile_0"), by) for by in (1, 2, 3)]
+    area = [own] + [shifted(own, ("plane_0", "tile_0"), by) for by in (2, 1, 3)]
     area = area + [shifted(x, "tile_2", 1) for x in area]
     first = lax.axis_index(TILE) * 256 + half * COLS
     first = first.reshape(1).astype(jnp.int32)

time: 109 us -> 110 us (level)
  starting transfers between devices: 19.8 us -> 24.6 us
  waiting for transfers between devices: 11.4 us -> 6.95 us
    ppermute x7, starting transfers between devices: 12.2 us -> 17 us  [shifted(): lax.ppermute(x, axis, [(i, (i + by) % length) for i in range(length)])]
    ppermute x7, waiting for transfers between devices: 5.6 us -> 1.16 us  [shifted(): lax.ppermute(x, axis, [(i, (i + by) % length) for i in range(length)])]
  transfers between devices with their start and end apart: 8 -> 8, of which waited for: 4 -> 3; matrix products, arithmetic and copies ran while one was open for 1% -> 1% of each run, Pallas kernels for 0% -> 0%
where the time goes in v7:
time: 110 us
  Pallas kernels  43.4 us (39%)
  blocking collectives  31.4 us (29%)
  starting transfers between devices  24.6 us (22%)
  waiting for transfers between devices  6.95 us (6%)
  local copies, waits for them, and re-layouts  1.44 us (1%)
    pallas_call x1, Pallas kernels, part_image(): pl.pallas_call(image_kernel, out_shape=jax.ShapeDtypeStruct((16, 256, COL...  41.2 us
    all_to_all x1, blocking collectives, local(): lax.all_to_all(part, PLANE[::-1], split_axis=0, concat_axis=0, tiled=True)  31.4 us
    ppermute x7, starting transfers between devices, shifted(): lax.ppermute(x, axis, [(i, (i + by) % length) for i in range(length)])  17 us
    all_to_all x1, starting transfers between devices, local(): lax.all_to_all(out, ('tile_1', 'plane_1'), split_axis=0, concat_axis=0, t...  7.57 us
    all_to_all x1, waiting for transfers between devices, local(): lax.all_to_all(out, ('tile_1', 'plane_1'), split_axis=0, concat_axis=0, t...  5.79 us
    pallas_call x1, Pallas kernels, buckets(): pl.pallas_call(bucket_kernel, out_shape=jax.ShapeDtypeStruct((16, 24, 128...  2.21 us
  transfers between devices with their start and end apart: 8, of which 3 were waited for; matrix products, arithmetic and copies ran while one was open for 1% of the time, Pallas kernels for 0%

profile of v7, /device:TPU:1, one launch (start us, length us, event | category | flops | bytes accessed | tf_op | source)
XLA Modules:
  0.0 109.7 jit_solution(8608244218632450148)
XLA Ops:
  0.0 2.2 %shard_map.55 = f32[16,24,128]{2,1,0:T(8,128)} custom-call(s32[1,2048]{1,0:T(1,128)} %bitcast.17, s32[16,128]{1,0:T(8,128)} %bitcast.18, f32[2,2048]{1,0:T(2,128)} %vis_ref.1), custom_call_target="tpu_custom_call" | custom-call | tf_op jit(solution)/shard_map/pallas_call | solution.py:156
  2.2 7.6 %all-to-all-start = ((f32[16,24,128]{2,1,0:T(8,128)}), f32[16,24,128]{2,1,0:T(8,128)S(1)}, u32[]{:S(2)}, u32[]{:S(2)}) async-start(f32[16,24,128]{2,1,0:T(8,128)} %shard_map.55), calls=%async_computation | async-start | bytes 393216 | tf_op jit(solution)/shard_map/all_to_all | solution.py:442
  10.5 0.1 pad.10.clone
  10.5 0.7 pad_bitcast_fusion
  11.2 5.8 %all-to-all-done = f32[16,24,128]{2,1,0:T(8,128)S(1)} async-done(((f32[16,24,128]{2,1,0:T(8,128)}), f32[16,24,128]{2,1,0:T(8,128)S(1)}, u32[]{:S(2)}, u32[]{:S(2)}) %all-to-all-start) | async-done | bytes 196640 | tf_op jit(solution)/shard_map/all_to_all | solution.py:442
  17.0 0.1 maximum_maximum_fusion.refs_0_
  17.1 0.0 copy-start
  17.1 3.8 %collective-permute-start.2 = (f32[392,128]{1,0:T(8,128)S(1)}, f32[392,128]{1,0:T(8,128)S(1)}, u32[]{:S(2)}, u32[]{:S(2)}) collective-permute-start(f32[392,128]{1,0:T(8,128)S(1)} %maximum_maximum_fusion.refs_0_), channel_id=1, source_target_pairs={{0,72},{8,0},{64,8},{72,64},{1,73},{9,1},{65,9},{73,65},{2,74},{10... | collective-permute-start | bytes 602120 | tf_op jit(solution)/shard_map/ppermute | solution.py:436
  21.0 0.0 collective-permute-start.1
  21.0 1.3 %collective-permute-start = (f32[392,128]{1,0:T(8,128)S(1)}, f32[392,128]{1,0:T(8,128)S(1)}, u32[]{:S(2)}, u32[]{:S(2)}) collective-permute-start(f32[392,128]{1,0:T(8,128)S(1)} %maximum_maximum_fusion.refs_0_), channel_id=1, source_target_pairs={{0,64},{8,72},{64,0},{72,8},{1,65},{9,73},{65,1},{73,9},{2,66},{10... | collective-permute-start | bytes 602120 | tf_op jit(solution)/shard_map/ppermute | solution.py:436
  22.3 3.0 %collective-permute-start.3 = (f32[392,128]{1,0:T(8,128)S(1)}, f32[392,128]{1,0:T(8,128)S(1)}, u32[]{:S(2)}, u32[]{:S(2)}) collective-permute-start(f32[392,128]{1,0:T(8,128)S(1)} %maximum_maximum_fusion.refs_0_), channel_id=1, source_target_pairs={{0,1},{1,0},{2,3},{3,2},{4,5},{5,4},{6,7},{7,6},{8,9},{9,8},{10,11... | collective-permute-start | bytes 602120 | tf_op jit(solution)/shard_map/ppermute | solution.py:436
  25.2 0.0 collective-permute-done.2.refs_3_
  25.2 0.0 copy-start.1
  25.2 5.7 %collective-permute-start.6 = (f32[392,128]{1,0:T(8,128)S(1)}, f32[392,128]{1,0:T(8,128)S(1)}, u32[]{:S(2)}, u32[]{:S(2)}) collective-permute-start(f32[392,128]{1,0:T(8,128)S(1)} %collective-permute-done.2.refs_3_), channel_id=1, source_target_pairs={{0,1},{1,0},{2,3},{3,2},{4,5},{5,4},{6,7},{7,6},{8,9},{9,8},{10,11... | collective-permute-start | bytes 602120 | tf_op jit(solution)/shard_map/ppermute | solution.py:436
  30.9 0.0 collective-permute-done.1.refs_2_
  30.9 0.0 copy-start.2
  30.9 3.0 %collective-permute-start.5 = (f32[392,128]{1,0:T(8,128)S(1)}, f32[392,128]{1,0:T(8,128)S(1)}, u32[]{:S(2)}, u32[]{:S(2)}) collective-permute-start(f32[392,128]{1,0:T(8,128)S(1)} %collective-permute-done.1.refs_2_), channel_id=1, source_target_pairs={{0,1},{1,0},{2,3},{3,2},{4,5},{5,4},{6,7},{7,6},{8,9},{9,8},{10,11... | collective-permute-start | bytes 602120 | tf_op jit(solution)/shard_map/ppermute | solution.py:436
  33.9 0.0 collective-permute-done.refs_1_
  33.9 0.0 copy-start.3
  33.9 0.3 collective-permute-start.4
  34.1 0.0 collective-permute-done.3.refs_4_
  34.2 0.0 copy-start.4
  34.2 0.0 collective-permute-done.6.refs_7_
  34.2 0.0 copy-start.5
  34.2 0.8 collective-permute-done.5.refs_6_
  34.9 0.0 copy-start.6
  34.9 0.4 collective-permute-done.4.refs_5_
  35.3 0.0 copy-start.7
  35.3 0.0 copy-done
  35.3 0.0 copy-done.1
  35.3 0.0 copy-done.2
  35.3 0.0 copy-done.3
  35.3 0.0 copy-done.4
  35.4 0.0 copy-done.5
  35.4 0.3 copy-done.6
  35.6 0.4 copy-done.7
  36.0 41.2 %shard_map.56 = f32[16,256,128]{2,1,0:T(8,128)} custom-call(s32[1]{0:T(128)} %bitcast.first_ref, f32[392,128]{1,0:T(8,128)} %copy-done, f32[392,128]{1,0:T(8,128)} %copy-done.3, f32[392,128]{1,0:T(8,128)} %copy-done.2, f32[392,128]{1,0:T(8,128)} %copy-done.1, f32[392,128]{1,0:T(8,128)} %copy-done.4, f32[392,128]{1,0:T(8,128)} %copy-done.7, ...), custom_call_target="tpu_custom_call" | custom-call | tf_op jit(solution)/shard_map/pallas_call | solution.py:407
  77.2 31.4 %all_to_all.14 = f32[8,512,128]{2,1,0:T(8,128)S(1)} all-to-all(f32[8,512,128]{2,1,0:T(8,128)} %bitcast.14), channel_id=1, replica_groups=mesh['plane_0'=2,'plane_1'=4,'tile_0'=2,'tile_1'=4,'tile_2'=2] {'plane_1..., dimensions={0} | all-to-all | bytes 4194304 | tf_op jit(solution)/shard_map/all_to_all | solution.py:450
  108.7 0.1 reduce_sum.9
  108.9 0.8 pad_maximum_fusion
  (3 shorter events, 0.0 us)
Async XLA Ops:
  2.2 14.8 %all-to-all-start = ((f32[16,24,128]{2,1,0:T(8,128)}), f32[16,24,128]{2,1,0:T(8,128)S(1)}, u32[]{:S(2)}, u32[]{:S(2)}) async-start(f32[16,24,128]{2,1,0:T(8,128)} %shard_map.55), calls=%async_computation | async-start | bytes 393216 | tf_op jit(solution)/shard_map/all_to_all | solution.py:442
  17.1 18.2 %copy-start = (f32[392,128]{1,0:T(8,128)}, f32[392,128]{1,0:T(8,128)S(1)}, u32[]{:S(2)}) copy-start(f32[392,128]{1,0:T(8,128)S(1)} %maximum_maximum_fusion.refs_0_) | copy-start | bytes 602116
  17.1 8.1 %collective-permute-start.2 = (f32[392,128]{1,0:T(8,128)S(1)}, f32[392,128]{1,0:T(8,128)S(1)}, u32[]{:S(2)}, u32[]{:S(2)}) collective-permute-start(f32[392,128]{1,0:T(8,128)S(1)} %maximum_maximum_fusion.refs_0_), channel_id=1, source_target_pairs={{0,72},{8,0},{64,8},{72,64},{1,73},{9,1},{65,9},{73,65},{2,74},{10... | collective-permute-start | bytes 602120 | tf_op jit(solution)/shard_map/ppermute | solution.py:436
  21.0 9.9 %collective-permute-start.1 = (f32[392,128]{1,0:T(8,128)S(1)}, f32[392,128]{1,0:T(8,128)S(1)}, u32[]{:S(2)}, u32[]{:S(2)}) collective-permute-start(f32[392,128]{1,0:T(8,128)S(1)} %maximum_maximum_fusion.refs_0_), channel_id=1, source_target_pairs={{0,8},{8,64},{64,72},{72,0},{1,9},{9,65},{65,73},{73,1},{2,10},{10... | collective-permute-start | bytes 602120 | tf_op jit(solution)/shard_map/ppermute | solution.py:436
  21.0 12.9 %collective-permute-start = (f32[392,128]{1,0:T(8,128)S(1)}, f32[392,128]{1,0:T(8,128)S(1)}, u32[]{:S(2)}, u32[]{:S(2)}) collective-permute-start(f32[392,128]{1,0:T(8,128)S(1)} %maximum_maximum_fusion.refs_0_), channel_id=1, source_target_pairs={{0,64},{8,72},{64,0},{72,8},{1,65},{9,73},{65,1},{73,9},{2,66},{10... | collective-permute-start | bytes 602120 | tf_op jit(solution)/shard_map/ppermute | solution.py:436
  22.3 11.9 %collective-permute-start.3 = (f32[392,128]{1,0:T(8,128)S(1)}, f32[392,128]{1,0:T(8,128)S(1)}, u32[]{:S(2)}, u32[]{:S(2)}) collective-permute-start(f32[392,128]{1,0:T(8,128)S(1)} %maximum_maximum_fusion.refs_0_), channel_id=1, source_target_pairs={{0,1},{1,0},{2,3},{3,2},{4,5},{5,4},{6,7},{7,6},{8,9},{9,8},{10,11... | collective-permute-start | bytes 602120 | tf_op jit(solution)/shard_map/ppermute | solution.py:436
  25.2 10.1 %copy-start.1 = (f32[392,128]{1,0:T(8,128)}, f32[392,128]{1,0:T(8,128)S(1)}, u32[]{:S(2)}) copy-start(f32[392,128]{1,0:T(8,128)S(1)} %collective-permute-done.2.refs_3_) | copy-start | bytes 602116
  25.2 8.9 %collective-permute-start.6 = (f32[392,128]{1,0:T(8,128)S(1)}, f32[392,128]{1,0:T(8,128)S(1)}, u32[]{:S(2)}, u32[]{:S(2)}) collective-permute-start(f32[392,128]{1,0:T(8,128)S(1)} %collective-permute-done.2.refs_3_), channel_id=1, source_target_pairs={{0,1},{1,0},{2,3},{3,2},{4,5},{5,4},{6,7},{7,6},{8,9},{9,8},{10,11... | collective-permute-start | bytes 602120 | tf_op jit(solution)/shard_map/ppermute | solution.py:436
  30.9 4.4 %copy-start.2 = (f32[392,128]{1,0:T(8,128)}, f32[392,128]{1,0:T(8,128)S(1)}, u32[]{:S(2)}) copy-start(f32[392,128]{1,0:T(8,128)S(1)} %collective-permute-done.1.refs_2_) | copy-start | bytes 602116
  30.9 4.0 %collective-permute-start.5 = (f32[392,128]{1,0:T(8,128)S(1)}, f32[392,128]{1,0:T(8,128)S(1)}, u32[]{:S(2)}, u32[]{:S(2)}) collective-permute-start(f32[392,128]{1,0:T(8,128)S(1)} %collective-permute-done.1.refs_2_), channel_id=1, source_target_pairs={{0,1},{1,0},{2,3},{3,2},{4,5},{5,4},{6,7},{7,6},{8,9},{9,8},{10,11... | collective-permute-start | bytes 602120 | tf_op jit(solution)/shard_map/ppermute | solution.py:436
  33.9 1.5 %copy-start.3 = (f32[392,128]{1,0:T(8,128)}, f32[392,128]{1,0:T(8,128)S(1)}, u32[]{:S(2)}) copy-start(f32[392,128]{1,0:T(8,128)S(1)} %collective-permute-done.refs_1_) | copy-start | bytes 602116
  33.9 1.4 %collective-permute-start.4 = (f32[392,128]{1,0:T(8,128)S(1)}, f32[392,128]{1,0:T(8,128)S(1)}, u32[]{:S(2)}, u32[]{:S(2)}) collective-permute-start(f32[392,128]{1,0:T(8,128)S(1)} %collective-permute-done.refs_1_), channel_id=1, source_target_pairs={{0,1},{1,0},{2,3},{3,2},{4,5},{5,4},{6,7},{7,6},{8,9},{9,8},{10,11... | collective-permute-start | bytes 602120 | tf_op jit(solution)/shard_map/ppermute | solution.py:436
  34.2 1.2 %copy-start.4 = (f32[392,128]{1,0:T(8,128)}, f32[392,128]{1,0:T(8,128)S(1)}, u32[]{:S(2)}) copy-start(f32[392,128]{1,0:T(8,128)S(1)} %collective-permute-done.3.refs_4_) | copy-start | bytes 602116
  34.2 1.2 %copy-start.5 = (f32[392,128]{1,0:T(8,128)}, f32[392,128]{1,0:T(8,128)S(1)}, u32[]{:S(2)}) copy-start(f32[392,128]{1,0:T(8,128)S(1)} %collective-permute-done.6.refs_7_) | copy-start | bytes 602116
  34.9 0.7 copy-start.6
  35.3 0.7 copy-start.7
